TPU v7x, 128 devices: a whole 4x4x4 slice. The times are simulated.
128 devices in a mesh: head: 8 (over y, z_lo), ctx: 16 (over z_hi, x, core).
Axes of the slice: x: 4, y: 4, z: 4 (z_hi: 2, z_lo: 2; z = z_hi * 2 + z_lo), core: 2. Of those that a mesh axis runs over, the one named last changes fastest.
Arguments:
- query: bfloat16 [12288, 4096], P(('ctx', 'head')), may hold values from -8 to 8
- key: bfloat16 [12288, 2048], P(('ctx', 'head')), may hold values from -8 to 8
- value: bfloat16 [12288, 2048], P(('ctx', 'head')), may hold values from -8 to 8
- block_order: int32 [32], replicated, may hold values from 0 to 31, each once
Outputs:
- attended: bfloat16 [12288, 4096], P('ctx', 'head')
Inputs may be any that keep to these rules, and one draw needn't show every extreme that they name: `block_order`: each storage block index 0 to 31 appears exactly once.
All inputs are finite; a program needn't handle non-finite values.
Results may differ from a plain program's by a relative error of at most 0.0049.
Values may be sent and summed in bfloat16 or wider, within the bound.
No kernel may reach another device: no remote copies, remote signals or barrier semaphores. Data moves between devices by JAX's collectives and lax.ppermute only.
A program may use at most 128 MiB of HBM per device.

v0:
```python
import jax
import jax.numpy as jnp
from jax import lax
from jax.sharding import PartitionSpec as P

HEAD_WIDTH = 128


query_scale = 1.0 / 12.0
softcap_limit = 50.0


def from_behind(value, axis, by):
    size = lax.axis_size(axis)
    return lax.ppermute(value, axis, [(i, (i + by) % size) for i in range(size)])


def block_pos(block_order, which_block, block_len):
    first = lax.dynamic_index_in_dim(block_order, which_block, 0, keepdims=False)
    return first * block_len + lax.iota(jnp.int32, block_len)


def add_block(totals, query_rows, query_pos, key_block, value_block, key_pos):
    numerator, denominator = totals
    scores = (
        jnp.einsum("rhgd,khd->hgrk", query_rows, key_block, preferred_element_type=jnp.float32)
        * query_scale
    )
    capped = softcap_limit * jnp.tanh(scores / softcap_limit)
    visible = key_pos[None, :] <= query_pos[:, None]
    weights = jnp.where(visible[None, None], jnp.exp(capped), jnp.zeros_like(capped))
    denominator = denominator + jnp.sum(weights, axis=-1)
    numerator = numerator + jnp.einsum(
        "hgrk,khd->rhgd",
        weights.astype(jnp.bfloat16),
        value_block,
        preferred_element_type=jnp.float32,
    )
    return (numerator, denominator)


def shards(query, key, value, block_order):
    query, key, value = (
        lax.all_to_all(query, "head", split_axis=1, concat_axis=0, tiled=True),
        lax.all_to_all(key, "head", split_axis=1, concat_axis=0, tiled=True),
        lax.all_to_all(value, "head", split_axis=1, concat_axis=0, tiled=True),
    )
    row_count = query.shape[0]
    block_len = row_count // 2
    kv_heads = key.shape[1] // HEAD_WIDTH
    group_size = query.shape[1] // key.shape[1]
    query_rows = query.reshape(row_count, kv_heads, group_size, HEAD_WIDTH)
    kv_pair = jnp.stack(
        [
            key.reshape(row_count, kv_heads, HEAD_WIDTH),
            value.reshape(row_count, kv_heads, HEAD_WIDTH),
        ]
    )
    cycle_size = lax.axis_size("ctx")
    cycle_index = lax.axis_index("ctx")
    query_pos = jnp.concatenate(
        [
            block_pos(block_order, 2 * cycle_index, block_len),
            block_pos(block_order, 2 * cycle_index + 1, block_len),
        ]
    )
    start_totals = (
        jnp.zeros((row_count, kv_heads, group_size, HEAD_WIDTH), jnp.float32),
        jnp.zeros((kv_heads, group_size, row_count), jnp.float32),
    )

    def add_shard(totals, held, source):
        for which_half in range(2):
            lower = which_half * block_len
            key_pos = block_pos(block_order, 2 * source + which_half, block_len)
            totals = add_block(
                totals,
                query_rows,
                query_pos,
                held[0, lower : lower + block_len],
                held[1, lower : lower + block_len],
                key_pos,
            )
        return totals

    totals = add_shard(start_totals, kv_pair, cycle_index)

    def from_lower(held):
        return from_behind(held, "ctx", 1)

    def turn_both(turn_index, state):
        forward_kv, backward_kv, sums = state
        forward_kv = from_lower(forward_kv)
        backward_kv = from_behind(backward_kv, "ctx", -1)
        sums = add_shard(sums, forward_kv, (cycle_index - turn_index) % cycle_size)
        sums = add_shard(sums, backward_kv, (cycle_index + turn_index) % cycle_size)
        return (forward_kv, backward_kv, sums)

    forward_kv, backward_kv, totals = lax.fori_loop(
        1, cycle_size // 2, turn_both, (kv_pair, kv_pair, totals)
    )
    forward_kv = from_lower(forward_kv)
    totals = add_shard(totals, forward_kv, (cycle_index + cycle_size // 2) % cycle_size)
    numerator, denominator = totals
    result = numerator / jnp.transpose(denominator, (2, 0, 1))[..., None]
    return result.reshape(row_count, kv_heads * group_size * HEAD_WIDTH).astype(jnp.bfloat16)


def solution(mesh):
    placed = (P(("ctx", "head"), None), P(("ctx", "head"), None), P(("ctx", "head"), None), P())
    return jax.shard_map(
        shards, mesh=mesh, in_specs=placed, out_specs=P("ctx", "head"), check_vma=False
    )
```

profile of v0, /device:TPU:0, one launch (start us, length us, event | category | flops | bytes accessed | tf_op | source)
XLA Modules:
  0.0 312.1 jit_solution(14813178823769544155)
XLA Ops:
  1.8 5.9 %all-to-all-start = ((bf16[96,8,256]{2,0,1:T(8,128)(2,1)}), bf16[96,8,256]{2,0,1:T(8,128)(2,1)S(1)}, u32[]{:S(2)}, u32[]{:S(2)}) async-start(bf16[96,8,256]{2,0,1:T(8,128)(2,1)} %bitcast.231), calls=%async_computation | async-start | bytes 786432 | tf_op jit(solution)/shard_map/all_to_all | solution.py:45
  9.5 6.4 %all-to-all-done = bf16[96,8,256]{2,0,1:T(8,128)(2,1)S(1)} async-done(((bf16[96,8,256]{2,0,1:T(8,128)(2,1)}), bf16[96,8,256]{2,0,1:T(8,128)(2,1)S(1)}, u32[]{:S(2)}, u32[]{:S(2)}) %all-to-all-start) | async-done | bytes 393248 | tf_op jit(solution)/shard_map/all_to_all | solution.py:45
  15.9 3.5 %all-to-all-start.1 = ((bf16[96,8,256]{2,0,1:T(8,128)(2,1)}), bf16[96,8,256]{2,0,1:T(8,128)(2,1)S(1)}, u32[]{:S(2)}, u32[]{:S(2)}) async-start(bf16[96,8,256]{2,0,1:T(8,128)(2,1)} %bitcast.230), calls=%async_computation.1 | async-start | bytes 786432 | tf_op jit(solution)/shard_map/all_to_all | solution.py:46
  23.3 2.1 copy.109
  27.1 3.8 %all-to-all-start.2 = ((bf16[96,8,512]{2,0,1:T(8,128)(2,1)}), bf16[96,8,512]{2,0,1:T(8,128)(2,1)S(1)}, u32[]{:S(2)}, u32[]{:S(2)}) async-start(bf16[96,8,512]{2,0,1:T(8,128)(2,1)} %bitcast.229), calls=%async_computation.2 | async-start | bytes 1572864 | tf_op jit(solution)/shard_map/all_to_all | solution.py:44
  34.8 2.1 copy.114
  37.4 4.8 %all-to-all-done.2 = bf16[96,8,512]{2,0,1:T(8,128)(2,1)S(1)} async-done(((bf16[96,8,512]{2,0,1:T(8,128)(2,1)}), bf16[96,8,512]{2,0,1:T(8,128)(2,1)S(1)}, u32[]{:S(2)}, u32[]{:S(2)}) %all-to-all-start.2) | async-done | bytes 786464 | tf_op jit(solution)/shard_map/all_to_all | solution.py:44
  43.6 2.8 fusion.40
  49.8 1.8 add_bitcast_fusion
  51.6 232.8 %while.22 = (s32[]{:T(128)}, bf16[2,768,2,128]{3,1,2,0:T(8,128)(2,1)}, bf16[2,768,2,128]{3,1,2,0:T(8,128)(2,1)}, f32[768,2,2,128]{3,0,2,1:T(8,128)S(1)}, f32[2,2...) while((s32[]{:T(128)}, ...), condition=%wide.region_7.8_spmd, body=%wide.region_2.7_spmd.sunk | while | flops 2456421888 | bytes 71311136 | solution.py:99
  51.9 5.3 %collective-permute-start.1 = (bf16[2,768,2,128]{3,1,2,0:T(8,128)(2,1)}, bf16[2,768,2,128]{3,1,2,0:T(8,128)(2,1)S(1)}, u32[]{:S(2)}, u32[]{:S(2)}) collective-permute-start(bf16[2,768,2,128]{3,1,2,0:T(8,128)(2,1)} %get-tuple-element.453), channel_id=1, source_target_pairs={{0,15},{1,0},{2,1},{3,2},{4,3},{5,4},{6,5},{7,6},{8,7},{9,8},{10,9... | collective-permute-start | bytes 2359304 | tf_op jit(solution)/shard_map/while/body/eval_jaxpr/ppermute | solution.py:15
  61.1 6.1 %collective-permute-done = bf16[2,768,2,128]{3,1,2,0:T(8,128)(2,1)S(1)} collective-permute-done((bf16[2,768,2,128]{3,1,2,0:T(8,128)(2,1)}, bf16[2,768,2,128]{3,1,2,0:T(8,128)(2,1)S(1)}, u32[]{:S(2)}, u32[]{:S(2)}) %collective-permute-start) | collective-permute-done | bytes 786464 | tf_op jit(solution)/shard_map/while/body/eval_jaxpr/ppermute | solution.py:15
  67.1 2.9 fusion.119
  70.1 1.9 fusion.121
  72.0 1.9 fusion.117
  74.0 1.9 fusion.123
  82.8 2.2 bitcast_add_fusion.7
  85.1 5.3 %collective-permute-start.1 = (bf16[2,768,2,128]{3,1,2,0:T(8,128)(2,1)}, bf16[2,768,2,128]{3,1,2,0:T(8,128)(2,1)S(1)}, u32[]{:S(2)}, u32[]{:S(2)}) collective-permute-start(bf16[2,768,2,128]{3,1,2,0:T(8,128)(2,1)} %get-tuple-element.453), channel_id=1, source_target_pairs={{0,15},{1,0},{2,1},{3,2},{4,3},{5,4},{6,5},{7,6},{8,7},{9,8},{10,9... | collective-permute-start | bytes 2359304 | tf_op jit(solution)/shard_map/while/body/eval_jaxpr/ppermute | solution.py:15
  94.3 6.1 %collective-permute-done = bf16[2,768,2,128]{3,1,2,0:T(8,128)(2,1)S(1)} collective-permute-done((bf16[2,768,2,128]{3,1,2,0:T(8,128)(2,1)}, bf16[2,768,2,128]{3,1,2,0:T(8,128)(2,1)S(1)}, u32[]{:S(2)}, u32[]{:S(2)}) %collective-permute-start) | collective-permute-done | bytes 786464 | tf_op jit(solution)/shard_map/while/body/eval_jaxpr/ppermute | solution.py:15
  100.3 2.9 fusion.119
  103.3 1.9 fusion.121
  105.2 1.9 fusion.117
  107.2 1.9 fusion.123
  116.0 2.2 bitcast_add_fusion.7
  118.3 5.3 %collective-permute-start.1 = (bf16[2,768,2,128]{3,1,2,0:T(8,128)(2,1)}, bf16[2,768,2,128]{3,1,2,0:T(8,128)(2,1)S(1)}, u32[]{:S(2)}, u32[]{:S(2)}) collective-permute-start(bf16[2,768,2,128]{3,1,2,0:T(8,128)(2,1)} %get-tuple-element.453), channel_id=1, source_target_pairs={{0,15},{1,0},{2,1},{3,2},{4,3},{5,4},{6,5},{7,6},{8,7},{9,8},{10,9... | collective-permute-start | bytes 2359304 | tf_op jit(solution)/shard_map/while/body/eval_jaxpr/ppermute | solution.py:15
  127.5 6.1 %collective-permute-done = bf16[2,768,2,128]{3,1,2,0:T(8,128)(2,1)S(1)} collective-permute-done((bf16[2,768,2,128]{3,1,2,0:T(8,128)(2,1)}, bf16[2,768,2,128]{3,1,2,0:T(8,128)(2,1)S(1)}, u32[]{:S(2)}, u32[]{:S(2)}) %collective-permute-start) | collective-permute-done | bytes 786464 | tf_op jit(solution)/shard_map/while/body/eval_jaxpr/ppermute | solution.py:15
  133.5 2.9 fusion.119
  136.5 1.9 fusion.121
  138.4 1.9 fusion.117
  140.4 1.9 fusion.123
  149.2 2.2 bitcast_add_fusion.7
  151.5 5.3 %collective-permute-start.1 = (bf16[2,768,2,128]{3,1,2,0:T(8,128)(2,1)}, bf16[2,768,2,128]{3,1,2,0:T(8,128)(2,1)S(1)}, u32[]{:S(2)}, u32[]{:S(2)}) collective-permute-start(bf16[2,768,2,128]{3,1,2,0:T(8,128)(2,1)} %get-tuple-element.453), channel_id=1, source_target_pairs={{0,15},{1,0},{2,1},{3,2},{4,3},{5,4},{6,5},{7,6},{8,7},{9,8},{10,9... | collective-permute-start | bytes 2359304 | tf_op jit(solution)/shard_map/while/body/eval_jaxpr/ppermute | solution.py:15
  160.7 6.1 %collective-permute-done = bf16[2,768,2,128]{3,1,2,0:T(8,128)(2,1)S(1)} collective-permute-done((bf16[2,768,2,128]{3,1,2,0:T(8,128)(2,1)}, bf16[2,768,2,128]{3,1,2,0:T(8,128)(2,1)S(1)}, u32[]{:S(2)}, u32[]{:S(2)}) %collective-permute-start) | collective-permute-done | bytes 786464 | tf_op jit(solution)/shard_map/while/body/eval_jaxpr/ppermute | solution.py:15
  166.7 2.9 fusion.119
  169.7 1.9 fusion.121
  171.6 1.9 fusion.117
  173.6 1.9 fusion.123
  182.4 2.2 bitcast_add_fusion.7
  184.7 5.3 %collective-permute-start.1 = (bf16[2,768,2,128]{3,1,2,0:T(8,128)(2,1)}, bf16[2,768,2,128]{3,1,2,0:T(8,128)(2,1)S(1)}, u32[]{:S(2)}, u32[]{:S(2)}) collective-permute-start(bf16[2,768,2,128]{3,1,2,0:T(8,128)(2,1)} %get-tuple-element.453), channel_id=1, source_target_pairs={{0,15},{1,0},{2,1},{3,2},{4,3},{5,4},{6,5},{7,6},{8,7},{9,8},{10,9... | collective-permute-start | bytes 2359304 | tf_op jit(solution)/shard_map/while/body/eval_jaxpr/ppermute | solution.py:15
  193.9 6.1 %collective-permute-done = bf16[2,768,2,128]{3,1,2,0:T(8,128)(2,1)S(1)} collective-permute-done((bf16[2,768,2,128]{3,1,2,0:T(8,128)(2,1)}, bf16[2,768,2,128]{3,1,2,0:T(8,128)(2,1)S(1)}, u32[]{:S(2)}, u32[]{:S(2)}) %collective-permute-start) | collective-permute-done | bytes 786464 | tf_op jit(solution)/shard_map/while/body/eval_jaxpr/ppermute | solution.py:15
  200.0 2.9 fusion.119
  202.9 1.9 fusion.121
  204.8 1.9 fusion.117
  206.8 1.9 fusion.123
  215.6 2.2 bitcast_add_fusion.7
  217.9 5.3 %collective-permute-start.1 = (bf16[2,768,2,128]{3,1,2,0:T(8,128)(2,1)}, bf16[2,768,2,128]{3,1,2,0:T(8,128)(2,1)S(1)}, u32[]{:S(2)}, u32[]{:S(2)}) collective-permute-start(bf16[2,768,2,128]{3,1,2,0:T(8,128)(2,1)} %get-tuple-element.453), channel_id=1, source_target_pairs={{0,15},{1,0},{2,1},{3,2},{4,3},{5,4},{6,5},{7,6},{8,7},{9,8},{10,9... | collective-permute-start | bytes 2359304 | tf_op jit(solution)/shard_map/while/body/eval_jaxpr/ppermute | solution.py:15
  227.1 6.1 %collective-permute-done = bf16[2,768,2,128]{3,1,2,0:T(8,128)(2,1)S(1)} collective-permute-done((bf16[2,768,2,128]{3,1,2,0:T(8,128)(2,1)}, bf16[2,768,2,128]{3,1,2,0:T(8,128)(2,1)S(1)}, u32[]{:S(2)}, u32[]{:S(2)}) %collective-permute-start) | collective-permute-done | bytes 786464 | tf_op jit(solution)/shard_map/while/body/eval_jaxpr/ppermute | solution.py:15
  233.2 2.9 fusion.119
  236.1 1.9 fusion.121
  238.0 1.9 fusion.117
  240.0 1.9 fusion.123
  248.8 2.2 bitcast_add_fusion.7
  251.1 5.3 %collective-permute-start.1 = (bf16[2,768,2,128]{3,1,2,0:T(8,128)(2,1)}, bf16[2,768,2,128]{3,1,2,0:T(8,128)(2,1)S(1)}, u32[]{:S(2)}, u32[]{:S(2)}) collective-permute-start(bf16[2,768,2,128]{3,1,2,0:T(8,128)(2,1)} %get-tuple-element.453), channel_id=1, source_target_pairs={{0,15},{1,0},{2,1},{3,2},{4,3},{5,4},{6,5},{7,6},{8,7},{9,8},{10,9... | collective-permute-start | bytes 2359304 | tf_op jit(solution)/shard_map/while/body/eval_jaxpr/ppermute | solution.py:15
  260.3 6.1 %collective-permute-done = bf16[2,768,2,128]{3,1,2,0:T(8,128)(2,1)S(1)} collective-permute-done((bf16[2,768,2,128]{3,1,2,0:T(8,128)(2,1)}, bf16[2,768,2,128]{3,1,2,0:T(8,128)(2,1)S(1)}, u32[]{:S(2)}, u32[]{:S(2)}) %collective-permute-start) | collective-permute-done | bytes 786464 | tf_op jit(solution)/shard_map/while/body/eval_jaxpr/ppermute | solution.py:15
  266.4 2.9 fusion.119
  269.3 1.9 fusion.121
  271.2 1.9 fusion.117
  273.2 1.9 fusion.123
  282.0 2.2 bitcast_add_fusion.7
  285.0 14.9 %collective-permute-done.2 = bf16[2,768,2,128]{3,1,2,0:T(8,128)(2,1)} collective-permute-done((bf16[2,768,2,128]{3,1,2,0:T(8,128)(2,1)}, bf16[2,768,2,128]{3,1,2,0:T(8,128)(2,1)}, u32[]{:S(2)}, u32[]{:S(2)}) %collective-permute-start.2) | collective-permute-done | bytes 786464 | tf_op jit(solution)/shard_map/ppermute | solution.py:15
  299.9 3.1 fusion.44
  303.0 2.7 fusion.42
  305.8 2.5 fusion.48
  308.3 2.6 fusion.59
  (131 shorter events, 76.0 us)
Async XLA Ops:
  1.8 14.1 %all-to-all-start = ((bf16[96,8,256]{2,0,1:T(8,128)(2,1)}), bf16[96,8,256]{2,0,1:T(8,128)(2,1)S(1)}, u32[]{:S(2)}, u32[]{:S(2)}) async-start(bf16[96,8,256]{2,0,1:T(8,128)(2,1)} %bitcast.231), calls=%async_computation | async-start | bytes 786432 | tf_op jit(solution)/shard_map/all_to_all | solution.py:45
  15.9 11.3 %all-to-all-start.1 = ((bf16[96,8,256]{2,0,1:T(8,128)(2,1)}), bf16[96,8,256]{2,0,1:T(8,128)(2,1)S(1)}, u32[]{:S(2)}, u32[]{:S(2)}) async-start(bf16[96,8,256]{2,0,1:T(8,128)(2,1)} %bitcast.230), calls=%async_computation.1 | async-start | bytes 786432 | tf_op jit(solution)/shard_map/all_to_all | solution.py:46
  27.1 15.1 %all-to-all-start.2 = ((bf16[96,8,512]{2,0,1:T(8,128)(2,1)}), bf16[96,8,512]{2,0,1:T(8,128)(2,1)S(1)}, u32[]{:S(2)}, u32[]{:S(2)}) async-start(bf16[96,8,512]{2,0,1:T(8,128)(2,1)} %bitcast.229), calls=%async_computation.2 | async-start | bytes 1572864 | tf_op jit(solution)/shard_map/all_to_all | solution.py:44
  42.4 5.6 %copy-start = (bf16[768,2,2,128]{3,2,1,0:T(2,128)(2,1)}, bf16[768,2,2,128]{3,2,1,0:T(2,128)(2,1)S(1)}, u32[]{:S(2)}) copy-start(bf16[768,2,2,128]{3,2,1,0:T(2,128)(2,1)S(1)} %reshape.274) | copy-start | bytes 2359300
  43.6 2.8 copy-start.5
  49.8 1.8 copy-start.3
  51.8 15.3 %collective-permute-start = (bf16[2,768,2,128]{3,1,2,0:T(8,128)(2,1)}, bf16[2,768,2,128]{3,1,2,0:T(8,128)(2,1)S(1)}, u32[]{:S(2)}, u32[]{:S(2)}) collective-permute-start(bf16[2,768,2,128]{3,1,2,0:T(8,128)(2,1)} %get-tuple-element.452), channel_id=1, source_target_pairs={{0,1},{1,2},{2,3},{3,4},{4,5},{5,6},{6,7},{7,8},{8,9},{9,10},{10,1... | collective-permute-start | bytes 2359304 | tf_op jit(solution)/shard_map/while/body/eval_jaxpr/ppermute | solution.py:15
  51.9 20.1 %collective-permute-start.1 = (bf16[2,768,2,128]{3,1,2,0:T(8,128)(2,1)}, bf16[2,768,2,128]{3,1,2,0:T(8,128)(2,1)S(1)}, u32[]{:S(2)}, u32[]{:S(2)}) collective-permute-start(bf16[2,768,2,128]{3,1,2,0:T(8,128)(2,1)} %get-tuple-element.453), channel_id=1, source_target_pairs={{0,15},{1,0},{2,1},{3,2},{4,3},{5,4},{6,5},{7,6},{8,7},{9,8},{10,9... | collective-permute-start | bytes 2359304 | tf_op jit(solution)/shard_map/while/body/eval_jaxpr/ppermute | solution.py:15
  67.1 2.9 copy-start.2
  85.0 15.3 %collective-permute-start = (bf16[2,768,2,128]{3,1,2,0:T(8,128)(2,1)}, bf16[2,768,2,128]{3,1,2,0:T(8,128)(2,1)S(1)}, u32[]{:S(2)}, u32[]{:S(2)}) collective-permute-start(bf16[2,768,2,128]{3,1,2,0:T(8,128)(2,1)} %get-tuple-element.452), channel_id=1, source_target_pairs={{0,1},{1,2},{2,3},{3,4},{4,5},{5,6},{6,7},{7,8},{8,9},{9,10},{10,1... | collective-permute-start | bytes 2359304 | tf_op jit(solution)/shard_map/while/body/eval_jaxpr/ppermute | solution.py:15
  85.1 20.1 %collective-permute-start.1 = (bf16[2,768,2,128]{3,1,2,0:T(8,128)(2,1)}, bf16[2,768,2,128]{3,1,2,0:T(8,128)(2,1)S(1)}, u32[]{:S(2)}, u32[]{:S(2)}) collective-permute-start(bf16[2,768,2,128]{3,1,2,0:T(8,128)(2,1)} %get-tuple-element.453), channel_id=1, source_target_pairs={{0,15},{1,0},{2,1},{3,2},{4,3},{5,4},{6,5},{7,6},{8,7},{9,8},{10,9... | collective-permute-start | bytes 2359304 | tf_op jit(solution)/shard_map/while/body/eval_jaxpr/ppermute | solution.py:15
  100.3 2.9 copy-start.2
  118.2 15.3 %collective-permute-start = (bf16[2,768,2,128]{3,1,2,0:T(8,128)(2,1)}, bf16[2,768,2,128]{3,1,2,0:T(8,128)(2,1)S(1)}, u32[]{:S(2)}, u32[]{:S(2)}) collective-permute-start(bf16[2,768,2,128]{3,1,2,0:T(8,128)(2,1)} %get-tuple-element.452), channel_id=1, source_target_pairs={{0,1},{1,2},{2,3},{3,4},{4,5},{5,6},{6,7},{7,8},{8,9},{9,10},{10,1... | collective-permute-start | bytes 2359304 | tf_op jit(solution)/shard_map/while/body/eval_jaxpr/ppermute | solution.py:15
  118.3 20.1 %collective-permute-start.1 = (bf16[2,768,2,128]{3,1,2,0:T(8,128)(2,1)}, bf16[2,768,2,128]{3,1,2,0:T(8,128)(2,1)S(1)}, u32[]{:S(2)}, u32[]{:S(2)}) collective-permute-start(bf16[2,768,2,128]{3,1,2,0:T(8,128)(2,1)} %get-tuple-element.453), channel_id=1, source_target_pairs={{0,15},{1,0},{2,1},{3,2},{4,3},{5,4},{6,5},{7,6},{8,7},{9,8},{10,9... | collective-permute-start | bytes 2359304 | tf_op jit(solution)/shard_map/while/body/eval_jaxpr/ppermute | solution.py:15
  133.5 2.9 copy-start.2
  151.4 15.3 %collective-permute-start = (bf16[2,768,2,128]{3,1,2,0:T(8,128)(2,1)}, bf16[2,768,2,128]{3,1,2,0:T(8,128)(2,1)S(1)}, u32[]{:S(2)}, u32[]{:S(2)}) collective-permute-start(bf16[2,768,2,128]{3,1,2,0:T(8,128)(2,1)} %get-tuple-element.452), channel_id=1, source_target_pairs={{0,1},{1,2},{2,3},{3,4},{4,5},{5,6},{6,7},{7,8},{8,9},{9,10},{10,1... | collective-permute-start | bytes 2359304 | tf_op jit(solution)/shard_map/while/body/eval_jaxpr/ppermute | solution.py:15
  151.5 20.1 %collective-permute-start.1 = (bf16[2,768,2,128]{3,1,2,0:T(8,128)(2,1)}, bf16[2,768,2,128]{3,1,2,0:T(8,128)(2,1)S(1)}, u32[]{:S(2)}, u32[]{:S(2)}) collective-permute-start(bf16[2,768,2,128]{3,1,2,0:T(8,128)(2,1)} %get-tuple-element.453), channel_id=1, source_target_pairs={{0,15},{1,0},{2,1},{3,2},{4,3},{5,4},{6,5},{7,6},{8,7},{9,8},{10,9... | collective-permute-start | bytes 2359304 | tf_op jit(solution)/shard_map/while/body/eval_jaxpr/ppermute | solution.py:15
  166.7 2.9 copy-start.2
  184.6 15.3 %collective-permute-start = (bf16[2,768,2,128]{3,1,2,0:T(8,128)(2,1)}, bf16[2,768,2,128]{3,1,2,0:T(8,128)(2,1)S(1)}, u32[]{:S(2)}, u32[]{:S(2)}) collective-permute-start(bf16[2,768,2,128]{3,1,2,0:T(8,128)(2,1)} %get-tuple-element.452), channel_id=1, source_target_pairs={{0,1},{1,2},{2,3},{3,4},{4,5},{5,6},{6,7},{7,8},{8,9},{9,10},{10,1... | collective-permute-start | bytes 2359304 | tf_op jit(solution)/shard_map/while/body/eval_jaxpr/ppermute | solution.py:15
  184.7 20.1 %collective-permute-start.1 = (bf16[2,768,2,128]{3,1,2,0:T(8,128)(2,1)}, bf16[2,768,2,128]{3,1,2,0:T(8,128)(2,1)S(1)}, u32[]{:S(2)}, u32[]{:S(2)}) collective-permute-start(bf16[2,768,2,128]{3,1,2,0:T(8,128)(2,1)} %get-tuple-element.453), channel_id=1, source_target_pairs={{0,15},{1,0},{2,1},{3,2},{4,3},{5,4},{6,5},{7,6},{8,7},{9,8},{10,9... | collective-permute-start | bytes 2359304 | tf_op jit(solution)/shard_map/while/body/eval_jaxpr/ppermute | solution.py:15
  200.0 2.9 copy-start.2
  217.8 15.3 %collective-permute-start = (bf16[2,768,2,128]{3,1,2,0:T(8,128)(2,1)}, bf16[2,768,2,128]{3,1,2,0:T(8,128)(2,1)S(1)}, u32[]{:S(2)}, u32[]{:S(2)}) collective-permute-start(bf16[2,768,2,128]{3,1,2,0:T(8,128)(2,1)} %get-tuple-element.452), channel_id=1, source_target_pairs={{0,1},{1,2},{2,3},{3,4},{4,5},{5,6},{6,7},{7,8},{8,9},{9,10},{10,1... | collective-permute-start | bytes 2359304 | tf_op jit(solution)/shard_map/while/body/eval_jaxpr/ppermute | solution.py:15
  217.9 20.1 %collective-permute-start.1 = (bf16[2,768,2,128]{3,1,2,0:T(8,128)(2,1)}, bf16[2,768,2,128]{3,1,2,0:T(8,128)(2,1)S(1)}, u32[]{:S(2)}, u32[]{:S(2)}) collective-permute-start(bf16[2,768,2,128]{3,1,2,0:T(8,128)(2,1)} %get-tuple-element.453), channel_id=1, source_target_pairs={{0,15},{1,0},{2,1},{3,2},{4,3},{5,4},{6,5},{7,6},{8,7},{9,8},{10,9... | collective-permute-start | bytes 2359304 | tf_op jit(solution)/shard_map/while/body/eval_jaxpr/ppermute | solution.py:15
  233.2 2.9 copy-start.2
  251.1 15.3 %collective-permute-start = (bf16[2,768,2,128]{3,1,2,0:T(8,128)(2,1)}, bf16[2,768,2,128]{3,1,2,0:T(8,128)(2,1)S(1)}, u32[]{:S(2)}, u32[]{:S(2)}) collective-permute-start(bf16[2,768,2,128]{3,1,2,0:T(8,128)(2,1)} %get-tuple-element.452), channel_id=1, source_target_pairs={{0,1},{1,2},{2,3},{3,4},{4,5},{5,6},{6,7},{7,8},{8,9},{9,10},{10,1... | collective-permute-start | bytes 2359304 | tf_op jit(solution)/shard_map/while/body/eval_jaxpr/ppermute | solution.py:15
  251.1 20.1 %collective-permute-start.1 = (bf16[2,768,2,128]{3,1,2,0:T(8,128)(2,1)}, bf16[2,768,2,128]{3,1,2,0:T(8,128)(2,1)S(1)}, u32[]{:S(2)}, u32[]{:S(2)}) collective-permute-start(bf16[2,768,2,128]{3,1,2,0:T(8,128)(2,1)} %get-tuple-element.453), channel_id=1, source_target_pairs={{0,15},{1,0},{2,1},{3,2},{4,3},{5,4},{6,5},{7,6},{8,7},{9,8},{10,9... | collective-permute-start | bytes 2359304 | tf_op jit(solution)/shard_map/while/body/eval_jaxpr/ppermute | solution.py:15
  266.4 2.9 copy-start.2
  284.5 15.4 %collective-permute-start.2 = (bf16[2,768,2,128]{3,1,2,0:T(8,128)(2,1)}, bf16[2,768,2,128]{3,1,2,0:T(8,128)(2,1)}, u32[]{:S(2)}, u32[]{:S(2)}) collective-permute-start(bf16[2,768,2,128]{3,1,2,0:T(8,128)(2,1)} %get-tuple-element.266), channel_id=1, source_target_pairs={{0,1},{1,2},{2,3},{3,4},{4,5},{5,6},{6,7},{7,8},{8,9},{9,10},{10,1... | collective-permute-start | bytes 2359304 | tf_op jit(solution)/shard_map/ppermute | solution.py:15
  299.9 3.1 copy-start.1
  299.9 3.1 copy-start.4
where the time goes:
time: 313 us; the launch traced here: 312 us
  matrix products  131 us (42%)
  waiting for transfers between devices  70.4 us (22%)
  starting transfers between devices  51.3 us (16%)
  local copies, waits for them, and re-layouts  30.6 us (10%)
  loops' own time  18 us (6%)
  other arithmetic  8 us (3%)
    dot_general x32, matrix products, add_block(): jnp.einsum('rhgd,khd->hgrk', query_rows, key_block, preferred_element_typ...  71.3 us
    dot_general x32, matrix products, add_block(): jnp.einsum('hgrk,khd->rhgd', weights.astype(jnp.bfloat16), value_block, p...  59.8 us
    ppermute x15, waiting for transfers between devices, from_behind(): lax.ppermute(value, axis, [(i, (i + by) % size) for i in range(size)])  57.4 us
    ppermute x15, starting transfers between devices, from_behind(): lax.ppermute(value, axis, [(i, (i + by) % size) for i in range(size)])  38 us
    another operation x1, loops' own time, shards(): lax.fori_loop(1, cycle_size // 2, turn_both, (kv_pair, kv_pair, totals))  18 us
    while x28, local copies, waits for them, and re-layouts  12.3 us
    le x8, other arithmetic, add_block(): visible = key_pos[None, :] <= query_pos[:, None]  6.59 us
    all_to_all x1, waiting for transfers between devices, shards(): lax.all_to_all(key, 'head', split_axis=1, concat_axis=0, tiled=True)  6.38 us
  transfers between devices with their start and end apart: 18, of which 11 were waited for; matrix products, arithmetic and copies ran while one was open for 18% of the time, Pallas kernels for 0%

commit v1 on v0

v1 whole, which is shorter than its diff:
```python
import functools

import jax
import jax.numpy as jnp
from jax import lax
from jax.experimental import pallas as pl
from jax.experimental.pallas import tpu as pltpu
from jax.sharding import Mesh
from jax.sharding import PartitionSpec as P

HEAD = 128
BLK = 384
PIECE = 96
TILE = 256
Q_BLOCKS = 8
TILES = Q_BLOCKS * BLK // TILE
DUMMY = TILES
SCORE_SCALE = 1.0 / (12.0 * 50.0)
CAP_LOG2E = 50.0 * 1.4426950408889634

AXES = ("y", "zlo", "zhi", "x", "core")


def attend_kernel(*refs, offsets, first, last):
    n_shards = len(offsets)
    nb = 4 * n_shards
    refs = list(refs)
    order = refs.pop(0)
    kv = [refs.pop(0) for _ in range(n_shards)]
    if first:
        q_ref = refs.pop(0)
    else:
        qt_in, num_in, den_in = (refs.pop(0) for _ in range(3))
    if last:
        out_ref = refs.pop(0)
    else:
        qt_out, num_out, den_out = (refs.pop(0) for _ in range(3))
    qt, num, den, qpos, kbuf, vt, s0, s1, p0, p1, rows, q_seq, q_slot, kb_list, kb_start, kb_seq = refs

    x = lax.axis_index("x")
    core = lax.axis_index("core")

    seqs = []
    for slot in range(Q_BLOCKS):
        yhi, zhi, cc = slot // 4, (slot // 2) % 2, slot % 2
        seqs.append(order[2 * (zhi * 8 + x * 2 + cc) + yhi])
    for slot in range(Q_BLOCKS):
        rank = jnp.int32(0)
        for other in range(Q_BLOCKS):
            if other != slot:
                rank = rank + (seqs[other] < seqs[slot]).astype(jnp.int32)
        q_seq[rank] = seqs[slot]
        q_slot[rank] = jnp.int32(slot)

    lane = lax.broadcasted_iota(jnp.int32, (8, 128), 1)
    for g in range(2 * TILES):
        base = q_seq[g // 3] * BLK + (g % 3) * 128
        qpos[g // 2, :, (g % 2) * 128 : (g % 2) * 128 + 128] = lane + base

    if first:
        for rank in range(Q_BLOCKS):
            slot = q_slot[rank]
            yhi = slot // 4
            rest = slot % 4
            for sub in range(4):
                rows[pl.ds(rank * BLK + sub * PIECE, PIECE), :] = q_ref[yhi * 16 + sub * 4 + rest]
        for t in range(TILES):
            qt[t] = rows[t * TILE : (t + 1) * TILE, :].T
            num[t] = jnp.zeros((HEAD, TILE), jnp.float32)
            den[t] = jnp.zeros((8, TILE), jnp.float32)
    else:
        for t in range(TILES):
            qt[t] = qt_in[t]
            num[t] = num_in[t]
            den[t] = den_in[t]
    qt[DUMMY] = jnp.zeros((HEAD, TILE), jnp.bfloat16)
    num[DUMMY] = jnp.zeros((HEAD, TILE), jnp.float32)
    den[DUMMY] = jnp.zeros((8, TILE), jnp.float32)
    qpos[DUMMY] = jnp.zeros((8, TILE), jnp.int32)

    count = jnp.int32(0)
    total = jnp.int32(0)
    for n, (dx, flip) in enumerate(offsets):
        xs = (x + (4 - dx)) % 4
        cs = core + flip - 2 * core * flip
        for b in range(4):
            yhi, zhi = b // 2, b % 2
            kb = 4 * n + b
            vals = []
            for sub in range(4):
                piece = kv[n][yhi * 8 + sub * 2 + zhi]
                kbuf[kb, sub * PIECE : (sub + 1) * PIECE, :] = piece[:, :HEAD]
                vals.append(piece[:, HEAD:])
            vt[kb] = jnp.concatenate(vals, axis=0).T
            seq = order[2 * (zhi * 8 + xs * 2 + cs) + yhi]
            below = jnp.int32(0)
            for rank in range(Q_BLOCKS):
                below = below + (q_seq[rank] < seq).astype(jnp.int32)
            start = (3 * below) // 2
            kb_list[count] = jnp.int32(kb)
            kb_start[count] = start
            kb_seq[count] = seq
            has = (start < TILES).astype(jnp.int32)
            count = count + has
            total = total + (TILES - start)
    for extra in range(6):
        kb_list[count + extra] = jnp.int32(0)
        kb_start[count + extra] = jnp.int32(DUMMY)
        kb_seq[count + extra] = jnp.int32(0)

    def after(item):
        j, t = item
        wrap = t + 1 >= TILES
        j = jnp.where(wrap, j + 1, j)
        return j, jnp.where(wrap, kb_start[j], t + 1)

    def score(item, s):
        j, t = item
        s[...] = jnp.dot(kbuf[kb_list[j]], qt[t], preferred_element_type=jnp.float32)

    row = lax.broadcasted_iota(jnp.int32, (8, TILE), 0)

    def weigh(item, s, p):
        j, t = item
        rel = qpos[t] - kb_seq[j] * BLK
        acc = den[t]
        for r in range(0, BLK, 16):
            halves = []
            for h in range(2):
                z = s[r + 8 * h : r + 8 * h + 8, :]
                w = jnp.exp2(CAP_LOG2E * jnp.tanh(z * SCORE_SCALE))
                w = jnp.where(row + (r + 8 * h) <= rel, w, 0.0)
                acc = acc + w
                halves.append(w)
            p[r : r + 16, :] = jnp.concatenate(halves, axis=0).astype(jnp.bfloat16)
        den[t] = acc

    def gather(item, p):
        j, t = item
        num[t] = num[t] + jnp.dot(vt[kb_list[j]], p[...], preferred_element_type=jnp.float32)

    i0 = (jnp.int32(0), kb_start[0])
    i1 = after(i0)
    score(i0, s0)
    score(i1, s1)
    p0[...] = jnp.zeros_like(p0)
    p1[...] = jnp.zeros_like(p1)
    dummy = (count, jnp.int32(DUMMY))

    def body(_, state):
        a, b, pa, pb = state
        na = after(b)
        nb_ = after(na)
        gather(pa, p0)
        gather(pb, p1)
        weigh(a, s0, p0)
        weigh(b, s1, p1)
        score(na, s0)
        score(nb_, s1)
        return na, nb_, a, b

    _, _, pa, pb = lax.fori_loop(0, (total + 1) // 2, body, (i0, i1, dummy, dummy))
    gather(pa, p0)
    gather(pb, p1)

    if last:
        for t in range(TILES):
            inv = 1.0 / jnp.sum(den[t], axis=0, keepdims=True)
            rows[t * TILE : (t + 1) * TILE, :] = (num[t] * inv).T.astype(jnp.bfloat16)
        for rank in range(Q_BLOCKS):
            slot = q_slot[rank]
            yhi = slot // 4
            rest = slot % 4
            out_ref[rest, pl.ds(pl.multiple_of(yhi * BLK, BLK), BLK), :] = rows[
                rank * BLK : (rank + 1) * BLK, :
            ]
    else:
        for t in range(TILES):
            qt_out[t] = qt[t]
            num_out[t] = num[t]
            den_out[t] = den[t]


def attend(order, kvs, offsets, carry, first, last):
    vmem = pl.BlockSpec(memory_space=pltpu.VMEM)
    smem = pl.BlockSpec(memory_space=pltpu.SMEM)
    nb = 4 * len(kvs)
    state = (
        jax.ShapeDtypeStruct((TILES, HEAD, TILE), jnp.bfloat16),
        jax.ShapeDtypeStruct((TILES, HEAD, TILE), jnp.float32),
        jax.ShapeDtypeStruct((TILES, 8, TILE), jnp.float32),
    )
    if last:
        out = jax.ShapeDtypeStruct((4, 2 * BLK, HEAD), jnp.bfloat16)
        out_specs = vmem
    else:
        out = state
        out_specs = (vmem, vmem, vmem)
    inputs = [order, *kvs, *carry]
    return pl.pallas_call(
        functools.partial(attend_kernel, offsets=offsets, first=first, last=last),
        out_shape=out,
        in_specs=[smem] + [vmem] * (len(inputs) - 1),
        out_specs=out_specs,
        scratch_shapes=[
            pltpu.VMEM((TILES + 1, HEAD, TILE), jnp.bfloat16),
            pltpu.VMEM((TILES + 1, HEAD, TILE), jnp.float32),
            pltpu.VMEM((TILES + 1, 8, TILE), jnp.float32),
            pltpu.VMEM((TILES + 1, 8, TILE), jnp.int32),
            pltpu.VMEM((nb, BLK, HEAD), jnp.bfloat16),
            pltpu.VMEM((nb, HEAD, BLK), jnp.bfloat16),
            pltpu.VMEM((BLK, TILE), jnp.float32),
            pltpu.VMEM((BLK, TILE), jnp.float32),
            pltpu.VMEM((BLK, TILE), jnp.bfloat16),
            pltpu.VMEM((BLK, TILE), jnp.bfloat16),
            pltpu.VMEM((Q_BLOCKS * BLK, HEAD), jnp.bfloat16),
            pltpu.SMEM((Q_BLOCKS,), jnp.int32),
            pltpu.SMEM((Q_BLOCKS,), jnp.int32),
            pltpu.SMEM((nb + 8,), jnp.int32),
            pltpu.SMEM((nb + 8,), jnp.int32),
            pltpu.SMEM((nb + 8,), jnp.int32),
        ],
        compiler_params=pltpu.CompilerParams(vmem_limit_bytes=40 * 1024 * 1024),
        cost_estimate=pl.CostEstimate(
            flops=len(kvs) * 2_400_000_000, transcendentals=0, bytes_accessed=4_000_000
        ),
        name=f"attend_{len(kvs)}_{int(first)}{int(last)}",
    )(*inputs)


def along_x(value, by):
    return lax.ppermute(value, "x", [(i, (i + by) % 4) for i in range(4)])


def other_core(value):
    return lax.ppermute(value, "core", [(0, 1), (1, 0)])


def shards(query, key, value, block_order):
    rows = query.shape[0]
    kv = jnp.concatenate(
        [key.reshape(rows, 16, HEAD), value.reshape(rows, 16, HEAD)], axis=2
    ).transpose(1, 0, 2)
    kv = lax.all_to_all(kv, ("y", "zlo", "zhi"), 0, 0)
    q = query.reshape(rows, 32, HEAD).transpose(1, 0, 2)
    q = lax.all_to_all(q, ("y", "zlo", "zhi", "core"), 0, 0)

    own_other = other_core(kv)
    up = along_x(kv, 1)
    down = along_x(kv, -1)
    far_a = along_x(up[:8], 1)
    far_b = along_x(down[8:], -1)
    up_other = other_core(up)
    down_other = other_core(down)
    far = jnp.concatenate([far_a, far_b], axis=0)
    far_other = other_core(far)

    state = attend(block_order, (kv, own_other), ((0, 0), (0, 1)), (q,), True, False)
    state = attend(
        block_order,
        (up, down, up_other, down_other),
        ((1, 0), (3, 0), (1, 1), (3, 1)),
        state,
        False,
        False,
    )
    out = attend(block_order, (far, far_other), ((2, 0), (2, 1)), state, False, True)
    out = lax.all_to_all(out, ("zhi", "core"), 0, 0)
    return out.transpose(1, 0, 2).reshape(2 * BLK, 4 * HEAD)


def solution(mesh):
    fine = Mesh(mesh.devices.reshape(4, 2, 2, 4, 2), AXES)
    placed = P(("zhi", "x", "core", "y", "zlo"), None)
    return jax.shard_map(
        shards,
        mesh=fine,
        in_specs=(placed, placed, placed, P()),
        out_specs=P(("zhi", "x", "core"), ("y", "zlo")),
        check_vma=False,
    )
```

time: 313 us -> 129 us (0.41)
  matrix products: 131 us -> 0 us
  Pallas kernels: 0 us -> 60 us
  waiting for transfers between devices: 70.4 us -> 13 us
  starting transfers between devices: 51.3 us -> 11 us
  blocking collectives: 0 us -> 38 us
  local copies, waits for them, and re-layouts: 30.6 us -> 7.4 us
  loops' own time: 18 us -> 0 us
  other arithmetic: 8 us -> 0.1 us
    dot_general x64 -> x0, matrix products: 131 us -> none  [the longest x32 71.3 us: add_block(): jnp.einsum('rhgd,khd->hgrk', query_rows, key_block, preferred_element_typ...]
    pallas_call x0 -> x3, Pallas kernels: none -> 60 us  [attend(): pl.pallas_call(functools.partial(attend_kernel, offsets=offsets, first=fi...]
    ppermute x15 -> x8, waiting for transfers between devices: 57.4 us -> 13 us  [the longest x4 13 us: along_x(): return lax.ppermute(value, 'x', [(i, (i + by) % 4) for i in range(4)])]
    all_to_all x0 -> x2, blocking collectives: none -> 38 us  [the longest x1 22.4 us: shards(): kv = lax.all_to_all(kv, ('y', 'zlo', 'zhi'), 0, 0)]
    ppermute x15 -> x8, starting transfers between devices: 38 us -> 6.97 us  [the longest x4 6.47 us: along_x(): return lax.ppermute(value, 'x', [(i, (i + by) % 4) for i in range(4)])]
    another operation x1 -> x0, loops' own time: 18 us -> none  [shards(): lax.fori_loop(1, cycle_size // 2, turn_both, (kv_pair, kv_pair, totals))]
    while x30 -> x0, local copies, waits for them, and re-layouts: 13.7 us -> none
    all_to_all x3 -> x1, waiting for transfers between devices: 13 us -> 0.01 us  [shards(): q = lax.all_to_all(q, ('y', 'zlo', 'zhi', 'core'), 0, 0)]
  transfers between devices with their start and end apart: 18 -> 9, of which waited for: 11 -> 2; matrix products, arithmetic and copies ran while one was open for 18% -> 4% of each run, Pallas kernels for 0% -> 34%
where the time goes in v1:
time: 129 us; the launch traced here: 130 us
  Pallas kernels  60 us (47%)
  blocking collectives  38 us (29%)
  waiting for transfers between devices  13 us (10%)
  starting transfers between devices  11 us (9%)
  local copies, waits for them, and re-layouts  7.4 us (6%)
    pallas_call x3, Pallas kernels, attend(): pl.pallas_call(functools.partial(attend_kernel, offsets=offsets, first=fi...  60 us
    all_to_all x1, blocking collectives, shards(): kv = lax.all_to_all(kv, ('y', 'zlo', 'zhi'), 0, 0)  22.4 us
    all_to_all x1, blocking collectives, shards(): out = lax.all_to_all(out, ('zhi', 'core'), 0, 0)  15.5 us
    ppermute x4, waiting for transfers between devices, along_x(): return lax.ppermute(value, 'x', [(i, (i + by) % 4) for i in range(4)])  13 us
    ppermute x4, starting transfers between devices, along_x(): return lax.ppermute(value, 'x', [(i, (i + by) % 4) for i in range(4)])  6.47 us
    all_to_all x1, starting transfers between devices, shards(): q = lax.all_to_all(q, ('y', 'zlo', 'zhi', 'core'), 0, 0)  4.04 us
  transfers between devices with their start and end apart: 9, of which 2 were waited for; matrix products, arithmetic and copies ran while one was open for 4% of the time, Pallas kernels for 34%

profile of v1, /device:TPU:0, one launch (start us, length us, event | category | flops | bytes accessed | tf_op | source)
XLA Modules:
  0.0 129.6 jit_solution(3625027527460807711)
XLA Ops:
  0.0 0.0 copy-start
  0.0 1.3 %copy_bitcast_fusion = (bf16[96,16,128]{2,0,1:T(8,128)(2,1)S(1)}, bf16[96,16,128]{2,0,1:T(8,128)(2,1)S(1)}) fusion(bf16[96,2048]{1,0:T(8,128)(2,1)} %param.5, bf16[96,2048]{1,0:T(8,128)(2,1)} %param.6), kind=kLoop, calls=%fused_computation.2 | loop fusion | bytes 1572864 | tf_op jit(solution)/shard_map/reshape | solution.py:242
  1.3 0.1 maximum_bitcast_fusion
  1.4 22.4 %all_to_all.15.refs_1_ = bf16[16,96,256]{2,1,0:T(8,128)(2,1)S(1)} all-to-all(bf16[16,96,256]{2,1,0:T(8,128)(2,1)S(1)} %maximum_bitcast_fusion), channel_id=1, replica_groups=mesh['y'=4,'zlo'=2,'zhi'=2,'x'=4,'core'=2] {'y','zlo','zhi'}, dimensions={0} | all-to-all | bytes 1572864 | tf_op jit(solution)/shard_map/all_to_all | solution.py:244
  23.9 0.0 collective-permute-start.7
  23.9 1.5 %collective-permute-start = (bf16[16,96,256]{2,1,0:T(8,128)(2,1)S(1)}, bf16[16,96,256]{2,1,0:T(8,128)(2,1)S(1)}, u32[]{:S(2)}, u32[]{:S(2)}) collective-permute-start(bf16[16,96,256]{2,1,0:T(8,128)(2,1)S(1)} %all_to_all.15.refs_1_), channel_id=1, source_target_pairs={{0,2},{2,4},{4,6},{6,0},{1,3},{3,5},{5,7},{7,1},{8,10},{10,12},{12... | collective-permute-start | bytes 2359304 | tf_op jit(solution)/shard_map/ppermute | solution.py:232
  25.4 1.7 %collective-permute-start.2 = (bf16[16,96,256]{2,1,0:T(8,128)(2,1)S(1)}, bf16[16,96,256]{2,1,0:T(8,128)(2,1)}, u32[]{:S(2)}, u32[]{:S(2)}) collective-permute-start(bf16[16,96,256]{2,1,0:T(8,128)(2,1)S(1)} %all_to_all.15.refs_1_), channel_id=1, source_target_pairs={{0,6},{2,0},{4,2},{6,4},{1,7},{3,1},{5,3},{7,5},{8,14},{10,8},{12,... | collective-permute-start | bytes 2359304 | tf_op jit(solution)/shard_map/ppermute | solution.py:232
  27.1 0.0 copy-done
  27.1 1.0 bitcast_bitcast_fusion
  28.1 0.0 copy-start.1
  28.1 4.0 %all-to-all-start.1 = ((bf16[32,96,128]{2,1,0:T(8,128)(2,1)}), bf16[32,96,128]{2,1,0:T(8,128)(2,1)S(1)}, u32[]{:S(2)}, u32[]{:S(2)}) async-start(bf16[32,96,128]{2,1,0:T(8,128)(2,1)} %bitcast_bitcast_fusion), calls=%async_computation.1 | async-start | bytes 1572864 | tf_op jit(solution)/shard_map/all_to_all | solution.py:246
  32.2 12.9 %collective-permute-done.refs_1_ = bf16[16,96,256]{2,1,0:T(8,128)(2,1)S(1)} collective-permute-done((bf16[16,96,256]{2,1,0:T(8,128)(2,1)S(1)}, bf16[16,96,256]{2,1,0:T(8,128)(2,1)S(1)}, u32[]{:S(2)}, u32[]{:S(2)}) %collective-permute-start) | collective-permute-done | bytes 786464 | tf_op jit(solution)/shard_map/ppermute | solution.py:232
  45.0 0.0 collective-permute-start.5
  45.0 0.1 collective-permute-done.2.refs_2_
  45.1 0.4 collective-permute-start.6
  45.5 0.8 slice.8
  46.3 1.1 collective-permute-start.1
  47.4 1.8 %slice.9 = bf16[8,96,256]{2,1,0:T(8,128)(2,1)} slice(bf16[16,96,256]{2,1,0:T(8,128)(2,1)} %collective-permute-done.2.refs_2_), slice={[8:16], [0:96], [0:256]} | slice | bytes 786432 | tf_op jit(solution)/shard_map/slice | solution.py:252
  49.2 2.1 %collective-permute-start.3 = (bf16[8,96,256]{2,1,0:T(8,128)(2,1)}, bf16[8,96,256]{2,1,0:T(8,128)(2,1)S(1)}, u32[]{:S(2)}, u32[]{:S(2)}) collective-permute-start(bf16[8,96,256]{2,1,0:T(8,128)(2,1)} %slice.9), channel_id=1, source_target_pairs={{0,6},{2,0},{4,2},{6,4},{1,7},{3,1},{5,3},{7,5},{8,14},{10,8},{12,... | collective-permute-start | bytes 1179656 | tf_op jit(solution)/shard_map/ppermute | solution.py:232
  51.3 0.0 all-to-all-done.1.refs_3_
  51.3 0.0 collective-permute-done.7.refs_2_
  51.3 0.0 copy-done.1
  51.3 15.0 %attend_2_10.1 = (bf16[12,128,256]{2,1,0:T(8,128)(2,1)S(1)}, f32[12,128,256]{2,1,0:T(8,128)S(1)}, f32[12,8,256]{2,1,0:T(8,128)S(1)}) custom-call(s32[32]{0:T(128)S(1)} %copy-done.1, bf16[16,96,256]{2,1,0:T(8,128)(2,1)S(1)} %all_to_all.15.refs_1_, bf16[16,96,256]{2,1,0:T(8,128)(2,1)} %collective-permute-done.7.refs_2_, ...), custom_call_target="tpu_custom_call" | custom-call | flops 4800000000 | bytes 4000000 | tf_op jit(solution)/shard_map/attend_2_10/pallas_call | solution.py:200
  66.3 0.0 collective-permute-done.1
  66.3 1.0 constant_dynamic-update-slice_fusion.1
  67.3 0.0 collective-permute-done.3
  67.4 0.1 collective-permute-start.4
  67.5 0.0 collective-permute-done.5.refs_3_
  67.5 0.0 collective-permute-done.6.refs_4_
  67.5 29.6 %attend_4_00.1 = (bf16[12,128,256]{2,1,0:T(8,128)(2,1)S(1)}, f32[12,128,256]{2,1,0:T(8,128)S(1)}, f32[12,8,256]{2,1,0:T(8,128)S(1)}) custom-call(s32[32]{0:T(128)S(1)} %copy-done.1, bf16[16,96,256]{2,1,0:T(8,128)(2,1)S(1)} %collective-permute-done.refs_1_, bf16[16,96,256]{2,1,0:T(8,128)(2,1)} %collective-permute-done.2.refs_2_, ...), custom_call_target="tpu_custom_call" | custom-call | flops 9600000000 | bytes 4000000 | tf_op jit(solution)/shard_map/attend_4_00/pallas_call | solution.py:200
  97.1 0.0 collective-permute-done.4.refs_2_
  97.1 15.5 %attend_2_01.1 = bf16[4,768,128]{2,1,0:T(8,128)(2,1)S(1)} custom-call(s32[32]{0:T(128)S(1)} %copy-done.1, bf16[16,96,256]{2,1,0:T(8,128)(2,1)S(1)} %constant_dynamic-update-slice_fusion.refs_1_, bf16[16,96,256]{2,1,0:T(8,128)(2,1)S(1)} %collective-permute-done.4.refs_2_, bf16[12,128,256]{2,1,0:T(8,128)(2,1)S(1)} %get-tuple-element.14.refs_3_, ...), custom_call_target="tpu_custom_call" | custom-call | flops 4800000000 | bytes 4000000 | tf_op jit(solution)/shard_map/attend_2_01/pallas_call | solution.py:200
  112.6 15.5 %all_to_all.16 = bf16[4,768,128]{2,1,0:T(8,128)(2,1)S(1)} all-to-all(bf16[4,768,128]{2,1,0:T(8,128)(2,1)S(1)} %attend_2_01.1), channel_id=1, replica_groups=mesh['y'=4,'zlo'=2,'zhi'=2,'x'=4,'core'=2] {'zhi','core'}, dimensions={0} | all-to-all | bytes 1572864 | tf_op jit(solution)/shard_map/all_to_all | solution.py:268
  128.1 0.3 copy.8
  128.4 1.2 copy.9
  (1 shorter events, 0.0 us)
Async XLA Ops:
  0.0 27.1 %copy-start = (bf16[96,4096]{1,0:T(8,128)(2,1)S(1)}, bf16[96,4096]{1,0:T(8,128)(2,1)}, u32[]{:S(2)}) copy-start(bf16[96,4096]{1,0:T(8,128)(2,1)} %param.4) | copy-start | bytes 2359300
  23.9 27.5 %collective-permute-start.7 = (bf16[16,96,256]{2,1,0:T(8,128)(2,1)S(1)}, bf16[16,96,256]{2,1,0:T(8,128)(2,1)}, u32[]{:S(2)}, u32[]{:S(2)}) collective-permute-start(bf16[16,96,256]{2,1,0:T(8,128)(2,1)S(1)} %all_to_all.15.refs_1_), channel_id=1, source_target_pairs={{0,1},{1,0},{2,3},{3,2},{4,5},{5,4},{6,7},{7,6},{8,9},{9,8},{10,11... | collective-permute-start | bytes 2359304 | tf_op jit(solution)/shard_map/ppermute | solution.py:236
  23.9 21.2 %collective-permute-start = (bf16[16,96,256]{2,1,0:T(8,128)(2,1)S(1)}, bf16[16,96,256]{2,1,0:T(8,128)(2,1)S(1)}, u32[]{:S(2)}, u32[]{:S(2)}) collective-permute-start(bf16[16,96,256]{2,1,0:T(8,128)(2,1)S(1)} %all_to_all.15.refs_1_), channel_id=1, source_target_pairs={{0,2},{2,4},{4,6},{6,0},{1,3},{3,5},{5,7},{7,1},{8,10},{10,12},{12... | collective-permute-start | bytes 2359304 | tf_op jit(solution)/shard_map/ppermute | solution.py:232
  25.4 19.8 %collective-permute-start.2 = (bf16[16,96,256]{2,1,0:T(8,128)(2,1)S(1)}, bf16[16,96,256]{2,1,0:T(8,128)(2,1)}, u32[]{:S(2)}, u32[]{:S(2)}) collective-permute-start(bf16[16,96,256]{2,1,0:T(8,128)(2,1)S(1)} %all_to_all.15.refs_1_), channel_id=1, source_target_pairs={{0,6},{2,0},{4,2},{6,4},{1,7},{3,1},{5,3},{7,5},{8,14},{10,8},{12,... | collective-permute-start | bytes 2359304 | tf_op jit(solution)/shard_map/ppermute | solution.py:232
  28.1 23.2 %copy-start.1 = (s32[32]{0:T(128)S(1)}, s32[32]{0:T(128)}, u32[]{:S(2)}) copy-start(s32[32]{0:T(128)} %refs_0_.5) | copy-start | bytes 388
  28.1 23.2 %all-to-all-start.1 = ((bf16[32,96,128]{2,1,0:T(8,128)(2,1)}), bf16[32,96,128]{2,1,0:T(8,128)(2,1)S(1)}, u32[]{:S(2)}, u32[]{:S(2)}) async-start(bf16[32,96,128]{2,1,0:T(8,128)(2,1)} %bitcast_bitcast_fusion), calls=%async_computation.1 | async-start | bytes 1572864 | tf_op jit(solution)/shard_map/all_to_all | solution.py:246
  45.0 22.5 %collective-permute-start.5 = (bf16[16,96,256]{2,1,0:T(8,128)(2,1)S(1)}, bf16[16,96,256]{2,1,0:T(8,128)(2,1)}, u32[]{:S(2)}, u32[]{:S(2)}) collective-permute-start(bf16[16,96,256]{2,1,0:T(8,128)(2,1)S(1)} %collective-permute-done.refs_1_), channel_id=1, source_target_pairs={{0,1},{1,0},{2,3},{3,2},{4,5},{5,4},{6,7},{7,6},{8,9},{9,8},{10,11... | collective-permute-start | bytes 2359304 | tf_op jit(solution)/shard_map/ppermute | solution.py:236
  45.1 22.4 %collective-permute-start.6 = (bf16[16,96,256]{2,1,0:T(8,128)(2,1)}, bf16[16,96,256]{2,1,0:T(8,128)(2,1)}, u32[]{:S(2)}, u32[]{:S(2)}) collective-permute-start(bf16[16,96,256]{2,1,0:T(8,128)(2,1)} %collective-permute-done.2.refs_2_), channel_id=1, source_target_pairs={{0,1},{1,0},{2,3},{3,2},{4,5},{5,4},{6,7},{7,6},{8,9},{9,8},{10,11... | collective-permute-start | bytes 2359304 | tf_op jit(solution)/shard_map/ppermute | solution.py:236
  46.3 20.0 %collective-permute-start.1 = (bf16[8,96,256]{2,1,0:T(8,128)(2,1)}, bf16[8,96,256]{2,1,0:T(8,128)(2,1)}, u32[]{:S(2)}, u32[]{:S(2)}) collective-permute-start(bf16[8,96,256]{2,1,0:T(8,128)(2,1)} %slice.8), channel_id=1, source_target_pairs={{0,2},{2,4},{4,6},{6,0},{1,3},{3,5},{5,7},{7,1},{8,10},{10,12},{12... | collective-permute-start | bytes 1179656 | tf_op jit(solution)/shard_map/ppermute | solution.py:232
  49.2 18.2 %collective-permute-start.3 = (bf16[8,96,256]{2,1,0:T(8,128)(2,1)}, bf16[8,96,256]{2,1,0:T(8,128)(2,1)S(1)}, u32[]{:S(2)}, u32[]{:S(2)}) collective-permute-start(bf16[8,96,256]{2,1,0:T(8,128)(2,1)} %slice.9), channel_id=1, source_target_pairs={{0,6},{2,0},{4,2},{6,4},{1,7},{3,1},{5,3},{7,5},{8,14},{10,8},{12,... | collective-permute-start | bytes 1179656 | tf_op jit(solution)/shard_map/ppermute | solution.py:232
  67.4 29.7 %collective-permute-start.4 = (bf16[16,96,256]{2,1,0:T(8,128)(2,1)S(1)}, bf16[16,96,256]{2,1,0:T(8,128)(2,1)S(1)}, u32[]{:S(2)}, u32[]{:S(2)}) collective-permute-start(bf16[16,96,256]{2,1,0:T(8,128)(2,1)S(1)} %constant_dynamic-update-slice_fusion.refs_1_), channel_id=1, source_target_pairs={{0,1},{1,0},{2,3},{3,2},{4,5},{5,4},{6,7},{7,6},{8,9},{9,8},{10,11... | collective-permute-start | bytes 2359304 | tf_op jit(solution)/shard_map/ppermute | solution.py:236

commit v2 on v1

v2 whole, which is shorter than its diff:
```python
import functools

import jax
import jax.numpy as jnp
from jax import lax
from jax.experimental import pallas as pl
from jax.experimental.pallas import tpu as pltpu
from jax.sharding import Mesh
from jax.sharding import PartitionSpec as P

HEAD = 128
BLK = 384
PIECE = 96
TILE = 256
HALF_BLOCKS = 4
TILES = HALF_BLOCKS * BLK // TILE
UNROLL = 4
SCORE_SCALE = 1.0 / (12.0 * 50.0)
CAP_LOG2E = 50.0 * 1.4426950408889634

AXES = ("y", "zlo", "zhi", "x", "core")
REMOTE, LOCAL = 0, 1


def attend_kernel(*refs, offsets, halves, first, last):
    n_halves = len(halves)
    dummy_tile = n_halves * TILES
    refs = list(refs)
    order = refs.pop(0)
    kv = []
    for _, _, parts in offsets:
        pieces = [refs.pop(0) for _ in range(parts)]
        kv.append([(pieces[0], 0), (pieces[-1], 0 if parts == 2 else 8)])
    if first:
        q_ref = refs.pop(0)
    else:
        states_in = [[refs.pop(0) for _ in range(3)] for _ in halves]
    if last:
        outs = [[refs.pop(0) for _ in range(2)] for _ in halves]
    else:
        states_out = [[refs.pop(0) for _ in range(3)] for _ in halves]
    qt, num, den, qpos, kbuf, vt = refs[:6]
    s_bufs = refs[6 : 6 + UNROLL]
    p_bufs = refs[6 + UNROLL : 6 + 2 * UNROLL]
    rows, q_seq, q_rank, kb_list, kb_start, kb_end, kb_seq = refs[6 + 2 * UNROLL :]

    x = lax.axis_index("x")
    core = lax.axis_index("core")
    zhi = lax.axis_index("zhi")

    lane = lax.broadcasted_iota(jnp.int32, (8, 128), 1)
    where_from = []
    for n, half in enumerate(halves):
        zz = 1 - zhi if half == REMOTE else zhi
        seqs = []
        for slot in range(HALF_BLOCKS):
            yhi, flip = slot // 2, slot % 2
            cc = 1 - core if flip else core
            where_from.append(yhi * 16 + zz * 2 + cc)
            seqs.append(order[2 * (zz * 8 + x * 2 + cc) + yhi])
        for slot in range(HALF_BLOCKS):
            rank = jnp.int32(4 * n)
            for other in range(HALF_BLOCKS):
                if other != slot:
                    rank = rank + (seqs[other] < seqs[slot]).astype(jnp.int32)
            q_seq[rank] = seqs[slot]
            q_rank[4 * n + slot] = rank
    for g in range(2 * n_halves * TILES):
        base = q_seq[g // 3] * BLK + (g % 3) * 128
        qpos[g // 2, :, (g % 2) * 128 : (g % 2) * 128 + 128] = lane + base
    qpos[dummy_tile] = jnp.zeros((8, TILE), jnp.int32)

    if first:
        for slot in range(HALF_BLOCKS * n_halves):
            top = pl.multiple_of(q_rank[slot] * BLK, BLK)
            for sub in range(4):
                rows[pl.ds(top + sub * PIECE, PIECE), :] = q_ref[where_from[slot] + sub * 4]
        for t in range(n_halves * TILES):
            qt[t] = rows[t * TILE : (t + 1) * TILE, :].T
            num[t] = jnp.zeros((HEAD, TILE), jnp.float32)
            den[t] = jnp.zeros((8, TILE), jnp.float32)
    else:
        for n in range(n_halves):
            for t in range(TILES):
                qt[n * TILES + t] = states_in[n][0][t]
                num[n * TILES + t] = states_in[n][1][t]
                den[n * TILES + t] = states_in[n][2][t]
    qt[dummy_tile] = jnp.zeros((HEAD, TILE), jnp.bfloat16)
    num[dummy_tile] = jnp.zeros((HEAD, TILE), jnp.float32)
    den[dummy_tile] = jnp.zeros((8, TILE), jnp.float32)

    count = jnp.int32(0)
    total = jnp.int32(0)
    for n, (dx, flip, _) in enumerate(offsets):
        xs = (x + (4 - dx)) % 4
        cs = 1 - core if flip else core
        for b in range(4):
            yhi, zz = b // 2, b % 2
            kb = 4 * n + b
            vals = []
            for sub in range(4):
                source, at = kv[n][yhi]
                piece = source[at + sub * 2 + zz]
                kbuf[kb, sub * PIECE : (sub + 1) * PIECE, :] = piece[:, :HEAD]
                vals.append(piece[:, HEAD:])
            vt[kb] = jnp.concatenate(vals, axis=0).T
            seq = order[2 * (zz * 8 + xs * 2 + cs) + yhi]
            for h in range(n_halves):
                below = jnp.int32(0)
                for rank in range(HALF_BLOCKS):
                    below = below + (q_seq[4 * h + rank] < seq).astype(jnp.int32)
                start = (3 * below) // 2
                kb_list[count] = jnp.int32(kb)
                kb_start[count] = start + h * TILES
                kb_end[count] = jnp.int32((h + 1) * TILES)
                kb_seq[count] = seq
                count = count + (start < TILES).astype(jnp.int32)
                total = total + (TILES - start)
    for extra in range(2 * UNROLL + 2):
        kb_list[count + extra] = jnp.int32(0)
        kb_start[count + extra] = jnp.int32(dummy_tile)
        kb_end[count + extra] = jnp.int32(0)
        kb_seq[count + extra] = jnp.int32(0)

    def after(item):
        j, t = item
        wrap = t + 1 >= kb_end[j]
        j = jnp.where(wrap, j + 1, j)
        return j, jnp.where(wrap, kb_start[j], t + 1)

    def score(item, s):
        j, t = item
        s[...] = jnp.dot(kbuf[kb_list[j]], qt[t], preferred_element_type=jnp.float32)

    row = lax.broadcasted_iota(jnp.int32, (8, TILE), 0)

    def weigh(item, s, p):
        j, t = item
        rel = qpos[t] - kb_seq[j] * BLK
        acc = None
        for r in range(0, BLK, 16):
            both = []
            for h in range(2):
                z = s[r + 8 * h : r + 8 * h + 8, :]
                w = jnp.exp2(CAP_LOG2E * jnp.tanh(z * SCORE_SCALE))
                w = jnp.where(row + (r + 8 * h) <= rel, w, 0.0)
                acc = w if acc is None else acc + w
                both.append(w)
            p[r : r + 16, :] = jnp.concatenate(both, axis=0).astype(jnp.bfloat16)
        den[t] = den[t] + acc

    def gather(item, p):
        j, t = item
        num[t] = num[t] + jnp.dot(vt[kb_list[j]], p[...], preferred_element_type=jnp.float32)

    items = [(jnp.int32(0), kb_start[0])]
    for _ in range(UNROLL - 1):
        items.append(after(items[-1]))
    for k in range(UNROLL):
        score(items[k], s_bufs[k])
    p_bufs[UNROLL - 1][...] = jnp.zeros((BLK, TILE), jnp.bfloat16)

    def body(_, state):
        cur, prev = state
        nxt = []
        item = cur[-1]
        for _ in range(UNROLL):
            item = after(item)
            nxt.append(item)
        for k in range(UNROLL):
            weigh(cur[k], s_bufs[k], p_bufs[k])
            score(nxt[k], s_bufs[k])
            if k == 0:
                gather(prev, p_bufs[UNROLL - 1])
            else:
                gather(cur[k - 1], p_bufs[k - 1])
        return tuple(nxt), cur[-1]

    idle = (count, jnp.int32(dummy_tile))
    _, tail = lax.fori_loop(0, (total + UNROLL - 1) // UNROLL, body, (tuple(items), idle))
    gather(tail, p_bufs[UNROLL - 1])

    if last:
        for t in range(n_halves * TILES):
            inv = 1.0 / jnp.sum(den[t], axis=0, keepdims=True)
            rows[t * TILE : (t + 1) * TILE, :] = (num[t] * inv).T.astype(jnp.bfloat16)
        for n in range(n_halves):
            for slot in range(HALF_BLOCKS):
                yhi, flip = slot // 2, slot % 2
                top = pl.multiple_of(q_rank[4 * n + slot] * BLK, BLK)
                outs[n][flip][yhi * BLK : (yhi + 1) * BLK, :] = rows[pl.ds(top, BLK), :]
    else:
        for n in range(n_halves):
            for t in range(TILES):
                states_out[n][0][t] = qt[n * TILES + t]
                states_out[n][1][t] = num[n * TILES + t]
                states_out[n][2][t] = den[n * TILES + t]


def attend(order, given, halves, carry, first, last):
    kvs = [piece for pieces, _, _ in given for piece in pieces]
    offsets = tuple((dx, flip, len(pieces)) for pieces, dx, flip in given)
    vmem = pl.BlockSpec(memory_space=pltpu.VMEM)
    smem = pl.BlockSpec(memory_space=pltpu.SMEM)
    nb = 4 * len(given)
    tiles = TILES * len(halves)
    runs = nb * len(halves) + 2 * UNROLL + 4
    if last:
        out = (jax.ShapeDtypeStruct((2 * BLK, HEAD), jnp.bfloat16),) * (2 * len(halves))
    else:
        out = (
            jax.ShapeDtypeStruct((TILES, HEAD, TILE), jnp.bfloat16),
            jax.ShapeDtypeStruct((TILES, HEAD, TILE), jnp.float32),
            jax.ShapeDtypeStruct((TILES, 8, TILE), jnp.float32),
        ) * len(halves)
    inputs = [order, *kvs, *carry]
    return pl.pallas_call(
        functools.partial(attend_kernel, offsets=offsets, halves=halves, first=first, last=last),
        out_shape=out,
        in_specs=[smem] + [vmem] * (len(inputs) - 1),
        out_specs=(vmem,) * len(out),
        scratch_shapes=[
            pltpu.VMEM((tiles + 1, HEAD, TILE), jnp.bfloat16),
            pltpu.VMEM((tiles + 1, HEAD, TILE), jnp.float32),
            pltpu.VMEM((tiles + 1, 8, TILE), jnp.float32),
            pltpu.VMEM((tiles + 1, 8, TILE), jnp.int32),
            pltpu.VMEM((nb, BLK, HEAD), jnp.bfloat16),
            pltpu.VMEM((nb, HEAD, BLK), jnp.bfloat16),
            *[pltpu.VMEM((BLK, TILE), jnp.float32) for _ in range(UNROLL)],
            *[pltpu.VMEM((BLK, TILE), jnp.bfloat16) for _ in range(UNROLL)],
            pltpu.VMEM((tiles * TILE, HEAD), jnp.bfloat16),
            pltpu.SMEM((HALF_BLOCKS * len(halves),), jnp.int32),
            pltpu.SMEM((HALF_BLOCKS * len(halves),), jnp.int32),
            pltpu.SMEM((runs,), jnp.int32),
            pltpu.SMEM((runs,), jnp.int32),
            pltpu.SMEM((runs,), jnp.int32),
            pltpu.SMEM((runs,), jnp.int32),
        ],
        compiler_params=pltpu.CompilerParams(vmem_limit_bytes=36 * 1024 * 1024),
        cost_estimate=pl.CostEstimate(
            flops=len(given) * len(halves) * 1_200_000_000,
            transcendentals=0,
            bytes_accessed=4_000_000,
        ),
    )(*inputs)


def assemble_kernel(own, swapped, z_same, z_cross, out):
    zhi = lax.axis_index("zhi")
    core = lax.axis_index("core")
    for piece, zz, cc in (
        (z_same, 1 - zhi, core),
        (z_cross, 1 - zhi, 1 - core),
        (own, zhi, core),
        (swapped, zhi, 1 - core),
    ):
        left = pl.multiple_of((zz * 2 + cc) * HEAD, HEAD)
        out[:, pl.ds(left, HEAD)] = piece[...]


def along_x(value, by):
    return lax.ppermute(value, "x", [(i, (i + by) % 4) for i in range(4)])


def other_core(value):
    return lax.ppermute(value, "core", [(0, 1), (1, 0)])


def layer(query, key, value, block_order):
    rows = query.shape[0]
    kv = jnp.concatenate(
        [key.reshape(rows, 16, HEAD), value.reshape(rows, 16, HEAD)], axis=2
    ).transpose(1, 0, 2)
    kv = lax.all_to_all(kv, ("y", "zlo", "zhi"), 0, 0)
    q = query.reshape(rows, 32, HEAD).transpose(1, 0, 2)
    q = lax.all_to_all(q, ("y", "zlo", "zhi", "core"), 0, 0)

    up = along_x(kv, 1)
    down = along_x(kv, -1)
    own_o = other_core(kv)
    far_a = along_x(up[:8], 1)
    far_b = along_x(down[8:], -1)
    up_o = other_core(up)
    down_o = other_core(down)
    far_a_o = other_core(far_a)
    far_b_o = other_core(far_b)

    near = [((up,), 1, 0), ((down,), 3, 0)]
    near_o = [((up_o,), 1, 1), ((down_o,), 3, 1)]
    far = [((far_a, far_b), 2, 0), ((far_a_o, far_b_o), 2, 1)]

    def step(given, halves, carry, first=False, last=False):
        return attend(block_order, given, halves, carry, first, last)

    state = step([((kv,), 0, 0)], (REMOTE, LOCAL), (q,), first=True)
    state = step([((own_o,), 0, 1)], (REMOTE, LOCAL), state)
    remote, local = state[:3], state[3:]
    remote = step(near, (REMOTE,), remote)
    remote = step(near_o, (REMOTE,), remote)
    same, cross = step(far, (REMOTE,), remote, last=True)
    z_same = lax.ppermute(same, "zhi", [(0, 1), (1, 0)])
    z_cross = lax.ppermute(cross, ("zhi", "core"), [(i, 3 - i) for i in range(4)])
    own, cross = step(near + near_o + far, (LOCAL,), local, last=True)
    swapped = other_core(cross)
    vmem = pl.BlockSpec(memory_space=pltpu.VMEM)
    return pl.pallas_call(
        assemble_kernel,
        out_shape=jax.ShapeDtypeStruct((2 * BLK, 4 * HEAD), jnp.bfloat16),
        in_specs=[vmem] * 4,
        out_specs=vmem,
        name="assemble",
    )(own, swapped, z_same, z_cross)


def solution(mesh):
    fine = Mesh(mesh.devices.reshape(4, 2, 2, 4, 2), AXES)
    placed = P(("zhi", "x", "core", "y", "zlo"), None)
    return jax.shard_map(
        layer,
        mesh=fine,
        in_specs=(placed, placed, placed, P()),
        out_specs=P(("zhi", "x", "core"), ("y", "zlo")),
        check_vma=False,
    )
```

time: 129 us -> 110 us (0.85)
  the two profiles are of different devices: /device:TPU:0 before, /device:TPU:5 now
where the time goes in v2:
time: 110 us
  Pallas kernels  55.1 us (50%)
  blocking collectives  21.1 us (19%)
  starting transfers between devices  17.5 us (16%)
  waiting for transfers between devices  9.75 us (9%)
  local copies, waits for them, and re-layouts  6.23 us (6%)
    pallas_call x6, Pallas kernels, attend(): pl.pallas_call(functools.partial(attend_kernel, offsets=offsets, halves=h...  52.8 us
    all_to_all x1, blocking collectives, layer(): kv = lax.all_to_all(kv, ('y', 'zlo', 'zhi'), 0, 0)  21.1 us
    ppermute x4, waiting for transfers between devices, along_x(): return lax.ppermute(value, 'x', [(i, (i + by) % 4) for i in range(4)])  8.43 us
    all_to_all x1, starting transfers between devices, layer(): q = lax.all_to_all(q, ('y', 'zlo', 'zhi', 'core'), 0, 0)  5.98 us
    ppermute x6, starting transfers between devices, other_core(): return lax.ppermute(value, 'core', [(0, 1), (1, 0)])  4.93 us
    ppermute x1, starting transfers between devices, layer(): z_same = lax.ppermute(same, 'zhi', [(0, 1), (1, 0)])  3.06 us
    ppermute x4, starting transfers between devices, along_x(): return lax.ppermute(value, 'x', [(i, (i + by) % 4) for i in range(4)])  2.93 us
    pallas_call x1, Pallas kernels, layer(): pl.pallas_call(assemble_kernel, out_shape=jax.ShapeDtypeStruct((2 * BLK,...  2.31 us
  transfers between devices with their start and end apart: 13, of which 2 were waited for; matrix products, arithmetic and copies ran while one was open for 3% of the time, Pallas kernels for 42%

profile of v2, /device:TPU:5, one launch (start us, length us, event | category | flops | bytes accessed | tf_op | source)
XLA Modules:
  0.0 110.0 jit_solution(4213529222808568024)
XLA Ops:
  0.0 0.0 copy-start
  0.0 1.3 %copy_bitcast_fusion = (bf16[96,16,128]{2,0,1:T(8,128)(2,1)S(1)}, bf16[96,16,128]{2,0,1:T(8,128)(2,1)S(1)}) fusion(bf16[96,2048]{1,0:T(8,128)(2,1)} %param.5, bf16[96,2048]{1,0:T(8,128)(2,1)} %param.6), kind=kLoop, calls=%fused_computation.2 | loop fusion | bytes 1572864 | tf_op jit(solution)/shard_map/reshape | solution.py:272
  1.3 0.1 maximum_bitcast_fusion
  1.4 21.1 %all_to_all.10.refs_1_ = bf16[16,96,256]{2,1,0:T(8,128)(2,1)S(1)} all-to-all(bf16[16,96,256]{2,1,0:T(8,128)(2,1)S(1)} %maximum_bitcast_fusion), channel_id=1, replica_groups=mesh['y'=4,'zlo'=2,'zhi'=2,'x'=4,'core'=2] {'y','zlo','zhi'}, dimensions={0} | all-to-all | bytes 1572864 | tf_op jit(solution)/shard_map/all_to_all | solution.py:274
  22.6 0.9 collective-permute-start
  23.5 0.5 collective-permute-start.1
  24.0 0.0 copy-done
  24.0 1.0 bitcast_bitcast_fusion
  25.0 6.0 %all-to-all-start.1 = ((bf16[32,96,128]{2,1,0:T(8,128)(2,1)}), bf16[32,96,128]{2,1,0:T(8,128)(2,1)S(1)}, u32[]{:S(2)}, u32[]{:S(2)}) async-start(bf16[32,96,128]{2,1,0:T(8,128)(2,1)} %bitcast_bitcast_fusion), calls=%async_computation.1 | async-start | bytes 1572864 | tf_op jit(solution)/shard_map/all_to_all | solution.py:276
  31.0 0.0 copy-start.2
  31.0 0.4 collective-permute-start.8
  31.5 8.4 %collective-permute-done.refs_1_ = bf16[16,96,256]{2,1,0:T(8,128)(2,1)S(1)} collective-permute-done((bf16[16,96,256]{2,1,0:T(8,128)(2,1)S(1)}, bf16[16,96,256]{2,1,0:T(8,128)(2,1)S(1)}, u32[]{:S(2)}, u32[]{:S(2)}) %collective-permute-start) | collective-permute-done | bytes 786464 | tf_op jit(solution)/shard_map/ppermute | solution.py:262
  39.9 2.6 %collective-permute-start.2 = (bf16[16,96,256]{2,1,0:T(8,128)(2,1)S(1)}, bf16[16,96,256]{2,1,0:T(8,128)(2,1)}, u32[]{:S(2)}, u32[]{:S(2)}) collective-permute-start(bf16[16,96,256]{2,1,0:T(8,128)(2,1)S(1)} %collective-permute-done.refs_1_), channel_id=1, source_target_pairs={{0,1},{1,0},{2,3},{3,2},{4,5},{5,4},{6,7},{7,6},{8,9},{9,8},{10,11... | collective-permute-start | bytes 2359304 | tf_op jit(solution)/shard_map/ppermute | solution.py:266
  42.5 0.0 collective-permute-done.1.refs_2_
  42.5 1.0 collective-permute-start.3
  43.5 0.8 slice.8
  44.3 1.4 %collective-permute-start.4 = (bf16[8,96,256]{2,1,0:T(8,128)(2,1)}, bf16[8,96,256]{2,1,0:T(8,128)(2,1)S(1)}, u32[]{:S(2)}, u32[]{:S(2)}) collective-permute-start(bf16[8,96,256]{2,1,0:T(8,128)(2,1)} %slice.8), channel_id=1, source_target_pairs={{0,2},{2,4},{4,6},{6,0},{1,3},{3,5},{5,7},{7,1},{8,10},{10,12},{12... | collective-permute-start | bytes 1179656 | tf_op jit(solution)/shard_map/ppermute | solution.py:262
  45.7 1.8 %slice.9 = bf16[8,96,256]{2,1,0:T(8,128)(2,1)} slice(bf16[16,96,256]{2,1,0:T(8,128)(2,1)} %collective-permute-done.1.refs_2_), slice={[8:16], [0:96], [0:256]} | slice | bytes 786432 | tf_op jit(solution)/shard_map/slice | solution.py:282
  47.5 0.1 collective-permute-start.5
  47.5 0.0 all-to-all-done.1.refs_2_
  47.5 0.0 copy-done.2
  47.5 5.2 %shard_map.46 = (bf16[6,128,256]{2,1,0:T(8,128)(2,1)S(1)}, f32[6,128,256]{2,1,0:T(8,128)S(1)}, f32[6,8,256]{2,1,0:T(8,128)S(1)}, bf16[6,128,256]{2,1,0:T(8,128)(...) custom-call(s32[32]{0:T(128)S(1)} %copy-done.2, bf16[16,96,256]{2,1,0:T(8,128)(2,1)S(1)} %all_to_all.10.refs_1_, ...), custom_call_target="tpu_custom_call" | custom-call | flops 2400000000 | bytes 4000000 | tf_op jit(solution)/shard_map/pallas_call | solution.py:217
  52.7 0.0 collective-permute-done.8.refs_1_
  52.7 7.2 %shard_map.47 = (bf16[6,128,256]{2,1,0:T(8,128)(2,1)S(1)}, f32[6,128,256]{2,1,0:T(8,128)S(1)}, f32[6,8,256]{2,1,0:T(8,128)S(1)}, bf16[6,128,256]{2,1,0:T(8,128)(...) custom-call(s32[32]{0:T(128)S(1)} %copy-done.2, bf16[16,96,256]{2,1,0:T(8,128)(2,1)} %collective-permute-done.8.refs_1_, ...), custom_call_target="tpu_custom_call" | custom-call | flops 2400000000 | bytes 4000000 | tf_op jit(solution)/shard_map/pallas_call | solution.py:217
  59.9 0.0 collective-permute-done.4.refs_5_.refs_1_
  59.9 0.6 collective-permute-start.6
  60.6 0.0 collective-permute-done.5.refs_6_.refs_2_
  60.6 0.1 collective-permute-start.7
  60.7 7.6 %shard_map.49 = (bf16[6,128,256]{2,1,0:T(8,128)(2,1)S(1)}, f32[6,128,256]{2,1,0:T(8,128)S(1)}, f32[6,8,256]{2,1,0:T(8,128)S(1)}) custom-call(s32[32]{0:T(128)S(1)} %copy-done.2, bf16[16,96,256]{2,1,0:T(8,128)(2,1)S(1)} %collective-permute-done.refs_1_, bf16[16,96,256]{2,1,0:T(8,128)(2,1)} %collective-permute-done.1.refs_2_, ...), custom_call_target="tpu_custom_call" | custom-call | flops 2400000000 | bytes 4000000 | tf_op jit(solution)/shard_map/pallas_call | solution.py:217
  68.3 0.0 collective-permute-done.2.refs_3_.refs_1_
  68.3 0.0 collective-permute-done.3.refs_4_.refs_2_
  68.3 6.2 %shard_map.50 = (bf16[6,128,256]{2,1,0:T(8,128)(2,1)S(1)}, f32[6,128,256]{2,1,0:T(8,128)S(1)}, f32[6,8,256]{2,1,0:T(8,128)S(1)}) custom-call(s32[32]{0:T(128)S(1)} %copy-done.2, bf16[16,96,256]{2,1,0:T(8,128)(2,1)} %collective-permute-done.2.refs_3_.refs_1_, bf16[16,96,256]{2,1,0:T(8,128)(2,1)} %collective-permute-done.3.refs_4_.refs_2_, ...), custom_call_target="tpu_custom_call" | custom-call | flops 2400000000 | bytes 4000000 | tf_op jit(solution)/shard_map/pallas_call | solution.py:217
  74.5 0.0 collective-permute-done.6.refs_7_.refs_3_
  74.5 0.0 collective-permute-done.7.refs_8_.refs_4_
  74.5 7.1 %shard_map.51 = (bf16[768,128]{1,0:T(8,128)(2,1)S(1)}, bf16[768,128]{1,0:T(8,128)(2,1)S(1)}) custom-call(s32[32]{0:T(128)S(1)} %copy-done.2, bf16[8,96,256]{2,1,0:T(8,128)(2,1)S(1)} %collective-permute-done.4.refs_5_.refs_1_, bf16[8,96,256]{2,1,0:T(8,128)(2,1)} %collective-permute-done.5.refs_6_.refs_2_, ...), custom_call_target="tpu_custom_call" | custom-call | flops 2400000000 | bytes 4000000 | tf_op jit(solution)/shard_map/pallas_call | solution.py:217
  81.6 3.1 %collective-permute-start.10 = (bf16[768,128]{1,0:T(8,128)(2,1)S(1)}, bf16[768,128]{1,0:T(8,128)(2,1)S(1)}, u32[]{:S(2)}, u32[]{:S(2)}) collective-permute-start(bf16[768,128]{1,0:T(8,128)(2,1)S(1)} %get-tuple-element.47), channel_id=1, source_target_pairs={{0,8},{8,0},{1,9},{9,1},{2,10},{10,2},{3,11},{11,3},{4,12},{12,4},... | collective-permute-start | bytes 589832 | tf_op jit(solution)/shard_map/ppermute | solution.py:301
  84.7 0.6 collective-permute-start.11
  85.2 19.6 %shard_map.48 = (bf16[768,128]{1,0:T(8,128)(2,1)S(1)}, bf16[768,128]{1,0:T(8,128)(2,1)S(1)}) custom-call(s32[32]{0:T(128)S(1)} %copy-done.2, bf16[16,96,256]{2,1,0:T(8,128)(2,1)S(1)} %collective-permute-done.refs_1_, bf16[16,96,256]{2,1,0:T(8,128)(2,1)} %collective-permute-done.1.refs_2_, bf16[16,96,256]{2,1,0:T(8,128)(2,1)} %collective-permute-done.2.refs_3_.refs_1_, ...), custom_call_target="tpu_custom_call" | custom-call | flops 7200000000 | bytes 4000000 | tf_op jit(solution)/shard_map/pallas_call | solution.py:217
  104.9 0.0 copy-start.1
  104.9 0.7 copy-done.1
  105.5 0.1 collective-permute-start.9
  105.7 0.0 collective-permute-done.10.z_same
  105.7 0.0 copy-start.3
  105.7 0.0 collective-permute-done.11.z_cross
  105.7 0.0 copy-start.4
  105.7 1.3 %collective-permute-done.9.swapped = bf16[768,128]{1,0:T(8,128)(2,1)S(1)} collective-permute-done((bf16[768,128]{1,0:T(8,128)(2,1)S(1)}, bf16[768,128]{1,0:T(8,128)(2,1)S(1)}, u32[]{:S(2)}, u32[]{:S(2)}) %collective-permute-start.9) | collective-permute-done | bytes 196640 | tf_op jit(solution)/shard_map/ppermute | solution.py:266
  107.0 0.0 copy-start.5
  107.0 0.0 copy-done.3
  107.0 0.0 copy-done.4
  107.0 0.7 copy-done.5
  107.7 2.3 %assemble.1 = bf16[768,512]{1,0:T(8,128)(2,1)} custom-call(bf16[768,128]{1,0:T(8,128)(2,1)} %copy-done.1, bf16[768,128]{1,0:T(8,128)(2,1)} %copy-done.5, bf16[768,128]{1,0:T(8,128)(2,1)} %copy-done.3, bf16[768,128]{1,0:T(8,128)(2,1)} %copy-done.4), custom_call_target="tpu_custom_call" | custom-call | tf_op jit(solution)/shard_map/assemble/pallas_call | solution.py:306
Async XLA Ops:
  0.0 24.0 %copy-start = (bf16[96,4096]{1,0:T(8,128)(2,1)S(1)}, bf16[96,4096]{1,0:T(8,128)(2,1)}, u32[]{:S(2)}) copy-start(bf16[96,4096]{1,0:T(8,128)(2,1)} %param.4) | copy-start | bytes 2359300
  22.6 17.3 %collective-permute-start = (bf16[16,96,256]{2,1,0:T(8,128)(2,1)S(1)}, bf16[16,96,256]{2,1,0:T(8,128)(2,1)S(1)}, u32[]{:S(2)}, u32[]{:S(2)}) collective-permute-start(bf16[16,96,256]{2,1,0:T(8,128)(2,1)S(1)} %all_to_all.10.refs_1_), channel_id=1, source_target_pairs={{0,2},{2,4},{4,6},{6,0},{1,3},{3,5},{5,7},{7,1},{8,10},{10,12},{12... | collective-permute-start | bytes 2359304 | tf_op jit(solution)/shard_map/ppermute | solution.py:262
  23.5 19.0 %collective-permute-start.1 = (bf16[16,96,256]{2,1,0:T(8,128)(2,1)S(1)}, bf16[16,96,256]{2,1,0:T(8,128)(2,1)}, u32[]{:S(2)}, u32[]{:S(2)}) collective-permute-start(bf16[16,96,256]{2,1,0:T(8,128)(2,1)S(1)} %all_to_all.10.refs_1_), channel_id=1, source_target_pairs={{0,6},{2,0},{4,2},{6,4},{1,7},{3,1},{5,3},{7,5},{8,14},{10,8},{12,... | collective-permute-start | bytes 2359304 | tf_op jit(solution)/shard_map/ppermute | solution.py:262
  25.0 22.5 %all-to-all-start.1 = ((bf16[32,96,128]{2,1,0:T(8,128)(2,1)}), bf16[32,96,128]{2,1,0:T(8,128)(2,1)S(1)}, u32[]{:S(2)}, u32[]{:S(2)}) async-start(bf16[32,96,128]{2,1,0:T(8,128)(2,1)} %bitcast_bitcast_fusion), calls=%async_computation.1 | async-start | bytes 1572864 | tf_op jit(solution)/shard_map/all_to_all | solution.py:276
  31.0 16.5 %copy-start.2 = (s32[32]{0:T(128)S(1)}, s32[32]{0:T(128)}, u32[]{:S(2)}) copy-start(s32[32]{0:T(128)} %refs_0_.11) | copy-start | bytes 388
  31.0 21.7 %collective-permute-start.8 = (bf16[16,96,256]{2,1,0:T(8,128)(2,1)S(1)}, bf16[16,96,256]{2,1,0:T(8,128)(2,1)}, u32[]{:S(2)}, u32[]{:S(2)}) collective-permute-start(bf16[16,96,256]{2,1,0:T(8,128)(2,1)S(1)} %all_to_all.10.refs_1_), channel_id=1, source_target_pairs={{0,1},{1,0},{2,3},{3,2},{4,5},{5,4},{6,7},{7,6},{8,9},{9,8},{10,11... | collective-permute-start | bytes 2359304 | tf_op jit(solution)/shard_map/ppermute | solution.py:266
  39.9 28.4 %collective-permute-start.2 = (bf16[16,96,256]{2,1,0:T(8,128)(2,1)S(1)}, bf16[16,96,256]{2,1,0:T(8,128)(2,1)}, u32[]{:S(2)}, u32[]{:S(2)}) collective-permute-start(bf16[16,96,256]{2,1,0:T(8,128)(2,1)S(1)} %collective-permute-done.refs_1_), channel_id=1, source_target_pairs={{0,1},{1,0},{2,3},{3,2},{4,5},{5,4},{6,7},{7,6},{8,9},{9,8},{10,11... | collective-permute-start | bytes 2359304 | tf_op jit(solution)/shard_map/ppermute | solution.py:266
  42.5 25.8 %collective-permute-start.3 = (bf16[16,96,256]{2,1,0:T(8,128)(2,1)}, bf16[16,96,256]{2,1,0:T(8,128)(2,1)}, u32[]{:S(2)}, u32[]{:S(2)}) collective-permute-start(bf16[16,96,256]{2,1,0:T(8,128)(2,1)} %collective-permute-done.1.refs_2_), channel_id=1, source_target_pairs={{0,1},{1,0},{2,3},{3,2},{4,5},{5,4},{6,7},{7,6},{8,9},{9,8},{10,11... | collective-permute-start | bytes 2359304 | tf_op jit(solution)/shard_map/ppermute | solution.py:266
  44.3 15.6 %collective-permute-start.4 = (bf16[8,96,256]{2,1,0:T(8,128)(2,1)}, bf16[8,96,256]{2,1,0:T(8,128)(2,1)S(1)}, u32[]{:S(2)}, u32[]{:S(2)}) collective-permute-start(bf16[8,96,256]{2,1,0:T(8,128)(2,1)} %slice.8), channel_id=1, source_target_pairs={{0,2},{2,4},{4,6},{6,0},{1,3},{3,5},{5,7},{7,1},{8,10},{10,12},{12... | collective-permute-start | bytes 1179656 | tf_op jit(solution)/shard_map/ppermute | solution.py:262
  47.5 13.1 %collective-permute-start.5 = (bf16[8,96,256]{2,1,0:T(8,128)(2,1)}, bf16[8,96,256]{2,1,0:T(8,128)(2,1)}, u32[]{:S(2)}, u32[]{:S(2)}) collective-permute-start(bf16[8,96,256]{2,1,0:T(8,128)(2,1)} %slice.9), channel_id=1, source_target_pairs={{0,6},{2,0},{4,2},{6,4},{1,7},{3,1},{5,3},{7,5},{8,14},{10,8},{12,... | collective-permute-start | bytes 1179656 | tf_op jit(solution)/shard_map/ppermute | solution.py:262
  59.9 14.6 %collective-permute-start.6 = (bf16[8,96,256]{2,1,0:T(8,128)(2,1)S(1)}, bf16[8,96,256]{2,1,0:T(8,128)(2,1)S(1)}, u32[]{:S(2)}, u32[]{:S(2)}) collective-permute-start(bf16[8,96,256]{2,1,0:T(8,128)(2,1)S(1)} %collective-permute-done.4.refs_5_.refs_1_), channel_id=1, source_target_pairs={{0,1},{1,0},{2,3},{3,2},{4,5},{5,4},{6,7},{7,6},{8,9},{9,8},{10,11... | collective-permute-start | bytes 1179656 | tf_op jit(solution)/shard_map/ppermute | solution.py:266
  60.6 14.0 %collective-permute-start.7 = (bf16[8,96,256]{2,1,0:T(8,128)(2,1)}, bf16[8,96,256]{2,1,0:T(8,128)(2,1)S(1)}, u32[]{:S(2)}, u32[]{:S(2)}) collective-permute-start(bf16[8,96,256]{2,1,0:T(8,128)(2,1)} %collective-permute-done.5.refs_6_.refs_2_), channel_id=1, source_target_pairs={{0,1},{1,0},{2,3},{3,2},{4,5},{5,4},{6,7},{7,6},{8,9},{9,8},{10,11... | collective-permute-start | bytes 1179656 | tf_op jit(solution)/shard_map/ppermute | solution.py:266
  81.6 24.1 %collective-permute-start.10 = (bf16[768,128]{1,0:T(8,128)(2,1)S(1)}, bf16[768,128]{1,0:T(8,128)(2,1)S(1)}, u32[]{:S(2)}, u32[]{:S(2)}) collective-permute-start(bf16[768,128]{1,0:T(8,128)(2,1)S(1)} %get-tuple-element.47), channel_id=1, source_target_pairs={{0,8},{8,0},{1,9},{9,1},{2,10},{10,2},{3,11},{11,3},{4,12},{12,4},... | collective-permute-start | bytes 589832 | tf_op jit(solution)/shard_map/ppermute | solution.py:301
  84.7 21.0 %collective-permute-start.11 = (bf16[768,128]{1,0:T(8,128)(2,1)S(1)}, bf16[768,128]{1,0:T(8,128)(2,1)S(1)}, u32[]{:S(2)}, u32[]{:S(2)}) collective-permute-start(bf16[768,128]{1,0:T(8,128)(2,1)S(1)} %get-tuple-element.48), channel_id=1, source_target_pairs={{0,9},{1,8},{8,1},{9,0},{2,11},{3,10},{10,3},{11,2},{4,13},{5,12},... | collective-permute-start | bytes 589832 | tf_op jit(solution)/shard_map/ppermute | solution.py:302
  104.9 0.7 copy-start.1
  105.5 1.4 %collective-permute-start.9 = (bf16[768,128]{1,0:T(8,128)(2,1)S(1)}, bf16[768,128]{1,0:T(8,128)(2,1)S(1)}, u32[]{:S(2)}, u32[]{:S(2)}) collective-permute-start(bf16[768,128]{1,0:T(8,128)(2,1)S(1)} %get-tuple-element.37), channel_id=1, source_target_pairs={{0,1},{1,0},{2,3},{3,2},{4,5},{5,4},{6,7},{7,6},{8,9},{9,8},{10,11... | collective-permute-start | bytes 589832 | tf_op jit(solution)/shard_map/ppermute | solution.py:266
  105.7 1.3 %copy-start.3 = (bf16[768,128]{1,0:T(8,128)(2,1)}, bf16[768,128]{1,0:T(8,128)(2,1)S(1)}, u32[]{:S(2)}) copy-start(bf16[768,128]{1,0:T(8,128)(2,1)S(1)} %collective-permute-done.10.z_same) | copy-start | bytes 589828
  105.7 1.3 %copy-start.4 = (bf16[768,128]{1,0:T(8,128)(2,1)}, bf16[768,128]{1,0:T(8,128)(2,1)S(1)}, u32[]{:S(2)}) copy-start(bf16[768,128]{1,0:T(8,128)(2,1)S(1)} %collective-permute-done.11.z_cross) | copy-start | bytes 589828
  107.0 0.7 copy-start.5

commit v3 on v2

--- a/solution.py
+++ b/solution.py
@@ -23,40 +23,44 @@
 
 
 def attend_kernel(*refs, offsets, halves, first, last):
+    n_shards = len(offsets)
     n_halves = len(halves)
     dummy_tile = n_halves * TILES
     refs = list(refs)
     order = refs.pop(0)
-    kv = []
-    for _, _, parts in offsets:
-        pieces = [refs.pop(0) for _ in range(parts)]
-        kv.append([(pieces[0], 0), (pieces[-1], 0 if parts == 2 else 8)])
+    kv = [[refs.pop(0) for _ in range(2)] for _ in range(n_shards)]
     if first:
-        q_ref = refs.pop(0)
+        q_refs = [refs.pop(0) for _ in range(4)]
     else:
         states_in = [[refs.pop(0) for _ in range(3)] for _ in halves]
     if last:
         outs = [[refs.pop(0) for _ in range(2)] for _ in halves]
     else:
         states_out = [[refs.pop(0) for _ in range(3)] for _ in halves]
-    qt, num, den, qpos, kbuf, vt = refs[:6]
-    s_bufs = refs[6 : 6 + UNROLL]
-    p_bufs = refs[6 + UNROLL : 6 + 2 * UNROLL]
-    rows, q_seq, q_rank, kb_list, kb_start, kb_end, kb_seq = refs[6 + 2 * UNROLL :]
+    qt, num, den, qpos, kbuf, vbuf, vt = refs[:7]
+    s_bufs = refs[7 : 7 + UNROLL]
+    p_bufs = refs[7 + UNROLL : 7 + 2 * UNROLL]
+    rows, q_seq, q_rank, kb_list, kb_start, kb_end, kb_seq = refs[7 + 2 * UNROLL :]
 
     x = lax.axis_index("x")
     core = lax.axis_index("core")
     zhi = lax.axis_index("zhi")
+    zlo = lax.axis_index("zlo")
+    y = lax.axis_index("y")
+
+    def sender(dy, e):
+        ys = (y + (4 - dy)) % 4
+        zl = 1 - zlo if e % 2 else zlo
+        zh = 1 - zhi if e // 2 else zhi
+        return ys // 2, pl.multiple_of(((ys % 2) * 2 + zl) * PIECE, PIECE), zh
 
     lane = lax.broadcasted_iota(jnp.int32, (8, 128), 1)
-    where_from = []
     for n, half in enumerate(halves):
         zz = 1 - zhi if half == REMOTE else zhi
         seqs = []
         for slot in range(HALF_BLOCKS):
             yhi, flip = slot // 2, slot % 2
             cc = 1 - core if flip else core
-            where_from.append(yhi * 16 + zz * 2 + cc)
             seqs.append(order[2 * (zz * 8 + x * 2 + cc) + yhi])
         for slot in range(HALF_BLOCKS):
             rank = jnp.int32(4 * n)
@@ -71,10 +75,13 @@
     qpos[dummy_tile] = jnp.zeros((8, TILE), jnp.int32)
 
     if first:
-        for slot in range(HALF_BLOCKS * n_halves):
-            top = pl.multiple_of(q_rank[slot] * BLK, BLK)
-            for sub in range(4):
-                rows[pl.ds(top + sub * PIECE, PIECE), :] = q_ref[where_from[slot] + sub * 4]
+        for dy in range(4):
+            for e in range(4):
+                yhi, sub, _ = sender(dy, e)
+                n = halves.index(REMOTE if e // 2 else LOCAL)
+                for flip in range(2):
+                    top = q_rank[4 * n + yhi * 2 + flip] * BLK + sub
+                    rows[pl.ds(pl.multiple_of(top, PIECE), PIECE), :] = q_refs[dy][e, flip]
         for t in range(n_halves * TILES):
             qt[t] = rows[t * TILE : (t + 1) * TILE, :].T
             num[t] = jnp.zeros((HEAD, TILE), jnp.float32)
@@ -91,19 +98,20 @@
 
     count = jnp.int32(0)
     total = jnp.int32(0)
-    for n, (dx, flip, _) in enumerate(offsets):
+    for n, (dx, flip) in enumerate(offsets):
+        for dy in range(4):
+            for e in range(4):
+                yhi, sub, zh = sender(dy, e)
+                kb = 4 * n + yhi * 2 + zh
+                piece = kv[n][dy // 2][dy % 2, e]
+                kbuf[kb, pl.ds(sub, PIECE), :] = piece[:, :HEAD]
+                vbuf[kb, pl.ds(sub, PIECE), :] = piece[:, HEAD:]
         xs = (x + (4 - dx)) % 4
         cs = 1 - core if flip else core
         for b in range(4):
             yhi, zz = b // 2, b % 2
             kb = 4 * n + b
-            vals = []
-            for sub in range(4):
-                source, at = kv[n][yhi]
-                piece = source[at + sub * 2 + zz]
-                kbuf[kb, sub * PIECE : (sub + 1) * PIECE, :] = piece[:, :HEAD]
-                vals.append(piece[:, HEAD:])
-            vt[kb] = jnp.concatenate(vals, axis=0).T
+            vt[kb] = vbuf[kb].T
             seq = order[2 * (zz * 8 + xs * 2 + cs) + yhi]
             for h in range(n_halves):
                 below = jnp.int32(0)
@@ -136,14 +144,14 @@
 
     def weigh(item, s, p):
         j, t = item
-        rel = qpos[t] - kb_seq[j] * BLK
+        rel = qpos[t] - (kb_seq[j] * BLK + row)
         acc = None
         for r in range(0, BLK, 16):
             both = []
             for h in range(2):
                 z = s[r + 8 * h : r + 8 * h + 8, :]
                 w = jnp.exp2(CAP_LOG2E * jnp.tanh(z * SCORE_SCALE))
-                w = jnp.where(row + (r + 8 * h) <= rel, w, 0.0)
+                w = jnp.where(rel >= r + 8 * h, w, 0.0)
                 acc = w if acc is None else acc + w
                 both.append(w)
             p[r : r + 16, :] = jnp.concatenate(both, axis=0).astype(jnp.bfloat16)
@@ -199,7 +207,7 @@
 
 def attend(order, given, halves, carry, first, last):
     kvs = [piece for pieces, _, _ in given for piece in pieces]
-    offsets = tuple((dx, flip, len(pieces)) for pieces, dx, flip in given)
+    offsets = tuple((dx, flip) for _, dx, flip in given)
     vmem = pl.BlockSpec(memory_space=pltpu.VMEM)
     smem = pl.BlockSpec(memory_space=pltpu.SMEM)
     nb = 4 * len(given)
@@ -224,6 +232,7 @@
             pltpu.VMEM((tiles + 1, HEAD, TILE), jnp.float32),
             pltpu.VMEM((tiles + 1, 8, TILE), jnp.float32),
             pltpu.VMEM((tiles + 1, 8, TILE), jnp.int32),
+            pltpu.VMEM((nb, BLK, HEAD), jnp.bfloat16),
             pltpu.VMEM((nb, BLK, HEAD), jnp.bfloat16),
             pltpu.VMEM((nb, HEAD, BLK), jnp.bfloat16),
             *[pltpu.VMEM((BLK, TILE), jnp.float32) for _ in range(UNROLL)],
@@ -245,6 +254,52 @@
     )(*inputs)
 
 
+def local_call(body, outs, inputs):
+    vmem = pl.BlockSpec(memory_space=pltpu.VMEM)
+    return pl.pallas_call(
+        body,
+        out_shape=tuple(jax.ShapeDtypeStruct(shape, jnp.bfloat16) for shape in outs),
+        in_specs=[vmem] * len(inputs),
+        out_specs=(vmem,) * len(outs),
+        compiler_params=pltpu.CompilerParams(vmem_limit_bytes=8 * 1024 * 1024),
+    )(*inputs)
+
+
+def sort_kernel(query, key, value, kv0, kv1, kv2, kv3, keep, send):
+    y, zlo, zhi = lax.axis_index("y"), lax.axis_index("zlo"), lax.axis_index("zhi")
+    core = lax.axis_index("core")
+    for e, out in enumerate((kv0, kv1, kv2, kv3)):
+        zl = 1 - zlo if e % 2 else zlo
+        zh = 1 - zhi if e // 2 else zhi
+        for dy in range(4):
+            head = (((y + dy) % 4) * 2 + zl) * 2 + zh
+            at = pl.ds(pl.multiple_of(head * HEAD, HEAD), HEAD)
+            out[dy, :, :HEAD] = key[:, at]
+            out[dy, :, HEAD:] = value[:, at]
+            mine = pl.multiple_of((2 * head + core) * HEAD, HEAD)
+            other = pl.multiple_of((2 * head + 1 - core) * HEAD, HEAD)
+            keep[e, dy] = query[:, pl.ds(mine, HEAD)]
+            send[e, dy] = query[:, pl.ds(other, HEAD)]
+
+
+def join_kernel(keep, got, q0, q1, q2, q3):
+    for e, out in enumerate((q0, q1, q2, q3)):
+        for dy in range(4):
+            out[dy, 0] = keep[e, dy]
+            out[dy, 1] = got[e, dy]
+
+
+def turn_kernel(*refs):
+    for dy in range(4):
+        for e in range(4):
+            refs[4 + dy][e] = refs[e][dy]
+
+
+def pair_kernel(r0, r1, r2, r3, low, high):
+    for dy, ref in enumerate((r0, r1, r2, r3)):
+        (low, high)[dy // 2][dy % 2] = ref[...]
+
+
 def assemble_kernel(own, swapped, z_same, z_cross, out):
     zhi = lax.axis_index("zhi")
     core = lax.axis_index("core")
@@ -258,58 +313,69 @@
         out[:, pl.ds(left, HEAD)] = piece[...]
 
 
-def along_x(value, by):
-    return lax.ppermute(value, "x", [(i, (i + by) % 4) for i in range(4)])
-
-
-def other_core(value):
-    return lax.ppermute(value, "core", [(0, 1), (1, 0)])
+def along(value, axis, by):
+    return lax.ppermute(value, axis, [(i, (i + by) % 4) for i in range(4)])
+
+
+def mirror(value, axes):
+    size = 2 if isinstance(axes, str) else 4
+    return lax.ppermute(value, axes, [(i, size - 1 - i) for i in range(size)])
+
+
+Z_FLIPS = (None, "zlo", "zhi", ("zlo", "zhi"))
 
 
 def layer(query, key, value, block_order):
     rows = query.shape[0]
-    kv = jnp.concatenate(
-        [key.reshape(rows, 16, HEAD), value.reshape(rows, 16, HEAD)], axis=2
-    ).transpose(1, 0, 2)
-    kv = lax.all_to_all(kv, ("y", "zlo", "zhi"), 0, 0)
-    q = query.reshape(rows, 32, HEAD).transpose(1, 0, 2)
-    q = lax.all_to_all(q, ("y", "zlo", "zhi", "core"), 0, 0)
-
-    up = along_x(kv, 1)
-    down = along_x(kv, -1)
-    own_o = other_core(kv)
-    far_a = along_x(up[:8], 1)
-    far_b = along_x(down[8:], -1)
-    up_o = other_core(up)
-    down_o = other_core(down)
-    far_a_o = other_core(far_a)
-    far_b_o = other_core(far_b)
-
-    near = [((up,), 1, 0), ((down,), 3, 0)]
-    near_o = [((up_o,), 1, 1), ((down_o,), 3, 1)]
-    far = [((far_a, far_b), 2, 0), ((far_a_o, far_b_o), 2, 1)]
+    quarter = (4, rows, 2 * HEAD)
+    q_quarter = (4, 2, rows, HEAD)
+    *kv_z, keep, send = local_call(
+        sort_kernel, [quarter] * 4 + [(4, 4, rows, HEAD)] * 2, (query, key, value)
+    )
+    kv_z = [kv_z[0]] + [mirror(kv_z[e], Z_FLIPS[e]) for e in (1, 3, 2)]
+    kv_z = [kv_z[0], kv_z[1], kv_z[3], kv_z[2]]
+    got = mirror(send, "core")
+    q_z = local_call(join_kernel, [q_quarter] * 4, (keep, got))
+    q_z = [q_z[0]] + [mirror(q_z[e], Z_FLIPS[e]) for e in (1, 2, 3)]
+
+    kv_y = local_call(turn_kernel, [quarter] * 4, kv_z)
+    kv_y = [kv_y[0]] + [along(kv_y[d], "y", d) for d in (1, 2, 3)]
+    q_y = local_call(turn_kernel, [q_quarter] * 4, q_z)
+    q_y = [q_y[0]] + [along(q_y[d], "y", d) for d in (1, 2, 3)]
+
+    low, high = local_call(pair_kernel, [(2,) + quarter] * 2, kv_y)
+    up_low = along(low, "x", 1)
+    down_high = along(high, "x", -1)
+    up_high = along(high, "x", 1)
+    down_low = along(low, "x", -1)
+    own_o = [mirror(low, "core"), mirror(high, "core")]
+    far_low = along(up_low, "x", 1)
+    far_high = along(down_high, "x", -1)
+    up_o = [mirror(up_low, "core"), mirror(up_high, "core")]
+    down_o = [mirror(down_low, "core"), mirror(down_high, "core")]
+    far_o = [mirror(far_low, "core"), mirror(far_high, "core")]
+
+    near = [((up_low, up_high), 1, 0), ((down_low, down_high), 3, 0)]
+    near_o = [(up_o, 1, 1), (down_o, 3, 1)]
+    far = [((far_low, far_high), 2, 0), (far_o, 2, 1)]
 
     def step(given, halves, carry, first=False, last=False):
         return attend(block_order, given, halves, carry, first, last)
 
-    state = step([((kv,), 0, 0)], (REMOTE, LOCAL), (q,), first=True)
-    state = step([((own_o,), 0, 1)], (REMOTE, LOCAL), state)
+    both = (REMOTE, LOCAL)
+    state = step([((low, high), 0, 0), (own_o, 0, 1)], both, q_y, first=True)
+    state = step(near, both, state)
     remote, local = state[:3], state[3:]
-    remote = step(near, (REMOTE,), remote)
     remote = step(near_o, (REMOTE,), remote)
     same, cross = step(far, (REMOTE,), remote, last=True)
-    z_same = lax.ppermute(same, "zhi", [(0, 1), (1, 0)])
-    z_cross = lax.ppermute(cross, ("zhi", "core"), [(i, 3 - i) for i in range(4)])
-    own, cross = step(near + near_o + far, (LOCAL,), local, last=True)
-    swapped = other_core(cross)
-    vmem = pl.BlockSpec(memory_space=pltpu.VMEM)
-    return pl.pallas_call(
-        assemble_kernel,
-        out_shape=jax.ShapeDtypeStruct((2 * BLK, 4 * HEAD), jnp.bfloat16),
-        in_specs=[vmem] * 4,
-        out_specs=vmem,
-        name="assemble",
-    )(own, swapped, z_same, z_cross)
+    z_same = mirror(same, "zhi")
+    z_cross = mirror(cross, ("zhi", "core"))
+    own, cross = step(near_o + far, (LOCAL,), local, last=True)
+    swapped = mirror(cross, "core")
+    (out,) = local_call(
+        assemble_kernel, [(2 * BLK, 4 * HEAD)], (own, swapped, z_same, z_cross)
+    )
+    return out
 
 
 def solution(mesh):

time: 110 us -> 124 us (1.13)
  the two profiles are of different devices: /device:TPU:5 before, /device:TPU:37 now
where the time goes in v3:
time: 124 us
  Pallas kernels  50.1 us (40%)
  starting transfers between devices  41.3 us (33%)
  waiting for transfers between devices  29 us (23%)
  local copies, waits for them, and re-layouts  3.13 us (3%)
    pallas_call x5, Pallas kernels, attend(): pl.pallas_call(functools.partial(attend_kernel, offsets=offsets, halves=h...  48.4 us
    ppermute x18, starting transfers between devices, mirror(): return lax.ppermute(value, axes, [(i, size - 1 - i) for i in range(size)])  28 us
    ppermute x18, waiting for transfers between devices, mirror(): return lax.ppermute(value, axes, [(i, size - 1 - i) for i in range(size)])  16.5 us
    ppermute x12, starting transfers between devices, along(): return lax.ppermute(value, axis, [(i, (i + by) % 4) for i in range(4)])  13.3 us
    ppermute x12, waiting for transfers between devices, along(): return lax.ppermute(value, axis, [(i, (i + by) % 4) for i in range(4)])  12.5 us
    unnamed x8, local copies, waits for them, and re-layouts  3.13 us
  transfers between devices with their start and end apart: 30, of which 11 were waited for; matrix products, arithmetic and copies ran while one was open for 0% of the time, Pallas kernels for 34%

profile of v3, /device:TPU:37, one launch (start us, length us, event | category | flops | bytes accessed | tf_op | source)
XLA Modules:
  0.0 123.7 jit_solution(5065008254715580231)
XLA Ops:
  0.0 1.1 copy-done
  1.1 1.0 copy-done.1
  2.1 1.0 copy-done.2
  3.1 0.4 shard_map.46
  3.5 0.1 collective-permute-start
  3.6 2.8 %collective-permute-start.1 = (bf16[4,96,256]{2,1,0:T(8,128)(2,1)S(1)}, bf16[4,96,256]{2,1,0:T(8,128)(2,1)S(1)}, u32[]{:S(2)}, u32[]{:S(2)}) collective-permute-start(bf16[4,96,256]{2,1,0:T(8,128)(2,1)S(1)} %get-tuple-element.46), channel_id=1, source_target_pairs={{0,8},{8,0},{1,9},{9,1},{2,10},{10,2},{3,11},{11,3},{4,12},{12,4},... | collective-permute-start | bytes 589832 | tf_op jit(solution)/shard_map/ppermute | solution.py:322
  6.4 0.2 collective-permute-start.2
  6.6 1.2 collective-permute-start.20
  7.8 1.6 %collective-permute-done.refs_1_ = bf16[4,96,256]{2,1,0:T(8,128)(2,1)S(1)} collective-permute-done((bf16[4,96,256]{2,1,0:T(8,128)(2,1)S(1)}, bf16[4,96,256]{2,1,0:T(8,128)(2,1)S(1)}, u32[]{:S(2)}, u32[]{:S(2)}) %collective-permute-start) | collective-permute-done | bytes 196640 | tf_op jit(solution)/shard_map/ppermute | solution.py:322
  9.4 5.6 %collective-permute-done.1.refs_2_ = bf16[4,96,256]{2,1,0:T(8,128)(2,1)S(1)} collective-permute-done((bf16[4,96,256]{2,1,0:T(8,128)(2,1)S(1)}, bf16[4,96,256]{2,1,0:T(8,128)(2,1)S(1)}, u32[]{:S(2)}, u32[]{:S(2)}) %collective-permute-start.1) | collective-permute-done | bytes 196640 | tf_op jit(solution)/shard_map/ppermute | solution.py:322
  15.0 0.0 collective-permute-done.2.refs_3_
  15.0 0.1 shard_map.47
  15.1 1.4 %collective-permute-start.3 = (bf16[4,96,256]{2,1,0:T(8,128)(2,1)S(1)}, bf16[4,96,256]{2,1,0:T(8,128)(2,1)S(1)}, u32[]{:S(2)}, u32[]{:S(2)}) collective-permute-start(bf16[4,96,256]{2,1,0:T(8,128)(2,1)S(1)} %get-tuple-element.49), channel_id=1, source_target_pairs={{0,32},{32,64},{64,96},{96,0},{1,33},{33,65},{65,97},{97,1},{2,34}... | collective-permute-start | bytes 589832 | tf_op jit(solution)/shard_map/ppermute | solution.py:317
  16.4 2.6 %collective-permute-start.4 = (bf16[4,96,256]{2,1,0:T(8,128)(2,1)S(1)}, bf16[4,96,256]{2,1,0:T(8,128)(2,1)S(1)}, u32[]{:S(2)}, u32[]{:S(2)}) collective-permute-start(bf16[4,96,256]{2,1,0:T(8,128)(2,1)S(1)} %get-tuple-element.50), channel_id=1, source_target_pairs={{0,64},{32,96},{64,0},{96,32},{1,65},{33,97},{65,1},{97,33},{2,66}... | collective-permute-start | bytes 589832 | tf_op jit(solution)/shard_map/ppermute | solution.py:317
  19.1 1.1 collective-permute-start.5
  20.1 0.8 collective-permute-done.3.r1
  20.9 4.1 %collective-permute-done.4.r2 = bf16[4,96,256]{2,1,0:T(8,128)(2,1)S(1)} collective-permute-done((bf16[4,96,256]{2,1,0:T(8,128)(2,1)S(1)}, bf16[4,96,256]{2,1,0:T(8,128)(2,1)S(1)}, u32[]{:S(2)}, u32[]{:S(2)}) %collective-permute-start.4) | collective-permute-done | bytes 196640 | tf_op jit(solution)/shard_map/ppermute | solution.py:317
  25.0 0.0 collective-permute-done.5.r3
  25.0 0.1 shard_map.48
  25.1 4.2 %collective-permute-start.18 = (bf16[2,4,96,256]{3,2,1,0:T(8,128)(2,1)S(1)}, bf16[2,4,96,256]{3,2,1,0:T(8,128)(2,1)S(1)}, u32[]{:S(2)}, u32[]{:S(2)}) collective-permute-start(bf16[2,4,96,256]{3,2,1,0:T(8,128)(2,1)S(1)} %get-tuple-element.52.refs_1_), channel_id=1, source_target_pairs={{0,1},{1,0},{2,3},{3,2},{4,5},{5,4},{6,7},{7,6},{8,9},{9,8},{10,11... | collective-permute-start | bytes 1179656 | tf_op jit(solution)/shard_map/ppermute | solution.py:322
  29.3 0.1 shard_map.49
  29.3 4.7 %collective-permute-start.21 = (bf16[4,2,96,128]{3,2,1,0:T(8,128)(2,1)S(1)}, bf16[4,2,96,128]{3,2,1,0:T(8,128)(2,1)S(1)}, u32[]{:S(2)}, u32[]{:S(2)}) collective-permute-start(bf16[4,2,96,128]{3,2,1,0:T(8,128)(2,1)S(1)} %get-tuple-element.57), channel_id=1, source_target_pairs={{0,16},{16,0},{1,17},{17,1},{2,18},{18,2},{3,19},{19,3},{4,20},{20... | collective-permute-start | bytes 589832 | tf_op jit(solution)/shard_map/ppermute | solution.py:322
  34.1 0.3 collective-permute-start.19
  34.4 0.0 collective-permute-start.22
  34.4 1.1 collective-permute-start.23
  35.4 3.9 %collective-permute-done.21.refs_1_ = bf16[4,2,96,128]{3,2,1,0:T(8,128)(2,1)S(1)} collective-permute-done((bf16[4,2,96,128]{3,2,1,0:T(8,128)(2,1)S(1)}, bf16[4,2,96,128]{3,2,1,0:T(8,128)(2,1)S(1)}, u32[]{:S(2)}, u32[]{:S(2)}) %collective-permute-start.21) | collective-permute-done | bytes 196640 | tf_op jit(solution)/shard_map/ppermute | solution.py:322
  39.3 0.3 collective-permute-start.12
  39.6 3.1 %collective-permute-done.22.refs_2_ = bf16[4,2,96,128]{3,2,1,0:T(8,128)(2,1)S(1)} collective-permute-done((bf16[4,2,96,128]{3,2,1,0:T(8,128)(2,1)S(1)}, bf16[4,2,96,128]{3,2,1,0:T(8,128)(2,1)S(1)}, u32[]{:S(2)}, u32[]{:S(2)}) %collective-permute-start.22) | collective-permute-done | bytes 196640 | tf_op jit(solution)/shard_map/ppermute | solution.py:322
  42.7 0.9 collective-permute-start.6
  43.6 1.3 %collective-permute-done.23.refs_3_ = bf16[4,2,96,128]{3,2,1,0:T(8,128)(2,1)S(1)} collective-permute-done((bf16[4,2,96,128]{3,2,1,0:T(8,128)(2,1)S(1)}, bf16[4,2,96,128]{3,2,1,0:T(8,128)(2,1)S(1)}, u32[]{:S(2)}, u32[]{:S(2)}) %collective-permute-start.23) | collective-permute-done | bytes 196640 | tf_op jit(solution)/shard_map/ppermute | solution.py:322
  44.8 0.1 shard_map.50
  44.9 1.0 collective-permute-start.24
  45.9 0.0 collective-permute-done.18.refs_3_
  45.9 2.1 %collective-permute-start.25 = (bf16[4,2,96,128]{3,2,1,0:T(8,128)(2,1)S(1)}, bf16[4,2,96,128]{3,2,1,0:T(8,128)(2,1)S(1)}, u32[]{:S(2)}, u32[]{:S(2)}) collective-permute-start(bf16[4,2,96,128]{3,2,1,0:T(8,128)(2,1)S(1)} %get-tuple-element.62), channel_id=1, source_target_pairs={{0,64},{32,96},{64,0},{96,32},{1,65},{33,97},{65,1},{97,33},{2,66}... | collective-permute-start | bytes 589832 | tf_op jit(solution)/shard_map/ppermute | solution.py:317
  48.0 1.3 %collective-permute-start.26 = (bf16[4,2,96,128]{3,2,1,0:T(8,128)(2,1)S(1)}, bf16[4,2,96,128]{3,2,1,0:T(8,128)(2,1)S(1)}, u32[]{:S(2)}, u32[]{:S(2)}) collective-permute-start(bf16[4,2,96,128]{3,2,1,0:T(8,128)(2,1)S(1)} %get-tuple-element.63), channel_id=1, source_target_pairs={{0,96},{32,0},{64,32},{96,64},{1,97},{33,1},{65,33},{97,65},{2,98}... | collective-permute-start | bytes 589832 | tf_op jit(solution)/shard_map/ppermute | solution.py:317
  49.3 2.2 %collective-permute-done.24.refs_6_ = bf16[4,2,96,128]{3,2,1,0:T(8,128)(2,1)S(1)} collective-permute-done((bf16[4,2,96,128]{3,2,1,0:T(8,128)(2,1)S(1)}, bf16[4,2,96,128]{3,2,1,0:T(8,128)(2,1)S(1)}, u32[]{:S(2)}, u32[]{:S(2)}) %collective-permute-start.24) | collective-permute-done | bytes 196640 | tf_op jit(solution)/shard_map/ppermute | solution.py:317
  51.6 0.3 collective-permute-start.10
  51.8 4.3 %collective-permute-done.25.refs_7_ = bf16[4,2,96,128]{3,2,1,0:T(8,128)(2,1)S(1)} collective-permute-done((bf16[4,2,96,128]{3,2,1,0:T(8,128)(2,1)S(1)}, bf16[4,2,96,128]{3,2,1,0:T(8,128)(2,1)S(1)}, u32[]{:S(2)}, u32[]{:S(2)}) %collective-permute-start.25) | collective-permute-done | bytes 196640 | tf_op jit(solution)/shard_map/ppermute | solution.py:317
  56.2 0.9 collective-permute-start.8
  57.1 0.0 collective-permute-done.12.refs_4_
  57.1 2.2 %collective-permute-start.13 = (bf16[2,4,96,256]{3,2,1,0:T(8,128)(2,1)S(1)}, bf16[2,4,96,256]{3,2,1,0:T(8,128)(2,1)S(1)}, u32[]{:S(2)}, u32[]{:S(2)}) collective-permute-start(bf16[2,4,96,256]{3,2,1,0:T(8,128)(2,1)S(1)} %collective-permute-done.12.refs_4_), channel_id=1, source_target_pairs={{0,1},{1,0},{2,3},{3,2},{4,5},{5,4},{6,7},{7,6},{8,9},{9,8},{10,11... | collective-permute-start | bytes 1179656 | tf_op jit(solution)/shard_map/ppermute | solution.py:322
  59.3 0.0 collective-permute-done.26.refs_8_
  59.3 0.5 collective-permute-start.15
  59.9 0.9 collective-permute-start.14
  60.8 10.3 %shard_map.51 = (bf16[6,128,256]{2,1,0:T(8,128)(2,1)S(1)}, f32[6,128,256]{2,1,0:T(8,128)S(1)}, f32[6,8,256]{2,1,0:T(8,128)S(1)}, bf16[6,128,256]{2,1,0:T(8,128)(...) custom-call(s32[32]{0:T(128)S(1)} %copy-done.3, bf16[2,4,96,256]{3,2,1,0:T(8,128)(2,1)S(1)} %get-tuple-element.52.refs_1_, ...), custom_call_target="tpu_custom_call" | custom-call | flops 4800000000 | bytes 4000000 | tf_op jit(solution)/shard_map/pallas_call | solution.py:225
  71.1 0.0 collective-permute-done.10.refs_3_
  71.1 0.7 collective-permute-start.7
  71.8 0.1 collective-permute-start.11
  71.9 0.4 collective-permute-start.9
  72.3 1.0 collective-permute-done.14.refs_5_.refs_1_
  73.4 2.8 %collective-permute-start.16 = (bf16[2,4,96,256]{3,2,1,0:T(8,128)(2,1)S(1)}, bf16[2,4,96,256]{3,2,1,0:T(8,128)(2,1)S(1)}, u32[]{:S(2)}, u32[]{:S(2)}) collective-permute-start(bf16[2,4,96,256]{3,2,1,0:T(8,128)(2,1)S(1)} %collective-permute-done.14.refs_5_.refs_1_), channel_id=1, source_target_pairs={{0,1},{1,0},{2,3},{3,2},{4,5},{5,4},{6,7},{7,6},{8,9},{9,8},{10,11... | collective-permute-start | bytes 1179656 | tf_op jit(solution)/shard_map/ppermute | solution.py:322
  76.1 0.0 collective-permute-start.17
  76.1 13.5 %shard_map.52 = (bf16[6,128,256]{2,1,0:T(8,128)(2,1)S(1)}, f32[6,128,256]{2,1,0:T(8,128)S(1)}, f32[6,8,256]{2,1,0:T(8,128)S(1)}, bf16[6,128,256]{2,1,0:T(8,128)(...) custom-call(s32[32]{0:T(128)S(1)} %copy-done.3, ...), custom_call_target="tpu_custom_call" | custom-call | flops 4800000000 | bytes 4000000 | tf_op jit(solution)/shard_map/pallas_call | solution.py:225
  89.7 0.0 collective-permute-done.7.refs_1_
  89.7 0.0 collective-permute-done.11.refs_3_
  89.7 5.5 %shard_map.54 = (bf16[6,128,256]{2,1,0:T(8,128)(2,1)S(1)}, f32[6,128,256]{2,1,0:T(8,128)S(1)}, f32[6,8,256]{2,1,0:T(8,128)S(1)}) custom-call(s32[32]{0:T(128)S(1)} %copy-done.3, bf16[2,4,96,256]{3,2,1,0:T(8,128)(2,1)S(1)} %collective-permute-done.7.refs_1_, bf16[2,4,96,256]{3,2,1,0:T(8,128)(2,1)S(1)} %collective-permute-done.9.refs_2_, ...), custom_call_target="tpu_custom_call" | custom-call | flops 2400000000 | bytes 4000000 | tf_op jit(solution)/shard_map/pallas_call | solution.py:225
  95.2 0.0 collective-permute-done.16.refs_7_.refs_3_
  95.2 6.8 %shard_map.55 = (bf16[768,128]{1,0:T(8,128)(2,1)S(1)}, bf16[768,128]{1,0:T(8,128)(2,1)S(1)}) custom-call(s32[32]{0:T(128)S(1)} %copy-done.3, bf16[2,4,96,256]{3,2,1,0:T(8,128)(2,1)S(1)} %collective-permute-done.14.refs_5_.refs_1_, bf16[2,4,96,256]{3,2,1,0:T(8,128)(2,1)S(1)} %collective-permute-done.15.refs_6_.refs_2_, ...), custom_call_target="tpu_custom_call" | custom-call | flops 2400000000 | bytes 4000000 | tf_op jit(solution)/shard_map/pallas_call | solution.py:225
  102.0 5.6 %collective-permute-start.28 = (bf16[768,128]{1,0:T(8,128)(2,1)S(1)}, bf16[768,128]{1,0:T(8,128)(2,1)S(1)}, u32[]{:S(2)}, u32[]{:S(2)}) collective-permute-start(bf16[768,128]{1,0:T(8,128)(2,1)S(1)} %get-tuple-element.81), channel_id=1, source_target_pairs={{0,8},{8,0},{1,9},{9,1},{2,10},{10,2},{3,11},{11,3},{4,12},{12,4},... | collective-permute-start | bytes 589832 | tf_op jit(solution)/shard_map/ppermute | solution.py:322
  107.6 12.3 %shard_map.53 = (bf16[768,128]{1,0:T(8,128)(2,1)S(1)}, bf16[768,128]{1,0:T(8,128)(2,1)S(1)}) custom-call(s32[32]{0:T(128)S(1)} %copy-done.3, bf16[2,4,96,256]{3,2,1,0:T(8,128)(2,1)S(1)} %collective-permute-done.7.refs_1_, bf16[2,4,96,256]{3,2,1,0:T(8,128)(2,1)S(1)} %collective-permute-done.9.refs_2_, ...), custom_call_target="tpu_custom_call" | custom-call | flops 4800000000 | bytes 4000000 | tf_op jit(solution)/shard_map/pallas_call | solution.py:225
  119.9 1.7 %collective-permute-start.27 = (bf16[768,128]{1,0:T(8,128)(2,1)S(1)}, bf16[768,128]{1,0:T(8,128)(2,1)S(1)}, u32[]{:S(2)}, u32[]{:S(2)}) collective-permute-start(bf16[768,128]{1,0:T(8,128)(2,1)S(1)} %get-tuple-element.74), channel_id=1, source_target_pairs={{0,1},{1,0},{2,3},{3,2},{4,5},{5,4},{6,7},{7,6},{8,9},{9,8},{10,11... | collective-permute-start | bytes 589832 | tf_op jit(solution)/shard_map/ppermute | solution.py:322
  121.6 0.0 collective-permute-done.28.z_same
  121.6 1.1 collective-permute-done.27.swapped
  122.6 1.1 shard_map.56
  (15 shorter events, 0.0 us)
Async XLA Ops:
  0.0 1.1 copy-start
  1.1 1.0 copy-start.1
  2.1 1.0 copy-start.2
  3.5 5.9 %collective-permute-start = (bf16[4,96,256]{2,1,0:T(8,128)(2,1)S(1)}, bf16[4,96,256]{2,1,0:T(8,128)(2,1)S(1)}, u32[]{:S(2)}, u32[]{:S(2)}) collective-permute-start(bf16[4,96,256]{2,1,0:T(8,128)(2,1)S(1)} %get-tuple-element.45), channel_id=1, source_target_pairs={{0,16},{16,0},{1,17},{17,1},{2,18},{18,2},{3,19},{19,3},{4,20},{20... | collective-permute-start | bytes 589832 | tf_op jit(solution)/shard_map/ppermute | solution.py:322
  3.6 11.4 %collective-permute-start.1 = (bf16[4,96,256]{2,1,0:T(8,128)(2,1)S(1)}, bf16[4,96,256]{2,1,0:T(8,128)(2,1)S(1)}, u32[]{:S(2)}, u32[]{:S(2)}) collective-permute-start(bf16[4,96,256]{2,1,0:T(8,128)(2,1)S(1)} %get-tuple-element.46), channel_id=1, source_target_pairs={{0,8},{8,0},{1,9},{9,1},{2,10},{10,2},{3,11},{11,3},{4,12},{12,4},... | collective-permute-start | bytes 589832 | tf_op jit(solution)/shard_map/ppermute | solution.py:322
  6.4 8.6 %collective-permute-start.2 = (bf16[4,96,256]{2,1,0:T(8,128)(2,1)S(1)}, bf16[4,96,256]{2,1,0:T(8,128)(2,1)S(1)}, u32[]{:S(2)}, u32[]{:S(2)}) collective-permute-start(bf16[4,96,256]{2,1,0:T(8,128)(2,1)S(1)} %get-tuple-element.47), channel_id=1, source_target_pairs={{0,24},{8,16},{16,8},{24,0},{1,25},{9,17},{17,9},{25,1},{2,26},{10... | collective-permute-start | bytes 589832 | tf_op jit(solution)/shard_map/ppermute | solution.py:322
  6.6 22.7 %collective-permute-start.20 = (bf16[4,4,96,128]{3,2,1,0:T(8,128)(2,1)S(1)}, bf16[4,4,96,128]{3,2,1,0:T(8,128)(2,1)S(1)}, u32[]{:S(2)}, u32[]{:S(2)}) collective-permute-start(bf16[4,4,96,128]{3,2,1,0:T(8,128)(2,1)S(1)} %get-tuple-element.55), channel_id=1, source_target_pairs={{0,1},{1,0},{2,3},{3,2},{4,5},{5,4},{6,7},{7,6},{8,9},{9,8},{10,11... | collective-permute-start | bytes 1179656 | tf_op jit(solution)/shard_map/ppermute | solution.py:322
  15.1 5.9 %collective-permute-start.3 = (bf16[4,96,256]{2,1,0:T(8,128)(2,1)S(1)}, bf16[4,96,256]{2,1,0:T(8,128)(2,1)S(1)}, u32[]{:S(2)}, u32[]{:S(2)}) collective-permute-start(bf16[4,96,256]{2,1,0:T(8,128)(2,1)S(1)} %get-tuple-element.49), channel_id=1, source_target_pairs={{0,32},{32,64},{64,96},{96,0},{1,33},{33,65},{65,97},{97,1},{2,34}... | collective-permute-start | bytes 589832 | tf_op jit(solution)/shard_map/ppermute | solution.py:317
  16.4 8.6 %collective-permute-start.4 = (bf16[4,96,256]{2,1,0:T(8,128)(2,1)S(1)}, bf16[4,96,256]{2,1,0:T(8,128)(2,1)S(1)}, u32[]{:S(2)}, u32[]{:S(2)}) collective-permute-start(bf16[4,96,256]{2,1,0:T(8,128)(2,1)S(1)} %get-tuple-element.50), channel_id=1, source_target_pairs={{0,64},{32,96},{64,0},{96,32},{1,65},{33,97},{65,1},{97,33},{2,66}... | collective-permute-start | bytes 589832 | tf_op jit(solution)/shard_map/ppermute | solution.py:317
  19.1 6.0 %collective-permute-start.5 = (bf16[4,96,256]{2,1,0:T(8,128)(2,1)S(1)}, bf16[4,96,256]{2,1,0:T(8,128)(2,1)S(1)}, u32[]{:S(2)}, u32[]{:S(2)}) collective-permute-start(bf16[4,96,256]{2,1,0:T(8,128)(2,1)S(1)} %get-tuple-element.51), channel_id=1, source_target_pairs={{0,96},{32,0},{64,32},{96,64},{1,97},{33,1},{65,33},{97,65},{2,98}... | collective-permute-start | bytes 589832 | tf_op jit(solution)/shard_map/ppermute | solution.py:317
  25.1 20.8 %collective-permute-start.18 = (bf16[2,4,96,256]{3,2,1,0:T(8,128)(2,1)S(1)}, bf16[2,4,96,256]{3,2,1,0:T(8,128)(2,1)S(1)}, u32[]{:S(2)}, u32[]{:S(2)}) collective-permute-start(bf16[2,4,96,256]{3,2,1,0:T(8,128)(2,1)S(1)} %get-tuple-element.52.refs_1_), channel_id=1, source_target_pairs={{0,1},{1,0},{2,3},{3,2},{4,5},{5,4},{6,7},{7,6},{8,9},{9,8},{10,11... | collective-permute-start | bytes 1179656 | tf_op jit(solution)/shard_map/ppermute | solution.py:322
  29.3 10.0 %collective-permute-start.21 = (bf16[4,2,96,128]{3,2,1,0:T(8,128)(2,1)S(1)}, bf16[4,2,96,128]{3,2,1,0:T(8,128)(2,1)S(1)}, u32[]{:S(2)}, u32[]{:S(2)}) collective-permute-start(bf16[4,2,96,128]{3,2,1,0:T(8,128)(2,1)S(1)} %get-tuple-element.57), channel_id=1, source_target_pairs={{0,16},{16,0},{1,17},{17,1},{2,18},{18,2},{3,19},{19,3},{4,20},{20... | collective-permute-start | bytes 589832 | tf_op jit(solution)/shard_map/ppermute | solution.py:322
  34.1 14.0 %collective-permute-start.19 = (bf16[2,4,96,256]{3,2,1,0:T(8,128)(2,1)S(1)}, bf16[2,4,96,256]{3,2,1,0:T(8,128)(2,1)S(1)}, u32[]{:S(2)}, u32[]{:S(2)}) collective-permute-start(bf16[2,4,96,256]{3,2,1,0:T(8,128)(2,1)S(1)} %get-tuple-element.53.refs_2_), channel_id=1, source_target_pairs={{0,1},{1,0},{2,3},{3,2},{4,5},{5,4},{6,7},{7,6},{8,9},{9,8},{10,11... | collective-permute-start | bytes 1179656 | tf_op jit(solution)/shard_map/ppermute | solution.py:322
  34.4 8.3 %collective-permute-start.22 = (bf16[4,2,96,128]{3,2,1,0:T(8,128)(2,1)S(1)}, bf16[4,2,96,128]{3,2,1,0:T(8,128)(2,1)S(1)}, u32[]{:S(2)}, u32[]{:S(2)}) collective-permute-start(bf16[4,2,96,128]{3,2,1,0:T(8,128)(2,1)S(1)} %get-tuple-element.58), channel_id=1, source_target_pairs={{0,8},{8,0},{1,9},{9,1},{2,10},{10,2},{3,11},{11,3},{4,12},{12,4},... | collective-permute-start | bytes 589832 | tf_op jit(solution)/shard_map/ppermute | solution.py:322
  34.4 10.5 %collective-permute-start.23 = (bf16[4,2,96,128]{3,2,1,0:T(8,128)(2,1)S(1)}, bf16[4,2,96,128]{3,2,1,0:T(8,128)(2,1)S(1)}, u32[]{:S(2)}, u32[]{:S(2)}) collective-permute-start(bf16[4,2,96,128]{3,2,1,0:T(8,128)(2,1)S(1)} %get-tuple-element.59), channel_id=1, source_target_pairs={{0,24},{8,16},{16,8},{24,0},{1,25},{9,17},{17,9},{25,1},{2,26},{10... | collective-permute-start | bytes 589832 | tf_op jit(solution)/shard_map/ppermute | solution.py:322
  39.3 17.8 %collective-permute-start.12 = (bf16[2,4,96,256]{3,2,1,0:T(8,128)(2,1)S(1)}, bf16[2,4,96,256]{3,2,1,0:T(8,128)(2,1)S(1)}, u32[]{:S(2)}, u32[]{:S(2)}) collective-permute-start(bf16[2,4,96,256]{3,2,1,0:T(8,128)(2,1)S(1)} %get-tuple-element.53.refs_2_), channel_id=1, source_target_pairs={{0,6},{2,0},{4,2},{6,4},{1,7},{3,1},{5,3},{7,5},{8,14},{10,8},{12,... | collective-permute-start | bytes 1179656 | tf_op jit(solution)/shard_map/ppermute | solution.py:317
  42.7 17.2 %collective-permute-start.6 = (bf16[2,4,96,256]{3,2,1,0:T(8,128)(2,1)S(1)}, bf16[2,4,96,256]{3,2,1,0:T(8,128)(2,1)S(1)}, u32[]{:S(2)}, u32[]{:S(2)}) collective-permute-start(bf16[2,4,96,256]{3,2,1,0:T(8,128)(2,1)S(1)} %get-tuple-element.52.refs_1_), channel_id=1, source_target_pairs={{0,2},{2,4},{4,6},{6,0},{1,3},{3,5},{5,7},{7,1},{8,10},{10,12},{12... | collective-permute-start | bytes 1179656 | tf_op jit(solution)/shard_map/ppermute | solution.py:317
  44.9 6.7 %collective-permute-start.24 = (bf16[4,2,96,128]{3,2,1,0:T(8,128)(2,1)S(1)}, bf16[4,2,96,128]{3,2,1,0:T(8,128)(2,1)S(1)}, u32[]{:S(2)}, u32[]{:S(2)}) collective-permute-start(bf16[4,2,96,128]{3,2,1,0:T(8,128)(2,1)S(1)} %get-tuple-element.61), channel_id=1, source_target_pairs={{0,32},{32,64},{64,96},{96,0},{1,33},{33,65},{65,97},{97,1},{2,34}... | collective-permute-start | bytes 589832 | tf_op jit(solution)/shard_map/ppermute | solution.py:317
  45.9 10.3 %collective-permute-start.25 = (bf16[4,2,96,128]{3,2,1,0:T(8,128)(2,1)S(1)}, bf16[4,2,96,128]{3,2,1,0:T(8,128)(2,1)S(1)}, u32[]{:S(2)}, u32[]{:S(2)}) collective-permute-start(bf16[4,2,96,128]{3,2,1,0:T(8,128)(2,1)S(1)} %get-tuple-element.62), channel_id=1, source_target_pairs={{0,64},{32,96},{64,0},{96,32},{1,65},{33,97},{65,1},{97,33},{2,66}... | collective-permute-start | bytes 589832 | tf_op jit(solution)/shard_map/ppermute | solution.py:317
  48.0 12.7 %copy-start.3 = (s32[32]{0:T(128)S(1)}, s32[32]{0:T(128)}, u32[]{:S(2)}) copy-start(s32[32]{0:T(128)} %refs_0_.9) | copy-start | bytes 388
  48.0 11.3 %collective-permute-start.26 = (bf16[4,2,96,128]{3,2,1,0:T(8,128)(2,1)S(1)}, bf16[4,2,96,128]{3,2,1,0:T(8,128)(2,1)S(1)}, u32[]{:S(2)}, u32[]{:S(2)}) collective-permute-start(bf16[4,2,96,128]{3,2,1,0:T(8,128)(2,1)S(1)} %get-tuple-element.63), channel_id=1, source_target_pairs={{0,96},{32,0},{64,32},{96,64},{1,97},{33,1},{65,33},{97,65},{2,98}... | collective-permute-start | bytes 589832 | tf_op jit(solution)/shard_map/ppermute | solution.py:317
  51.6 19.5 %collective-permute-start.10 = (bf16[2,4,96,256]{3,2,1,0:T(8,128)(2,1)S(1)}, bf16[2,4,96,256]{3,2,1,0:T(8,128)(2,1)S(1)}, u32[]{:S(2)}, u32[]{:S(2)}) collective-permute-start(bf16[2,4,96,256]{3,2,1,0:T(8,128)(2,1)S(1)} %get-tuple-element.52.refs_1_), channel_id=1, source_target_pairs={{0,6},{2,0},{4,2},{6,4},{1,7},{3,1},{5,3},{7,5},{8,14},{10,8},{12,... | collective-permute-start | bytes 1179656 | tf_op jit(solution)/shard_map/ppermute | solution.py:317
  56.2 15.6 %collective-permute-start.8 = (bf16[2,4,96,256]{3,2,1,0:T(8,128)(2,1)S(1)}, bf16[2,4,96,256]{3,2,1,0:T(8,128)(2,1)S(1)}, u32[]{:S(2)}, u32[]{:S(2)}) collective-permute-start(bf16[2,4,96,256]{3,2,1,0:T(8,128)(2,1)S(1)} %get-tuple-element.53.refs_2_), channel_id=1, source_target_pairs={{0,2},{2,4},{4,6},{6,0},{1,3},{3,5},{5,7},{7,1},{8,10},{10,12},{12... | collective-permute-start | bytes 1179656 | tf_op jit(solution)/shard_map/ppermute | solution.py:317
  57.1 14.8 %collective-permute-start.13 = (bf16[2,4,96,256]{3,2,1,0:T(8,128)(2,1)S(1)}, bf16[2,4,96,256]{3,2,1,0:T(8,128)(2,1)S(1)}, u32[]{:S(2)}, u32[]{:S(2)}) collective-permute-start(bf16[2,4,96,256]{3,2,1,0:T(8,128)(2,1)S(1)} %collective-permute-done.12.refs_4_), channel_id=1, source_target_pairs={{0,1},{1,0},{2,3},{3,2},{4,5},{5,4},{6,7},{7,6},{8,9},{9,8},{10,11... | collective-permute-start | bytes 1179656 | tf_op jit(solution)/shard_map/ppermute | solution.py:322
  59.3 16.8 %collective-permute-start.15 = (bf16[2,4,96,256]{3,2,1,0:T(8,128)(2,1)S(1)}, bf16[2,4,96,256]{3,2,1,0:T(8,128)(2,1)S(1)}, u32[]{:S(2)}, u32[]{:S(2)}) collective-permute-start(bf16[2,4,96,256]{3,2,1,0:T(8,128)(2,1)S(1)} %collective-permute-done.12.refs_4_), channel_id=1, source_target_pairs={{0,6},{2,0},{4,2},{6,4},{1,7},{3,1},{5,3},{7,5},{8,14},{10,8},{12,... | collective-permute-start | bytes 1179656 | tf_op jit(solution)/shard_map/ppermute | solution.py:317
  59.9 13.5 %collective-permute-start.14 = (bf16[2,4,96,256]{3,2,1,0:T(8,128)(2,1)S(1)}, bf16[2,4,96,256]{3,2,1,0:T(8,128)(2,1)S(1)}, u32[]{:S(2)}, u32[]{:S(2)}) collective-permute-start(bf16[2,4,96,256]{3,2,1,0:T(8,128)(2,1)S(1)} %collective-permute-done.6.refs_1_), channel_id=1, source_target_pairs={{0,2},{2,4},{4,6},{6,0},{1,3},{3,5},{5,7},{7,1},{8,10},{10,12},{12... | collective-permute-start | bytes 1179656 | tf_op jit(solution)/shard_map/ppermute | solution.py:317
  71.1 18.5 %collective-permute-start.7 = (bf16[2,4,96,256]{3,2,1,0:T(8,128)(2,1)S(1)}, bf16[2,4,96,256]{3,2,1,0:T(8,128)(2,1)S(1)}, u32[]{:S(2)}, u32[]{:S(2)}) collective-permute-start(bf16[2,4,96,256]{3,2,1,0:T(8,128)(2,1)S(1)} %collective-permute-done.6.refs_1_), channel_id=1, source_target_pairs={{0,1},{1,0},{2,3},{3,2},{4,5},{5,4},{6,7},{7,6},{8,9},{9,8},{10,11... | collective-permute-start | bytes 1179656 | tf_op jit(solution)/shard_map/ppermute | solution.py:322
  71.8 17.9 %collective-permute-start.11 = (bf16[2,4,96,256]{3,2,1,0:T(8,128)(2,1)S(1)}, bf16[2,4,96,256]{3,2,1,0:T(8,128)(2,1)S(1)}, u32[]{:S(2)}, u32[]{:S(2)}) collective-permute-start(bf16[2,4,96,256]{3,2,1,0:T(8,128)(2,1)S(1)} %collective-permute-done.10.refs_3_), channel_id=1, source_target_pairs={{0,1},{1,0},{2,3},{3,2},{4,5},{5,4},{6,7},{7,6},{8,9},{9,8},{10,11... | collective-permute-start | bytes 1179656 | tf_op jit(solution)/shard_map/ppermute | solution.py:322
  71.9 17.8 %collective-permute-start.9 = (bf16[2,4,96,256]{3,2,1,0:T(8,128)(2,1)S(1)}, bf16[2,4,96,256]{3,2,1,0:T(8,128)(2,1)S(1)}, u32[]{:S(2)}, u32[]{:S(2)}) collective-permute-start(bf16[2,4,96,256]{3,2,1,0:T(8,128)(2,1)S(1)} %collective-permute-done.8.refs_2_), channel_id=1, source_target_pairs={{0,1},{1,0},{2,3},{3,2},{4,5},{5,4},{6,7},{7,6},{8,9},{9,8},{10,11... | collective-permute-start | bytes 1179656 | tf_op jit(solution)/shard_map/ppermute | solution.py:322
  73.4 21.9 %collective-permute-start.16 = (bf16[2,4,96,256]{3,2,1,0:T(8,128)(2,1)S(1)}, bf16[2,4,96,256]{3,2,1,0:T(8,128)(2,1)S(1)}, u32[]{:S(2)}, u32[]{:S(2)}) collective-permute-start(bf16[2,4,96,256]{3,2,1,0:T(8,128)(2,1)S(1)} %collective-permute-done.14.refs_5_.refs_1_), channel_id=1, source_target_pairs={{0,1},{1,0},{2,3},{3,2},{4,5},{5,4},{6,7},{7,6},{8,9},{9,8},{10,11... | collective-permute-start | bytes 1179656 | tf_op jit(solution)/shard_map/ppermute | solution.py:322
  76.1 19.1 %collective-permute-start.17 = (bf16[2,4,96,256]{3,2,1,0:T(8,128)(2,1)S(1)}, bf16[2,4,96,256]{3,2,1,0:T(8,128)(2,1)S(1)}, u32[]{:S(2)}, u32[]{:S(2)}) collective-permute-start(bf16[2,4,96,256]{3,2,1,0:T(8,128)(2,1)S(1)} %collective-permute-done.15.refs_6_.refs_2_), channel_id=1, source_target_pairs={{0,1},{1,0},{2,3},{3,2},{4,5},{5,4},{6,7},{7,6},{8,9},{9,8},{10,11... | collective-permute-start | bytes 1179656 | tf_op jit(solution)/shard_map/ppermute | solution.py:322
  102.0 19.6 %collective-permute-start.28 = (bf16[768,128]{1,0:T(8,128)(2,1)S(1)}, bf16[768,128]{1,0:T(8,128)(2,1)S(1)}, u32[]{:S(2)}, u32[]{:S(2)}) collective-permute-start(bf16[768,128]{1,0:T(8,128)(2,1)S(1)} %get-tuple-element.81), channel_id=1, source_target_pairs={{0,8},{8,0},{1,9},{9,1},{2,10},{10,2},{3,11},{11,3},{4,12},{12,4},... | collective-permute-start | bytes 589832 | tf_op jit(solution)/shard_map/ppermute | solution.py:322
  107.6 14.0 %collective-permute-start.29 = (bf16[768,128]{1,0:T(8,128)(2,1)S(1)}, bf16[768,128]{1,0:T(8,128)(2,1)S(1)}, u32[]{:S(2)}, u32[]{:S(2)}) collective-permute-start(bf16[768,128]{1,0:T(8,128)(2,1)S(1)} %get-tuple-element.82), channel_id=1, source_target_pairs={{0,9},{1,8},{8,1},{9,0},{2,11},{3,10},{10,3},{11,2},{4,13},{5,12},... | collective-permute-start | bytes 589832 | tf_op jit(solution)/shard_map/ppermute | solution.py:322
  119.9 2.7 %collective-permute-start.27 = (bf16[768,128]{1,0:T(8,128)(2,1)S(1)}, bf16[768,128]{1,0:T(8,128)(2,1)S(1)}, u32[]{:S(2)}, u32[]{:S(2)}) collective-permute-start(bf16[768,128]{1,0:T(8,128)(2,1)S(1)} %get-tuple-element.74), channel_id=1, source_target_pairs={{0,1},{1,0},{2,3},{3,2},{4,5},{5,4},{6,7},{7,6},{8,9},{9,8},{10,11... | collective-permute-start | bytes 589832 | tf_op jit(solution)/shard_map/ppermute | solution.py:322

commit v4 on v2

--- a/solution.py
+++ b/solution.py
@@ -23,16 +23,14 @@
 
 
 def attend_kernel(*refs, offsets, halves, first, last):
+    n_shards = len(offsets)
     n_halves = len(halves)
     dummy_tile = n_halves * TILES
     refs = list(refs)
     order = refs.pop(0)
-    kv = []
-    for _, _, parts in offsets:
-        pieces = [refs.pop(0) for _ in range(parts)]
-        kv.append([(pieces[0], 0), (pieces[-1], 0 if parts == 2 else 8)])
+    kv = [refs.pop(0) for _ in range(n_shards)]
     if first:
-        q_ref = refs.pop(0)
+        q_refs = [refs.pop(0) for _ in range(2)]
     else:
         states_in = [[refs.pop(0) for _ in range(3)] for _ in halves]
     if last:
@@ -49,14 +47,12 @@
     zhi = lax.axis_index("zhi")
 
     lane = lax.broadcasted_iota(jnp.int32, (8, 128), 1)
-    where_from = []
     for n, half in enumerate(halves):
         zz = 1 - zhi if half == REMOTE else zhi
         seqs = []
         for slot in range(HALF_BLOCKS):
             yhi, flip = slot // 2, slot % 2
             cc = 1 - core if flip else core
-            where_from.append(yhi * 16 + zz * 2 + cc)
             seqs.append(order[2 * (zz * 8 + x * 2 + cc) + yhi])
         for slot in range(HALF_BLOCKS):
             rank = jnp.int32(4 * n)
@@ -71,10 +67,14 @@
     qpos[dummy_tile] = jnp.zeros((8, TILE), jnp.int32)
 
     if first:
-        for slot in range(HALF_BLOCKS * n_halves):
-            top = pl.multiple_of(q_rank[slot] * BLK, BLK)
-            for sub in range(4):
-                rows[pl.ds(top + sub * PIECE, PIECE), :] = q_ref[where_from[slot] + sub * 4]
+        for n, half in enumerate(halves):
+            zz = 1 - zhi if half == REMOTE else zhi
+            for slot in range(HALF_BLOCKS):
+                yhi, flip = slot // 2, slot % 2
+                top = pl.multiple_of(q_rank[4 * n + slot] * BLK, BLK)
+                for sub in range(4):
+                    piece = q_refs[flip][yhi * 8 + sub * 2 + zz]
+                    rows[pl.ds(top + sub * PIECE, PIECE), :] = piece
         for t in range(n_halves * TILES):
             qt[t] = rows[t * TILE : (t + 1) * TILE, :].T
             num[t] = jnp.zeros((HEAD, TILE), jnp.float32)
@@ -91,16 +91,14 @@
 
     count = jnp.int32(0)
     total = jnp.int32(0)
-    for n, (dx, flip, _) in enumerate(offsets):
+    for n, (dx, flip, yhi) in enumerate(offsets):
         xs = (x + (4 - dx)) % 4
         cs = 1 - core if flip else core
-        for b in range(4):
-            yhi, zz = b // 2, b % 2
-            kb = 4 * n + b
+        for zz in range(2):
+            kb = 2 * n + zz
             vals = []
             for sub in range(4):
-                source, at = kv[n][yhi]
-                piece = source[at + sub * 2 + zz]
+                piece = kv[n][sub * 2 + zz]
                 kbuf[kb, sub * PIECE : (sub + 1) * PIECE, :] = piece[:, :HEAD]
                 vals.append(piece[:, HEAD:])
             vt[kb] = jnp.concatenate(vals, axis=0).T
@@ -136,14 +134,14 @@
 
     def weigh(item, s, p):
         j, t = item
-        rel = qpos[t] - kb_seq[j] * BLK
+        rel = qpos[t] - (kb_seq[j] * BLK + row)
         acc = None
         for r in range(0, BLK, 16):
             both = []
             for h in range(2):
                 z = s[r + 8 * h : r + 8 * h + 8, :]
                 w = jnp.exp2(CAP_LOG2E * jnp.tanh(z * SCORE_SCALE))
-                w = jnp.where(row + (r + 8 * h) <= rel, w, 0.0)
+                w = jnp.where(rel >= r + 8 * h, w, 0.0)
                 acc = w if acc is None else acc + w
                 both.append(w)
             p[r : r + 16, :] = jnp.concatenate(both, axis=0).astype(jnp.bfloat16)
@@ -198,11 +196,11 @@
 
 
 def attend(order, given, halves, carry, first, last):
-    kvs = [piece for pieces, _, _ in given for piece in pieces]
-    offsets = tuple((dx, flip, len(pieces)) for pieces, dx, flip in given)
+    kvs = [piece for piece, _, _, _ in given]
+    offsets = tuple(at for _, *at in given)
     vmem = pl.BlockSpec(memory_space=pltpu.VMEM)
     smem = pl.BlockSpec(memory_space=pltpu.SMEM)
-    nb = 4 * len(given)
+    nb = 2 * len(given)
     tiles = TILES * len(halves)
     runs = nb * len(halves) + 2 * UNROLL + 4
     if last:
@@ -238,11 +236,49 @@
         ],
         compiler_params=pltpu.CompilerParams(vmem_limit_bytes=36 * 1024 * 1024),
         cost_estimate=pl.CostEstimate(
-            flops=len(given) * len(halves) * 1_200_000_000,
+            flops=len(given) * len(halves) * 600_000_000,
             transcendentals=0,
             bytes_accessed=4_000_000,
         ),
     )(*inputs)
+
+
+def local_call(body, outs, inputs):
+    vmem = pl.BlockSpec(memory_space=pltpu.VMEM)
+    return pl.pallas_call(
+        body,
+        out_shape=tuple(jax.ShapeDtypeStruct(shape, jnp.bfloat16) for shape in outs),
+        in_specs=[vmem] * len(inputs),
+        out_specs=(vmem,) * len(outs),
+        compiler_params=pltpu.CompilerParams(vmem_limit_bytes=8 * 1024 * 1024),
+    )(*inputs)
+
+
+def sort_kernel(query, key, value, out, sems):
+    copies = []
+    for head in range(16):
+        for source, left, width in ((query, 0, 2 * HEAD), (key, 2 * HEAD, HEAD), (value, 3 * HEAD, HEAD)):
+            copies.append(
+                pltpu.make_async_copy(
+                    source.at[:, head * width : (head + 1) * width],
+                    out.at[head, :, left : left + width],
+                    sems.at[len(copies)],
+                )
+            )
+    for copy in copies:
+        copy.start()
+    for copy in copies:
+        copy.wait()
+
+
+def split_kernel(got, low, high, keep, send):
+    core = lax.axis_index("core")
+    mine = pl.multiple_of(core * HEAD, HEAD)
+    other = pl.multiple_of((1 - core) * HEAD, HEAD)
+    for n in range(16):
+        (low, high)[n // 8][n % 8] = got[n, :, 2 * HEAD :]
+        keep[n] = got[n, :, pl.ds(mine, HEAD)]
+        send[n] = got[n, :, pl.ds(other, HEAD)]
 
 
 def assemble_kernel(own, swapped, z_same, z_cross, out):
@@ -258,58 +294,68 @@
         out[:, pl.ds(left, HEAD)] = piece[...]
 
 
-def along_x(value, by):
-    return lax.ppermute(value, "x", [(i, (i + by) % 4) for i in range(4)])
-
-
-def other_core(value):
-    return lax.ppermute(value, "core", [(0, 1), (1, 0)])
+def along(value, axis, by):
+    return lax.ppermute(value, axis, [(i, (i + by) % 4) for i in range(4)])
+
+
+def mirror(value, axes):
+    size = 2 if isinstance(axes, str) else 4
+    return lax.ppermute(value, axes, [(i, size - 1 - i) for i in range(size)])
 
 
 def layer(query, key, value, block_order):
     rows = query.shape[0]
-    kv = jnp.concatenate(
-        [key.reshape(rows, 16, HEAD), value.reshape(rows, 16, HEAD)], axis=2
-    ).transpose(1, 0, 2)
-    kv = lax.all_to_all(kv, ("y", "zlo", "zhi"), 0, 0)
-    q = query.reshape(rows, 32, HEAD).transpose(1, 0, 2)
-    q = lax.all_to_all(q, ("y", "zlo", "zhi", "core"), 0, 0)
-
-    up = along_x(kv, 1)
-    down = along_x(kv, -1)
-    own_o = other_core(kv)
-    far_a = along_x(up[:8], 1)
-    far_b = along_x(down[8:], -1)
-    up_o = other_core(up)
-    down_o = other_core(down)
-    far_a_o = other_core(far_a)
-    far_b_o = other_core(far_b)
-
-    near = [((up,), 1, 0), ((down,), 3, 0)]
-    near_o = [((up_o,), 1, 1), ((down_o,), 3, 1)]
-    far = [((far_a, far_b), 2, 0), ((far_a_o, far_b_o), 2, 1)]
+    packed = pl.pallas_call(
+        sort_kernel,
+        out_shape=jax.ShapeDtypeStruct((16, rows, 4 * HEAD), jnp.bfloat16),
+        in_specs=[pl.BlockSpec(memory_space=pltpu.HBM)] * 3,
+        out_specs=pl.BlockSpec(memory_space=pltpu.VMEM),
+        scratch_shapes=[pltpu.SemaphoreType.DMA((48,))],
+        compiler_params=pltpu.CompilerParams(vmem_limit_bytes=8 * 1024 * 1024),
+        name="k_sort",
+    )(query, key, value)
+    packed = lax.all_to_all(packed, ("y", "zlo", "zhi"), 0, 0)
+    low, high, keep, send = local_call(
+        split_kernel, [(8, rows, 2 * HEAD)] * 2 + [(16, rows, HEAD)] * 2, (packed,)
+    )
+    got = mirror(send, "core")
+    up_low = along(low, "x", 1)
+    down_high = along(high, "x", -1)
+    up_high = along(high, "x", 1)
+    down_low = along(low, "x", -1)
+    far_low = along(up_low, "x", 1)
+    far_high = along(down_high, "x", -1)
+
+    def swap(half):
+        return mirror(half, "core")
+
+    own = [(low, 0, 0, 0), (high, 0, 0, 1)]
+    own += [(swap(low), 0, 1, 0), (swap(high), 0, 1, 1)]
+    near_a = [(up_low, 1, 0, 0), (down_high, 3, 0, 1)]
+    near_b = [(up_high, 1, 0, 1), (down_low, 3, 0, 0)]
+    near_b += [(swap(up_low), 1, 1, 0), (swap(down_high), 3, 1, 1)]
+    near_c = [(swap(up_high), 1, 1, 1), (swap(down_low), 3, 1, 0)]
+    far = [(far_low, 2, 0, 0), (far_high, 2, 0, 1)]
+    far += [(swap(far_low), 2, 1, 0), (swap(far_high), 2, 1, 1)]
 
     def step(given, halves, carry, first=False, last=False):
         return attend(block_order, given, halves, carry, first, last)
 
-    state = step([((kv,), 0, 0)], (REMOTE, LOCAL), (q,), first=True)
-    state = step([((own_o,), 0, 1)], (REMOTE, LOCAL), state)
+    both = (REMOTE, LOCAL)
+    state = step(own, both, (keep, got), first=True)
+    state = step(near_a, both, state)
     remote, local = state[:3], state[3:]
-    remote = step(near, (REMOTE,), remote)
-    remote = step(near_o, (REMOTE,), remote)
+    remote = step(near_b, (REMOTE,), remote)
+    remote = step(near_c, (REMOTE,), remote)
     same, cross = step(far, (REMOTE,), remote, last=True)
-    z_same = lax.ppermute(same, "zhi", [(0, 1), (1, 0)])
-    z_cross = lax.ppermute(cross, ("zhi", "core"), [(i, 3 - i) for i in range(4)])
-    own, cross = step(near + near_o + far, (LOCAL,), local, last=True)
-    swapped = other_core(cross)
-    vmem = pl.BlockSpec(memory_space=pltpu.VMEM)
-    return pl.pallas_call(
-        assemble_kernel,
-        out_shape=jax.ShapeDtypeStruct((2 * BLK, 4 * HEAD), jnp.bfloat16),
-        in_specs=[vmem] * 4,
-        out_specs=vmem,
-        name="assemble",
-    )(own, swapped, z_same, z_cross)
+    z_same = mirror(same, "zhi")
+    z_cross = mirror(cross, ("zhi", "core"))
+    mine, cross = step(near_b + near_c + far, (LOCAL,), local, last=True)
+    swapped = mirror(cross, "core")
+    (out,) = local_call(
+        assemble_kernel, [(2 * BLK, 4 * HEAD)], (mine, swapped, z_same, z_cross)
+    )
+    return out
 
 
 def solution(mesh):

time: 110 us -> 114 us (1.036)
  blocking collectives: 21.1 us -> 29.4 us
  Pallas kernels: 55.1 us -> 51.1 us
  local copies, waits for them, and re-layouts: 6.23 us -> 3.13 us
  waiting for transfers between devices: 9.75 us -> 12.8 us
    all_to_all x1, blocking collectives: 21.1 us -> 29.4 us  [layer(): packed = lax.all_to_all(packed, ('y', 'zlo', 'zhi'), 0, 0)]
    all_to_all x1 -> x0, starting transfers between devices: 5.98 us -> none  [layer(): q = lax.all_to_all(q, ('y', 'zlo', 'zhi', 'core'), 0, 0)]
    ppermute x12 -> x18, starting transfers between devices: 11.5 us -> 17.1 us  [the longest x12 13 us: mirror(): return lax.ppermute(value, axes, [(i, size - 1 - i) for i in range(size)])]
    pallas_call x6, Pallas kernels: 52.8 us -> 49 us  [attend(): pl.pallas_call(functools.partial(attend_kernel, offsets=offsets, halves=h...]
    ppermute x12 -> x18, waiting for transfers between devices: 9.74 us -> 12.8 us  [the longest x6 11.7 us: along(): return lax.ppermute(value, axis, [(i, (i + by) % 4) for i in range(4)])]
    slice x2 -> x0, local copies, waits for them, and re-layouts: 2.54 us -> none  [the longest x1 1.77 us: layer(): far_b = along_x(down[8:], -1)]
    unnamed x12 -> x8, local copies, waits for them, and re-layouts: 1.35 us -> 3.13 us
    reshape x1 -> x0, local copies, waits for them, and re-layouts: 1.32 us -> none  [layer(): value.reshape(rows, 16, HEAD)]
  transfers between devices with their start and end apart: 13 -> 18, of which waited for: 2 -> 3; matrix products, arithmetic and copies ran while one was open for 3% -> 0% of each run, Pallas kernels for 42% -> 37%
where the time goes in v4:
time: 114 us
  Pallas kernels  51.1 us (45%)
  blocking collectives  29.4 us (26%)
  starting transfers between devices  17.1 us (15%)
  waiting for transfers between devices  12.8 us (11%)
  local copies, waits for them, and re-layouts  3.13 us (3%)
    pallas_call x6, Pallas kernels, attend(): pl.pallas_call(functools.partial(attend_kernel, offsets=offsets, halves=h...  49 us
    all_to_all x1, blocking collectives, layer(): packed = lax.all_to_all(packed, ('y', 'zlo', 'zhi'), 0, 0)  29.4 us
    ppermute x12, starting transfers between devices, mirror(): return lax.ppermute(value, axes, [(i, size - 1 - i) for i in range(size)])  13 us
    ppermute x6, waiting for transfers between devices, along(): return lax.ppermute(value, axis, [(i, (i + by) % 4) for i in range(4)])  11.7 us
    ppermute x6, starting transfers between devices, along(): return lax.ppermute(value, axis, [(i, (i + by) % 4) for i in range(4)])  4.11 us
    unnamed x8, local copies, waits for them, and re-layouts  3.13 us
  transfers between devices with their start and end apart: 18, of which 3 were waited for; matrix products, arithmetic and copies ran while one was open for 0% of the time, Pallas kernels for 37%

profile of v4, /device:TPU:5, one launch (start us, length us, event | category | flops | bytes accessed | tf_op | source)
XLA Modules:
  0.0 113.7 jit_solution(4458250446749450252)
XLA Ops:
  0.0 0.0 copy-start
  0.0 1.1 copy-done
  1.1 0.0 copy-start.1
  1.1 1.0 copy-done.1
  2.1 0.0 copy-start.2
  2.1 1.0 copy-done.2
  3.1 0.8 k_sort.1
  4.0 29.4 %all_to_all.5.got = bf16[16,96,512]{2,1,0:T(8,128)(2,1)S(1)} all-to-all(bf16[16,96,512]{2,1,0:T(8,128)(2,1)S(1)} %k_sort.1), channel_id=1, replica_groups=mesh['y'=4,'zlo'=2,'zhi'=2,'x'=4,'core'=2] {'y','zlo','zhi'}, dimensions={0} | all-to-all | bytes 3145728 | tf_op jit(solution)/shard_map/all_to_all | solution.py:317
  33.4 0.0 copy-start.3
  33.4 0.2 shard_map.46
  33.6 2.1 %collective-permute-start.12 = (bf16[8,96,256]{2,1,0:T(8,128)(2,1)S(1)}, bf16[8,96,256]{2,1,0:T(8,128)(2,1)S(1)}, u32[]{:S(2)}, u32[]{:S(2)}) collective-permute-start(bf16[8,96,256]{2,1,0:T(8,128)(2,1)S(1)} %get-tuple-element.32.refs_1_), channel_id=1, source_target_pairs={{0,1},{1,0},{2,3},{3,2},{4,5},{5,4},{6,7},{7,6},{8,9},{9,8},{10,11... | collective-permute-start | bytes 1179656 | tf_op jit(solution)/shard_map/ppermute | solution.py:303
  35.7 0.1 collective-permute-start.13
  35.8 0.9 collective-permute-start.2
  36.7 0.7 collective-permute-start.14
  37.4 0.5 collective-permute-start.4
  37.9 0.0 collective-permute-done.12.refs_3_
  37.9 0.9 collective-permute-start
  38.8 0.0 collective-permute-done.13.refs_4_
  38.8 0.5 collective-permute-start.1
  39.4 6.6 %collective-permute-done.2.refs_1_ = bf16[8,96,256]{2,1,0:T(8,128)(2,1)S(1)} collective-permute-done((bf16[8,96,256]{2,1,0:T(8,128)(2,1)S(1)}, bf16[8,96,256]{2,1,0:T(8,128)(2,1)S(1)}, u32[]{:S(2)}, u32[]{:S(2)}) %collective-permute-start.2) | collective-permute-done | bytes 393248 | tf_op jit(solution)/shard_map/ppermute | solution.py:298
  46.0 2.1 %collective-permute-start.3 = (bf16[8,96,256]{2,1,0:T(8,128)(2,1)S(1)}, bf16[8,96,256]{2,1,0:T(8,128)(2,1)S(1)}, u32[]{:S(2)}, u32[]{:S(2)}) collective-permute-start(bf16[8,96,256]{2,1,0:T(8,128)(2,1)S(1)} %collective-permute-done.2.refs_1_), channel_id=1, source_target_pairs={{0,1},{1,0},{2,3},{3,2},{4,5},{5,4},{6,7},{7,6},{8,9},{9,8},{10,11... | collective-permute-start | bytes 1179656 | tf_op jit(solution)/shard_map/ppermute | solution.py:303
  48.2 0.0 collective-permute-done.14.refs_6_
  48.2 0.9 collective-permute-start.8
  49.1 0.0 collective-permute-done.4.refs_2_
  49.1 0.3 collective-permute-start.5
  49.4 5.1 %collective-permute-done.refs_1_ = bf16[8,96,256]{2,1,0:T(8,128)(2,1)S(1)} collective-permute-done((bf16[8,96,256]{2,1,0:T(8,128)(2,1)S(1)}, bf16[8,96,256]{2,1,0:T(8,128)(2,1)S(1)}, u32[]{:S(2)}, u32[]{:S(2)}) %collective-permute-start) | collective-permute-done | bytes 393248 | tf_op jit(solution)/shard_map/ppermute | solution.py:298
  54.4 0.3 collective-permute-start.9
  54.7 0.0 copy-done.3
  54.7 10.5 %shard_map.47 = (bf16[6,128,256]{2,1,0:T(8,128)(2,1)S(1)}, f32[6,128,256]{2,1,0:T(8,128)S(1)}, f32[6,8,256]{2,1,0:T(8,128)S(1)}, bf16[6,128,256]{2,1,0:T(8,128)(...) custom-call(s32[32]{0:T(128)S(1)} %copy-done.3, bf16[8,96,256]{2,1,0:T(8,128)(2,1)S(1)} %get-tuple-element.32.refs_1_, ...), custom_call_target="tpu_custom_call" | custom-call | flops 4800000000 | bytes 4000000 | tf_op jit(solution)/shard_map/pallas_call | solution.py:215
  65.2 0.0 collective-permute-done.1.refs_2_
  65.2 2.5 %collective-permute-start.6 = (bf16[8,96,256]{2,1,0:T(8,128)(2,1)S(1)}, bf16[8,96,256]{2,1,0:T(8,128)(2,1)S(1)}, u32[]{:S(2)}, u32[]{:S(2)}) collective-permute-start(bf16[8,96,256]{2,1,0:T(8,128)(2,1)S(1)} %collective-permute-done.refs_1_), channel_id=1, source_target_pairs={{0,1},{1,0},{2,3},{3,2},{4,5},{5,4},{6,7},{7,6},{8,9},{9,8},{10,11... | collective-permute-start | bytes 1179656 | tf_op jit(solution)/shard_map/ppermute | solution.py:303
  67.7 0.0 collective-permute-done.3.refs_3_
  67.7 0.1 collective-permute-start.7
  67.8 0.0 collective-permute-done.8.refs_7_.refs_1_
  67.8 0.4 collective-permute-start.10
  68.2 0.0 collective-permute-done.9.refs_8_.refs_2_
  68.2 0.1 collective-permute-start.11
  68.3 7.6 %shard_map.48 = (bf16[6,128,256]{2,1,0:T(8,128)(2,1)S(1)}, f32[6,128,256]{2,1,0:T(8,128)S(1)}, f32[6,8,256]{2,1,0:T(8,128)S(1)}, bf16[6,128,256]{2,1,0:T(8,128)(...) custom-call(s32[32]{0:T(128)S(1)} %copy-done.3, bf16[8,96,256]{2,1,0:T(8,128)(2,1)S(1)} %collective-permute-done.2.refs_1_, ...), custom_call_target="tpu_custom_call" | custom-call | flops 2400000000 | bytes 4000000 | tf_op jit(solution)/shard_map/pallas_call | solution.py:215
  75.9 0.0 collective-permute-done.5.refs_4_
  75.9 5.9 %shard_map.50 = (bf16[6,128,256]{2,1,0:T(8,128)(2,1)S(1)}, f32[6,128,256]{2,1,0:T(8,128)S(1)}, f32[6,8,256]{2,1,0:T(8,128)S(1)}) custom-call(s32[32]{0:T(128)S(1)} %copy-done.3, bf16[8,96,256]{2,1,0:T(8,128)(2,1)S(1)} %collective-permute-done.refs_1_, bf16[8,96,256]{2,1,0:T(8,128)(2,1)S(1)} %collective-permute-done.1.refs_2_, ...), custom_call_target="tpu_custom_call" | custom-call | flops 2400000000 | bytes 4000000 | tf_op jit(solution)/shard_map/pallas_call | solution.py:215
  81.8 0.0 collective-permute-done.6.refs_5_.refs_1_
  81.8 0.0 collective-permute-done.7.refs_6_.refs_2_
  81.8 3.7 %shard_map.51 = (bf16[6,128,256]{2,1,0:T(8,128)(2,1)S(1)}, f32[6,128,256]{2,1,0:T(8,128)S(1)}, f32[6,8,256]{2,1,0:T(8,128)S(1)}) custom-call(s32[32]{0:T(128)S(1)} %copy-done.3, bf16[8,96,256]{2,1,0:T(8,128)(2,1)S(1)} %collective-permute-done.6.refs_5_.refs_1_, bf16[8,96,256]{2,1,0:T(8,128)(2,1)S(1)} %collective-permute-done.7.refs_6_.refs_2_, ...), custom_call_target="tpu_custom_call" | custom-call | flops 1200000000 | bytes 4000000 | tf_op jit(solution)/shard_map/pallas_call | solution.py:215
  85.5 0.0 collective-permute-done.10.refs_9_.refs_3_
  85.5 0.0 collective-permute-done.11.refs_10_.refs_4_
  85.6 6.6 %shard_map.52 = (bf16[768,128]{1,0:T(8,128)(2,1)S(1)}, bf16[768,128]{1,0:T(8,128)(2,1)S(1)}) custom-call(s32[32]{0:T(128)S(1)} %copy-done.3, bf16[8,96,256]{2,1,0:T(8,128)(2,1)S(1)} %collective-permute-done.8.refs_7_.refs_1_, bf16[8,96,256]{2,1,0:T(8,128)(2,1)S(1)} %collective-permute-done.9.refs_8_.refs_2_, ...), custom_call_target="tpu_custom_call" | custom-call | flops 2400000000 | bytes 4000000 | tf_op jit(solution)/shard_map/pallas_call | solution.py:215
  92.1 2.1 %collective-permute-start.16 = (bf16[768,128]{1,0:T(8,128)(2,1)S(1)}, bf16[768,128]{1,0:T(8,128)(2,1)S(1)}, u32[]{:S(2)}, u32[]{:S(2)}) collective-permute-start(bf16[768,128]{1,0:T(8,128)(2,1)S(1)} %get-tuple-element.55), channel_id=1, source_target_pairs={{0,8},{8,0},{1,9},{9,1},{2,10},{10,2},{3,11},{11,3},{4,12},{12,4},... | collective-permute-start | bytes 589832 | tf_op jit(solution)/shard_map/ppermute | solution.py:303
  94.2 0.4 collective-permute-start.17
  94.6 14.8 %shard_map.49 = (bf16[768,128]{1,0:T(8,128)(2,1)S(1)}, bf16[768,128]{1,0:T(8,128)(2,1)S(1)}) custom-call(s32[32]{0:T(128)S(1)} %copy-done.3, bf16[8,96,256]{2,1,0:T(8,128)(2,1)S(1)} %collective-permute-done.refs_1_, bf16[8,96,256]{2,1,0:T(8,128)(2,1)S(1)} %collective-permute-done.1.refs_2_, bf16[8,96,256]{2,1,0:T(8,128)(2,1)S(1)} %collective-permute-done.3.refs_3_, ...), custom_call_target="tpu_custom_call" | custom-call | flops 6000000000 | bytes 4000000 | tf_op jit(solution)/shard_map/pallas_call | solution.py:215
  109.5 2.1 %collective-permute-start.15 = (bf16[768,128]{1,0:T(8,128)(2,1)S(1)}, bf16[768,128]{1,0:T(8,128)(2,1)S(1)}, u32[]{:S(2)}, u32[]{:S(2)}) collective-permute-start(bf16[768,128]{1,0:T(8,128)(2,1)S(1)} %get-tuple-element.45), channel_id=1, source_target_pairs={{0,1},{1,0},{2,3},{3,2},{4,5},{5,4},{6,7},{7,6},{8,9},{9,8},{10,11... | collective-permute-start | bytes 589832 | tf_op jit(solution)/shard_map/ppermute | solution.py:303
  111.6 0.0 collective-permute-done.16.z_same
  111.6 0.0 collective-permute-done.17.z_cross
  111.6 1.1 collective-permute-done.15.swapped
  112.6 1.1 shard_map.53
Async XLA Ops:
  0.0 1.1 copy-start
  1.1 1.0 copy-start.1
  2.1 1.0 copy-start.2
  33.4 21.3 %copy-start.3 = (s32[32]{0:T(128)S(1)}, s32[32]{0:T(128)}, u32[]{:S(2)}) copy-start(s32[32]{0:T(128)} %refs_0_.11) | copy-start | bytes 388
  33.6 4.3 %collective-permute-start.12 = (bf16[8,96,256]{2,1,0:T(8,128)(2,1)S(1)}, bf16[8,96,256]{2,1,0:T(8,128)(2,1)S(1)}, u32[]{:S(2)}, u32[]{:S(2)}) collective-permute-start(bf16[8,96,256]{2,1,0:T(8,128)(2,1)S(1)} %get-tuple-element.32.refs_1_), channel_id=1, source_target_pairs={{0,1},{1,0},{2,3},{3,2},{4,5},{5,4},{6,7},{7,6},{8,9},{9,8},{10,11... | collective-permute-start | bytes 1179656 | tf_op jit(solution)/shard_map/ppermute | solution.py:303
  35.7 3.2 %collective-permute-start.13 = (bf16[8,96,256]{2,1,0:T(8,128)(2,1)S(1)}, bf16[8,96,256]{2,1,0:T(8,128)(2,1)S(1)}, u32[]{:S(2)}, u32[]{:S(2)}) collective-permute-start(bf16[8,96,256]{2,1,0:T(8,128)(2,1)S(1)} %get-tuple-element.31.refs_2_), channel_id=1, source_target_pairs={{0,1},{1,0},{2,3},{3,2},{4,5},{5,4},{6,7},{7,6},{8,9},{9,8},{10,11... | collective-permute-start | bytes 1179656 | tf_op jit(solution)/shard_map/ppermute | solution.py:303
  35.8 10.3 %collective-permute-start.2 = (bf16[8,96,256]{2,1,0:T(8,128)(2,1)S(1)}, bf16[8,96,256]{2,1,0:T(8,128)(2,1)S(1)}, u32[]{:S(2)}, u32[]{:S(2)}) collective-permute-start(bf16[8,96,256]{2,1,0:T(8,128)(2,1)S(1)} %get-tuple-element.32.refs_1_), channel_id=1, source_target_pairs={{0,2},{2,4},{4,6},{6,0},{1,3},{3,5},{5,7},{7,1},{8,10},{10,12},{12... | collective-permute-start | bytes 1179656 | tf_op jit(solution)/shard_map/ppermute | solution.py:298
  36.7 11.5 %collective-permute-start.14 = (bf16[16,96,128]{2,1,0:T(8,128)(2,1)S(1)}, bf16[16,96,128]{2,1,0:T(8,128)(2,1)S(1)}, u32[]{:S(2)}, u32[]{:S(2)}) collective-permute-start(bf16[16,96,128]{2,1,0:T(8,128)(2,1)S(1)} %get-tuple-element.34), channel_id=1, source_target_pairs={{0,1},{1,0},{2,3},{3,2},{4,5},{5,4},{6,7},{7,6},{8,9},{9,8},{10,11... | collective-permute-start | bytes 1179656 | tf_op jit(solution)/shard_map/ppermute | solution.py:303
  37.4 11.7 %collective-permute-start.4 = (bf16[8,96,256]{2,1,0:T(8,128)(2,1)S(1)}, bf16[8,96,256]{2,1,0:T(8,128)(2,1)S(1)}, u32[]{:S(2)}, u32[]{:S(2)}) collective-permute-start(bf16[8,96,256]{2,1,0:T(8,128)(2,1)S(1)} %get-tuple-element.31.refs_2_), channel_id=1, source_target_pairs={{0,6},{2,0},{4,2},{6,4},{1,7},{3,1},{5,3},{7,5},{8,14},{10,8},{12,... | collective-permute-start | bytes 1179656 | tf_op jit(solution)/shard_map/ppermute | solution.py:298
  37.9 16.5 %collective-permute-start = (bf16[8,96,256]{2,1,0:T(8,128)(2,1)S(1)}, bf16[8,96,256]{2,1,0:T(8,128)(2,1)S(1)}, u32[]{:S(2)}, u32[]{:S(2)}) collective-permute-start(bf16[8,96,256]{2,1,0:T(8,128)(2,1)S(1)} %get-tuple-element.31.refs_2_), channel_id=1, source_target_pairs={{0,2},{2,4},{4,6},{6,0},{1,3},{3,5},{5,7},{7,1},{8,10},{10,12},{12... | collective-permute-start | bytes 1179656 | tf_op jit(solution)/shard_map/ppermute | solution.py:298
  38.8 26.3 %collective-permute-start.1 = (bf16[8,96,256]{2,1,0:T(8,128)(2,1)S(1)}, bf16[8,96,256]{2,1,0:T(8,128)(2,1)S(1)}, u32[]{:S(2)}, u32[]{:S(2)}) collective-permute-start(bf16[8,96,256]{2,1,0:T(8,128)(2,1)S(1)} %get-tuple-element.32.refs_1_), channel_id=1, source_target_pairs={{0,6},{2,0},{4,2},{6,4},{1,7},{3,1},{5,3},{7,5},{8,14},{10,8},{12,... | collective-permute-start | bytes 1179656 | tf_op jit(solution)/shard_map/ppermute | solution.py:298
  46.0 21.6 %collective-permute-start.3 = (bf16[8,96,256]{2,1,0:T(8,128)(2,1)S(1)}, bf16[8,96,256]{2,1,0:T(8,128)(2,1)S(1)}, u32[]{:S(2)}, u32[]{:S(2)}) collective-permute-start(bf16[8,96,256]{2,1,0:T(8,128)(2,1)S(1)} %collective-permute-done.2.refs_1_), channel_id=1, source_target_pairs={{0,1},{1,0},{2,3},{3,2},{4,5},{5,4},{6,7},{7,6},{8,9},{9,8},{10,11... | collective-permute-start | bytes 1179656 | tf_op jit(solution)/shard_map/ppermute | solution.py:303
  48.2 19.6 %collective-permute-start.8 = (bf16[8,96,256]{2,1,0:T(8,128)(2,1)S(1)}, bf16[8,96,256]{2,1,0:T(8,128)(2,1)S(1)}, u32[]{:S(2)}, u32[]{:S(2)}) collective-permute-start(bf16[8,96,256]{2,1,0:T(8,128)(2,1)S(1)} %collective-permute-done.2.refs_1_), channel_id=1, source_target_pairs={{0,2},{2,4},{4,6},{6,0},{1,3},{3,5},{5,7},{7,1},{8,10},{10,12},{12... | collective-permute-start | bytes 1179656 | tf_op jit(solution)/shard_map/ppermute | solution.py:298
  49.1 26.8 %collective-permute-start.5 = (bf16[8,96,256]{2,1,0:T(8,128)(2,1)S(1)}, bf16[8,96,256]{2,1,0:T(8,128)(2,1)S(1)}, u32[]{:S(2)}, u32[]{:S(2)}) collective-permute-start(bf16[8,96,256]{2,1,0:T(8,128)(2,1)S(1)} %collective-permute-done.4.refs_2_), channel_id=1, source_target_pairs={{0,1},{1,0},{2,3},{3,2},{4,5},{5,4},{6,7},{7,6},{8,9},{9,8},{10,11... | collective-permute-start | bytes 1179656 | tf_op jit(solution)/shard_map/ppermute | solution.py:303
  54.4 13.7 %collective-permute-start.9 = (bf16[8,96,256]{2,1,0:T(8,128)(2,1)S(1)}, bf16[8,96,256]{2,1,0:T(8,128)(2,1)S(1)}, u32[]{:S(2)}, u32[]{:S(2)}) collective-permute-start(bf16[8,96,256]{2,1,0:T(8,128)(2,1)S(1)} %collective-permute-done.4.refs_2_), channel_id=1, source_target_pairs={{0,6},{2,0},{4,2},{6,4},{1,7},{3,1},{5,3},{7,5},{8,14},{10,8},{12,... | collective-permute-start | bytes 1179656 | tf_op jit(solution)/shard_map/ppermute | solution.py:298
  65.2 16.6 %collective-permute-start.6 = (bf16[8,96,256]{2,1,0:T(8,128)(2,1)S(1)}, bf16[8,96,256]{2,1,0:T(8,128)(2,1)S(1)}, u32[]{:S(2)}, u32[]{:S(2)}) collective-permute-start(bf16[8,96,256]{2,1,0:T(8,128)(2,1)S(1)} %collective-permute-done.refs_1_), channel_id=1, source_target_pairs={{0,1},{1,0},{2,3},{3,2},{4,5},{5,4},{6,7},{7,6},{8,9},{9,8},{10,11... | collective-permute-start | bytes 1179656 | tf_op jit(solution)/shard_map/ppermute | solution.py:303
  67.7 14.1 %collective-permute-start.7 = (bf16[8,96,256]{2,1,0:T(8,128)(2,1)S(1)}, bf16[8,96,256]{2,1,0:T(8,128)(2,1)S(1)}, u32[]{:S(2)}, u32[]{:S(2)}) collective-permute-start(bf16[8,96,256]{2,1,0:T(8,128)(2,1)S(1)} %collective-permute-done.1.refs_2_), channel_id=1, source_target_pairs={{0,1},{1,0},{2,3},{3,2},{4,5},{5,4},{6,7},{7,6},{8,9},{9,8},{10,11... | collective-permute-start | bytes 1179656 | tf_op jit(solution)/shard_map/ppermute | solution.py:303
  67.8 17.8 %collective-permute-start.10 = (bf16[8,96,256]{2,1,0:T(8,128)(2,1)S(1)}, bf16[8,96,256]{2,1,0:T(8,128)(2,1)S(1)}, u32[]{:S(2)}, u32[]{:S(2)}) collective-permute-start(bf16[8,96,256]{2,1,0:T(8,128)(2,1)S(1)} %collective-permute-done.8.refs_7_.refs_1_), channel_id=1, source_target_pairs={{0,1},{1,0},{2,3},{3,2},{4,5},{5,4},{6,7},{7,6},{8,9},{9,8},{10,11... | collective-permute-start | bytes 1179656 | tf_op jit(solution)/shard_map/ppermute | solution.py:303
  68.2 17.4 %collective-permute-start.11 = (bf16[8,96,256]{2,1,0:T(8,128)(2,1)S(1)}, bf16[8,96,256]{2,1,0:T(8,128)(2,1)S(1)}, u32[]{:S(2)}, u32[]{:S(2)}) collective-permute-start(bf16[8,96,256]{2,1,0:T(8,128)(2,1)S(1)} %collective-permute-done.9.refs_8_.refs_2_), channel_id=1, source_target_pairs={{0,1},{1,0},{2,3},{3,2},{4,5},{5,4},{6,7},{7,6},{8,9},{9,8},{10,11... | collective-permute-start | bytes 1179656 | tf_op jit(solution)/shard_map/ppermute | solution.py:303
  92.1 19.5 %collective-permute-start.16 = (bf16[768,128]{1,0:T(8,128)(2,1)S(1)}, bf16[768,128]{1,0:T(8,128)(2,1)S(1)}, u32[]{:S(2)}, u32[]{:S(2)}) collective-permute-start(bf16[768,128]{1,0:T(8,128)(2,1)S(1)} %get-tuple-element.55), channel_id=1, source_target_pairs={{0,8},{8,0},{1,9},{9,1},{2,10},{10,2},{3,11},{11,3},{4,12},{12,4},... | collective-permute-start | bytes 589832 | tf_op jit(solution)/shard_map/ppermute | solution.py:303
  94.2 17.3 %collective-permute-start.17 = (bf16[768,128]{1,0:T(8,128)(2,1)S(1)}, bf16[768,128]{1,0:T(8,128)(2,1)S(1)}, u32[]{:S(2)}, u32[]{:S(2)}) collective-permute-start(bf16[768,128]{1,0:T(8,128)(2,1)S(1)} %get-tuple-element.56), channel_id=1, source_target_pairs={{0,9},{1,8},{8,1},{9,0},{2,11},{3,10},{10,3},{11,2},{4,13},{5,12},... | collective-permute-start | bytes 589832 | tf_op jit(solution)/shard_map/ppermute | solution.py:303
  109.5 3.2 %collective-permute-start.15 = (bf16[768,128]{1,0:T(8,128)(2,1)S(1)}, bf16[768,128]{1,0:T(8,128)(2,1)S(1)}, u32[]{:S(2)}, u32[]{:S(2)}) collective-permute-start(bf16[768,128]{1,0:T(8,128)(2,1)S(1)} %get-tuple-element.45), channel_id=1, source_target_pairs={{0,1},{1,0},{2,3},{3,2},{4,5},{5,4},{6,7},{7,6},{8,9},{9,8},{10,11... | collective-permute-start | bytes 589832 | tf_op jit(solution)/shard_map/ppermute | solution.py:303

commit v5 on v4

--- a/solution.py
+++ b/solution.py
@@ -234,7 +234,7 @@
             pltpu.SMEM((runs,), jnp.int32),
             pltpu.SMEM((runs,), jnp.int32),
         ],
-        compiler_params=pltpu.CompilerParams(vmem_limit_bytes=36 * 1024 * 1024),
+        compiler_params=pltpu.CompilerParams(vmem_limit_bytes=28 * 1024 * 1024),
         cost_estimate=pl.CostEstimate(
             flops=len(given) * len(halves) * 600_000_000,
             transcendentals=0,
@@ -309,9 +309,9 @@
         sort_kernel,
         out_shape=jax.ShapeDtypeStruct((16, rows, 4 * HEAD), jnp.bfloat16),
         in_specs=[pl.BlockSpec(memory_space=pltpu.HBM)] * 3,
-        out_specs=pl.BlockSpec(memory_space=pltpu.VMEM),
+        out_specs=pl.BlockSpec(memory_space=pltpu.HBM),
         scratch_shapes=[pltpu.SemaphoreType.DMA((48,))],
-        compiler_params=pltpu.CompilerParams(vmem_limit_bytes=8 * 1024 * 1024),
+        compiler_params=pltpu.CompilerParams(vmem_limit_bytes=62 * 1024 * 1024),
         name="k_sort",
     )(query, key, value)
     packed = lax.all_to_all(packed, ("y", "zlo", "zhi"), 0, 0)
@@ -331,10 +331,9 @@
 
     own = [(low, 0, 0, 0), (high, 0, 0, 1)]
     own += [(swap(low), 0, 1, 0), (swap(high), 0, 1, 1)]
-    near_a = [(up_low, 1, 0, 0), (down_high, 3, 0, 1)]
-    near_b = [(up_high, 1, 0, 1), (down_low, 3, 0, 0)]
-    near_b += [(swap(up_low), 1, 1, 0), (swap(down_high), 3, 1, 1)]
-    near_c = [(swap(up_high), 1, 1, 1), (swap(down_low), 3, 1, 0)]
+    near = [(up_low, 1, 0, 0), (down_high, 3, 0, 1), (up_high, 1, 0, 1), (down_low, 3, 0, 0)]
+    near_o = [(swap(up_low), 1, 1, 0), (swap(down_high), 3, 1, 1)]
+    near_o += [(swap(up_high), 1, 1, 1), (swap(down_low), 3, 1, 0)]
     far = [(far_low, 2, 0, 0), (far_high, 2, 0, 1)]
     far += [(swap(far_low), 2, 1, 0), (swap(far_high), 2, 1, 1)]
 
@@ -343,18 +342,14 @@
 
     both = (REMOTE, LOCAL)
     state = step(own, both, (keep, got), first=True)
-    state = step(near_a, both, state)
+    state = step(near, both, state)
     remote, local = state[:3], state[3:]
-    remote = step(near_b, (REMOTE,), remote)
-    remote = step(near_c, (REMOTE,), remote)
-    same, cross = step(far, (REMOTE,), remote, last=True)
+    same, cross = step(near_o + far, (REMOTE,), remote, last=True)
     z_same = mirror(same, "zhi")
     z_cross = mirror(cross, ("zhi", "core"))
-    mine, cross = step(near_b + near_c + far, (LOCAL,), local, last=True)
+    mine, cross = step(near_o + far, (LOCAL,), local, last=True)
     swapped = mirror(cross, "core")
-    (out,) = local_call(
-        assemble_kernel, [(2 * BLK, 4 * HEAD)], (mine, swapped, z_same, z_cross)
-    )
+    (out,) = local_call(assemble_kernel, [(2 * BLK, 4 * HEAD)], (mine, swapped, z_same, z_cross))
     return out
 
 

time: 114 us -> 154 us (1.35)
  Pallas kernels: 51.1 us -> 97.1 us
  local copies, waits for them, and re-layouts: 3.13 us -> 0.01 us
  waiting for transfers between devices: 12.8 us -> 10.3 us
    pallas_call x1, Pallas kernels: 0.85 us -> 49.2 us  [layer(): pl.pallas_call(sort_kernel, out_shape=jax.ShapeDtypeStruct((16, rows, 4 *...]
    unnamed x8 -> x2, local copies, waits for them, and re-layouts: 3.13 us -> 0.01 us
    ppermute x6, waiting for transfers between devices: 11.7 us -> 9.22 us  [along(): return lax.ppermute(value, axis, [(i, (i + by) % 4) for i in range(4)])]
    pallas_call x6 -> x4, Pallas kernels: 49 us -> 46.7 us  [attend(): pl.pallas_call(functools.partial(attend_kernel, offsets=offsets, halves=h...]
  transfers between devices with their start and end apart: 18 -> 18, of which waited for: 3 -> 4; matrix products, arithmetic and copies ran while one was open for 0% -> 0% of each run, Pallas kernels for 37% -> 23%
where the time goes in v5:
time: 154 us
  Pallas kernels  97.1 us (63%)
  blocking collectives  29.6 us (19%)
  starting transfers between devices  17 us (11%)
  waiting for transfers between devices  10.3 us (7%)
    pallas_call x1, Pallas kernels, layer(): pl.pallas_call(sort_kernel, out_shape=jax.ShapeDtypeStruct((16, rows, 4 *...  49.2 us
    pallas_call x4, Pallas kernels, attend(): pl.pallas_call(functools.partial(attend_kernel, offsets=offsets, halves=h...  46.7 us
    all_to_all x1, blocking collectives, layer(): packed = lax.all_to_all(packed, ('y', 'zlo', 'zhi'), 0, 0)  29.6 us
    ppermute x12, starting transfers between devices, mirror(): return lax.ppermute(value, axes, [(i, size - 1 - i) for i in range(size)])  12.6 us
    ppermute x6, waiting for transfers between devices, along(): return lax.ppermute(value, axis, [(i, (i + by) % 4) for i in range(4)])  9.22 us
    ppermute x6, starting transfers between devices, along(): return lax.ppermute(value, axis, [(i, (i + by) % 4) for i in range(4)])  4.4 us
  transfers between devices with their start and end apart: 18, of which 4 were waited for; matrix products, arithmetic and copies ran while one was open for 0% of the time, Pallas kernels for 23%

profile of v5, /device:TPU:5, one launch (start us, length us, event | category | flops | bytes accessed | tf_op | source)
XLA Modules:
  0.0 154.2 jit_solution(13538008153492787430)
XLA Ops:
  0.0 49.2 %k_sort.1 = bf16[16,96,512]{2,1,0:T(8,128)(2,1)} custom-call(bf16[96,4096]{1,0:T(8,128)(2,1)} %query.1, bf16[96,2048]{1,0:T(8,128)(2,1)} %key.1, bf16[96,2048]{1,0:T(8,128)(2,1)} %value.1), custom_call_target="tpu_custom_call" | custom-call | tf_op jit(solution)/shard_map/k_sort/pallas_call | solution.py:308
  49.2 29.6 %all_to_all.5.got = bf16[16,96,512]{2,1,0:T(8,128)(2,1)S(1)} all-to-all(bf16[16,96,512]{2,1,0:T(8,128)(2,1)} %k_sort.1), channel_id=1, replica_groups=mesh['y'=4,'zlo'=2,'zhi'=2,'x'=4,'core'=2] {'y','zlo','zhi'}, dimensions={0} | all-to-all | bytes 3145728 | tf_op jit(solution)/shard_map/all_to_all | solution.py:317
  78.8 0.0 copy-start
  78.8 0.2 shard_map.46
  79.0 2.1 %collective-permute-start.12 = (bf16[8,96,256]{2,1,0:T(8,128)(2,1)S(1)}, bf16[8,96,256]{2,1,0:T(8,128)(2,1)S(1)}, u32[]{:S(2)}, u32[]{:S(2)}) collective-permute-start(bf16[8,96,256]{2,1,0:T(8,128)(2,1)S(1)} %get-tuple-element.25.refs_1_), channel_id=1, source_target_pairs={{0,1},{1,0},{2,3},{3,2},{4,5},{5,4},{6,7},{7,6},{8,9},{9,8},{10,11... | collective-permute-start | bytes 1179656 | tf_op jit(solution)/shard_map/ppermute | solution.py:303
  81.1 0.1 collective-permute-start.13
  81.2 0.9 collective-permute-start
  82.1 0.7 collective-permute-start.14
  82.8 0.5 collective-permute-start.2
  83.3 0.0 collective-permute-done.12.refs_3_
  83.3 0.9 collective-permute-start.4
  84.3 0.0 collective-permute-done.13.refs_4_
  84.3 0.5 collective-permute-start.6
  84.8 6.6 %collective-permute-done.refs_1_ = bf16[8,96,256]{2,1,0:T(8,128)(2,1)S(1)} collective-permute-done((bf16[8,96,256]{2,1,0:T(8,128)(2,1)S(1)}, bf16[8,96,256]{2,1,0:T(8,128)(2,1)S(1)}, u32[]{:S(2)}, u32[]{:S(2)}) %collective-permute-start) | collective-permute-done | bytes 393248 | tf_op jit(solution)/shard_map/ppermute | solution.py:298
  91.4 0.9 collective-permute-start.8
  92.4 0.0 collective-permute-done.14.refs_6_
  92.4 2.4 %collective-permute-start.1 = (bf16[8,96,256]{2,1,0:T(8,128)(2,1)S(1)}, bf16[8,96,256]{2,1,0:T(8,128)(2,1)S(1)}, u32[]{:S(2)}, u32[]{:S(2)}) collective-permute-start(bf16[8,96,256]{2,1,0:T(8,128)(2,1)S(1)} %collective-permute-done.refs_1_), channel_id=1, source_target_pairs={{0,1},{1,0},{2,3},{3,2},{4,5},{5,4},{6,7},{7,6},{8,9},{9,8},{10,11... | collective-permute-start | bytes 1179656 | tf_op jit(solution)/shard_map/ppermute | solution.py:303
  94.8 0.0 collective-permute-done.2.refs_2_
  94.8 0.5 collective-permute-start.9
  95.3 0.0 copy-done
  95.3 10.5 %shard_map.47 = (bf16[6,128,256]{2,1,0:T(8,128)(2,1)S(1)}, f32[6,128,256]{2,1,0:T(8,128)S(1)}, f32[6,8,256]{2,1,0:T(8,128)S(1)}, bf16[6,128,256]{2,1,0:T(8,128)(...) custom-call(s32[32]{0:T(128)S(1)} %copy-done, bf16[8,96,256]{2,1,0:T(8,128)(2,1)S(1)} %get-tuple-element.25.refs_1_, ...), custom_call_target="tpu_custom_call" | custom-call | flops 4800000000 | bytes 4000000 | tf_op jit(solution)/shard_map/pallas_call | solution.py:215
  105.8 0.0 collective-permute-done.4.refs_3_
  105.9 0.4 collective-permute-start.3
  106.3 0.0 collective-permute-done.6.refs_4_
  106.3 0.2 collective-permute-start.5
  106.4 1.8 %collective-permute-done.8.refs_5_ = bf16[8,96,256]{2,1,0:T(8,128)(2,1)S(1)} collective-permute-done((bf16[8,96,256]{2,1,0:T(8,128)(2,1)S(1)}, bf16[8,96,256]{2,1,0:T(8,128)(2,1)S(1)}, u32[]{:S(2)}, u32[]{:S(2)}) %collective-permute-start.8) | collective-permute-done | bytes 393248 | tf_op jit(solution)/shard_map/ppermute | solution.py:298
  108.3 1.3 collective-permute-start.7
  109.6 0.8 collective-permute-done.9.refs_6_
  110.3 0.9 collective-permute-start.10
  111.2 0.0 collective-permute-done.1.refs_1_
  111.2 0.0 collective-permute-start.11
  111.2 13.4 %shard_map.48 = (bf16[6,128,256]{2,1,0:T(8,128)(2,1)S(1)}, f32[6,128,256]{2,1,0:T(8,128)S(1)}, f32[6,8,256]{2,1,0:T(8,128)S(1)}, bf16[6,128,256]{2,1,0:T(8,128)(...) custom-call(s32[32]{0:T(128)S(1)} %copy-done, bf16[8,96,256]{2,1,0:T(8,128)(2,1)S(1)} %collective-permute-done.refs_1_, ...), custom_call_target="tpu_custom_call" | custom-call | flops 4800000000 | bytes 4000000 | tf_op jit(solution)/shard_map/pallas_call | solution.py:215
  124.6 0.0 collective-permute-done.3.refs_2_
  124.6 0.0 collective-permute-done.5.refs_3_
  124.6 0.0 collective-permute-done.7.refs_4_
  124.7 0.0 collective-permute-done.10.refs_7_
  124.7 0.0 collective-permute-done.11.refs_8_
  124.7 10.8 %shard_map.50 = (bf16[768,128]{1,0:T(8,128)(2,1)S(1)}, bf16[768,128]{1,0:T(8,128)(2,1)S(1)}) custom-call(s32[32]{0:T(128)S(1)} %copy-done, bf16[8,96,256]{2,1,0:T(8,128)(2,1)S(1)} %collective-permute-done.1.refs_1_, bf16[8,96,256]{2,1,0:T(8,128)(2,1)S(1)} %collective-permute-done.3.refs_2_, bf16[8,96,256]{2,1,0:T(8,128)(2,1)S(1)} %collective-permute-done.5.refs_3_, ...), custom_call_target="tpu_custom_call" | custom-call | flops 4800000000 | bytes 4000000 | tf_op jit(solution)/shard_map/pallas_call | solution.py:215
  135.5 1.6 %collective-permute-start.16 = (bf16[768,128]{1,0:T(8,128)(2,1)S(1)}, bf16[768,128]{1,0:T(8,128)(2,1)S(1)}, u32[]{:S(2)}, u32[]{:S(2)}) collective-permute-start(bf16[768,128]{1,0:T(8,128)(2,1)S(1)} %get-tuple-element.43), channel_id=1, source_target_pairs={{0,8},{8,0},{1,9},{9,1},{2,10},{10,2},{3,11},{11,3},{4,12},{12,4},... | collective-permute-start | bytes 589832 | tf_op jit(solution)/shard_map/ppermute | solution.py:303
  137.1 0.5 collective-permute-start.17
  137.6 11.9 %shard_map.49 = (bf16[768,128]{1,0:T(8,128)(2,1)S(1)}, bf16[768,128]{1,0:T(8,128)(2,1)S(1)}) custom-call(s32[32]{0:T(128)S(1)} %copy-done, bf16[8,96,256]{2,1,0:T(8,128)(2,1)S(1)} %collective-permute-done.1.refs_1_, bf16[8,96,256]{2,1,0:T(8,128)(2,1)S(1)} %collective-permute-done.3.refs_2_, bf16[8,96,256]{2,1,0:T(8,128)(2,1)S(1)} %collective-permute-done.5.refs_3_, ...), custom_call_target="tpu_custom_call" | custom-call | flops 4800000000 | bytes 4000000 | tf_op jit(solution)/shard_map/pallas_call | solution.py:215
  149.6 2.5 %collective-permute-start.15 = (bf16[768,128]{1,0:T(8,128)(2,1)S(1)}, bf16[768,128]{1,0:T(8,128)(2,1)S(1)}, u32[]{:S(2)}, u32[]{:S(2)}) collective-permute-start(bf16[768,128]{1,0:T(8,128)(2,1)S(1)} %get-tuple-element.39), channel_id=1, source_target_pairs={{0,1},{1,0},{2,3},{3,2},{4,5},{5,4},{6,7},{7,6},{8,9},{9,8},{10,11... | collective-permute-start | bytes 589832 | tf_op jit(solution)/shard_map/ppermute | solution.py:303
  152.0 0.0 collective-permute-done.16.z_same
  152.0 0.0 collective-permute-done.17.z_cross
  152.1 1.1 collective-permute-done.15.swapped
  153.1 1.1 shard_map.51
Async XLA Ops:
  78.8 16.5 %copy-start = (s32[32]{0:T(128)S(1)}, s32[32]{0:T(128)}, u32[]{:S(2)}) copy-start(s32[32]{0:T(128)} %refs_0_.7) | copy-start | bytes 388
  79.0 4.3 %collective-permute-start.12 = (bf16[8,96,256]{2,1,0:T(8,128)(2,1)S(1)}, bf16[8,96,256]{2,1,0:T(8,128)(2,1)S(1)}, u32[]{:S(2)}, u32[]{:S(2)}) collective-permute-start(bf16[8,96,256]{2,1,0:T(8,128)(2,1)S(1)} %get-tuple-element.25.refs_1_), channel_id=1, source_target_pairs={{0,1},{1,0},{2,3},{3,2},{4,5},{5,4},{6,7},{7,6},{8,9},{9,8},{10,11... | collective-permute-start | bytes 1179656 | tf_op jit(solution)/shard_map/ppermute | solution.py:303
  81.1 3.2 %collective-permute-start.13 = (bf16[8,96,256]{2,1,0:T(8,128)(2,1)S(1)}, bf16[8,96,256]{2,1,0:T(8,128)(2,1)S(1)}, u32[]{:S(2)}, u32[]{:S(2)}) collective-permute-start(bf16[8,96,256]{2,1,0:T(8,128)(2,1)S(1)} %get-tuple-element.26.refs_2_), channel_id=1, source_target_pairs={{0,1},{1,0},{2,3},{3,2},{4,5},{5,4},{6,7},{7,6},{8,9},{9,8},{10,11... | collective-permute-start | bytes 1179656 | tf_op jit(solution)/shard_map/ppermute | solution.py:303
  81.2 10.3 %collective-permute-start = (bf16[8,96,256]{2,1,0:T(8,128)(2,1)S(1)}, bf16[8,96,256]{2,1,0:T(8,128)(2,1)S(1)}, u32[]{:S(2)}, u32[]{:S(2)}) collective-permute-start(bf16[8,96,256]{2,1,0:T(8,128)(2,1)S(1)} %get-tuple-element.25.refs_1_), channel_id=1, source_target_pairs={{0,2},{2,4},{4,6},{6,0},{1,3},{3,5},{5,7},{7,1},{8,10},{10,12},{12... | collective-permute-start | bytes 1179656 | tf_op jit(solution)/shard_map/ppermute | solution.py:298
  82.1 10.3 %collective-permute-start.14 = (bf16[16,96,128]{2,1,0:T(8,128)(2,1)S(1)}, bf16[16,96,128]{2,1,0:T(8,128)(2,1)S(1)}, u32[]{:S(2)}, u32[]{:S(2)}) collective-permute-start(bf16[16,96,128]{2,1,0:T(8,128)(2,1)S(1)} %get-tuple-element.28), channel_id=1, source_target_pairs={{0,1},{1,0},{2,3},{3,2},{4,5},{5,4},{6,7},{7,6},{8,9},{9,8},{10,11... | collective-permute-start | bytes 1179656 | tf_op jit(solution)/shard_map/ppermute | solution.py:303
  82.8 12.0 %collective-permute-start.2 = (bf16[8,96,256]{2,1,0:T(8,128)(2,1)S(1)}, bf16[8,96,256]{2,1,0:T(8,128)(2,1)S(1)}, u32[]{:S(2)}, u32[]{:S(2)}) collective-permute-start(bf16[8,96,256]{2,1,0:T(8,128)(2,1)S(1)} %get-tuple-element.26.refs_2_), channel_id=1, source_target_pairs={{0,6},{2,0},{4,2},{6,4},{1,7},{3,1},{5,3},{7,5},{8,14},{10,8},{12,... | collective-permute-start | bytes 1179656 | tf_op jit(solution)/shard_map/ppermute | solution.py:298
  83.3 22.5 %collective-permute-start.4 = (bf16[8,96,256]{2,1,0:T(8,128)(2,1)S(1)}, bf16[8,96,256]{2,1,0:T(8,128)(2,1)S(1)}, u32[]{:S(2)}, u32[]{:S(2)}) collective-permute-start(bf16[8,96,256]{2,1,0:T(8,128)(2,1)S(1)} %get-tuple-element.26.refs_2_), channel_id=1, source_target_pairs={{0,2},{2,4},{4,6},{6,0},{1,3},{3,5},{5,7},{7,1},{8,10},{10,12},{12... | collective-permute-start | bytes 1179656 | tf_op jit(solution)/shard_map/ppermute | solution.py:298
  84.3 22.0 %collective-permute-start.6 = (bf16[8,96,256]{2,1,0:T(8,128)(2,1)S(1)}, bf16[8,96,256]{2,1,0:T(8,128)(2,1)S(1)}, u32[]{:S(2)}, u32[]{:S(2)}) collective-permute-start(bf16[8,96,256]{2,1,0:T(8,128)(2,1)S(1)} %get-tuple-element.25.refs_1_), channel_id=1, source_target_pairs={{0,6},{2,0},{4,2},{6,4},{1,7},{3,1},{5,3},{7,5},{8,14},{10,8},{12,... | collective-permute-start | bytes 1179656 | tf_op jit(solution)/shard_map/ppermute | solution.py:298
  91.4 16.9 %collective-permute-start.8 = (bf16[8,96,256]{2,1,0:T(8,128)(2,1)S(1)}, bf16[8,96,256]{2,1,0:T(8,128)(2,1)S(1)}, u32[]{:S(2)}, u32[]{:S(2)}) collective-permute-start(bf16[8,96,256]{2,1,0:T(8,128)(2,1)S(1)} %collective-permute-done.refs_1_), channel_id=1, source_target_pairs={{0,2},{2,4},{4,6},{6,0},{1,3},{3,5},{5,7},{7,1},{8,10},{10,12},{12... | collective-permute-start | bytes 1179656 | tf_op jit(solution)/shard_map/ppermute | solution.py:298
  92.4 18.8 %collective-permute-start.1 = (bf16[8,96,256]{2,1,0:T(8,128)(2,1)S(1)}, bf16[8,96,256]{2,1,0:T(8,128)(2,1)S(1)}, u32[]{:S(2)}, u32[]{:S(2)}) collective-permute-start(bf16[8,96,256]{2,1,0:T(8,128)(2,1)S(1)} %collective-permute-done.refs_1_), channel_id=1, source_target_pairs={{0,1},{1,0},{2,3},{3,2},{4,5},{5,4},{6,7},{7,6},{8,9},{9,8},{10,11... | collective-permute-start | bytes 1179656 | tf_op jit(solution)/shard_map/ppermute | solution.py:303
  94.8 15.5 %collective-permute-start.9 = (bf16[8,96,256]{2,1,0:T(8,128)(2,1)S(1)}, bf16[8,96,256]{2,1,0:T(8,128)(2,1)S(1)}, u32[]{:S(2)}, u32[]{:S(2)}) collective-permute-start(bf16[8,96,256]{2,1,0:T(8,128)(2,1)S(1)} %collective-permute-done.2.refs_2_), channel_id=1, source_target_pairs={{0,6},{2,0},{4,2},{6,4},{1,7},{3,1},{5,3},{7,5},{8,14},{10,8},{12,... | collective-permute-start | bytes 1179656 | tf_op jit(solution)/shard_map/ppermute | solution.py:298
  105.9 18.8 %collective-permute-start.3 = (bf16[8,96,256]{2,1,0:T(8,128)(2,1)S(1)}, bf16[8,96,256]{2,1,0:T(8,128)(2,1)S(1)}, u32[]{:S(2)}, u32[]{:S(2)}) collective-permute-start(bf16[8,96,256]{2,1,0:T(8,128)(2,1)S(1)} %collective-permute-done.2.refs_2_), channel_id=1, source_target_pairs={{0,1},{1,0},{2,3},{3,2},{4,5},{5,4},{6,7},{7,6},{8,9},{9,8},{10,11... | collective-permute-start | bytes 1179656 | tf_op jit(solution)/shard_map/ppermute | solution.py:303
  106.3 18.3 %collective-permute-start.5 = (bf16[8,96,256]{2,1,0:T(8,128)(2,1)S(1)}, bf16[8,96,256]{2,1,0:T(8,128)(2,1)S(1)}, u32[]{:S(2)}, u32[]{:S(2)}) collective-permute-start(bf16[8,96,256]{2,1,0:T(8,128)(2,1)S(1)} %collective-permute-done.4.refs_3_), channel_id=1, source_target_pairs={{0,1},{1,0},{2,3},{3,2},{4,5},{5,4},{6,7},{7,6},{8,9},{9,8},{10,11... | collective-permute-start | bytes 1179656 | tf_op jit(solution)/shard_map/ppermute | solution.py:303
  108.3 16.4 %collective-permute-start.7 = (bf16[8,96,256]{2,1,0:T(8,128)(2,1)S(1)}, bf16[8,96,256]{2,1,0:T(8,128)(2,1)S(1)}, u32[]{:S(2)}, u32[]{:S(2)}) collective-permute-start(bf16[8,96,256]{2,1,0:T(8,128)(2,1)S(1)} %collective-permute-done.6.refs_4_), channel_id=1, source_target_pairs={{0,1},{1,0},{2,3},{3,2},{4,5},{5,4},{6,7},{7,6},{8,9},{9,8},{10,11... | collective-permute-start | bytes 1179656 | tf_op jit(solution)/shard_map/ppermute | solution.py:303
  110.3 14.3 %collective-permute-start.10 = (bf16[8,96,256]{2,1,0:T(8,128)(2,1)S(1)}, bf16[8,96,256]{2,1,0:T(8,128)(2,1)S(1)}, u32[]{:S(2)}, u32[]{:S(2)}) collective-permute-start(bf16[8,96,256]{2,1,0:T(8,128)(2,1)S(1)} %collective-permute-done.8.refs_5_), channel_id=1, source_target_pairs={{0,1},{1,0},{2,3},{3,2},{4,5},{5,4},{6,7},{7,6},{8,9},{9,8},{10,11... | collective-permute-start | bytes 1179656 | tf_op jit(solution)/shard_map/ppermute | solution.py:303
  111.2 13.5 %collective-permute-start.11 = (bf16[8,96,256]{2,1,0:T(8,128)(2,1)S(1)}, bf16[8,96,256]{2,1,0:T(8,128)(2,1)S(1)}, u32[]{:S(2)}, u32[]{:S(2)}) collective-permute-start(bf16[8,96,256]{2,1,0:T(8,128)(2,1)S(1)} %collective-permute-done.9.refs_6_), channel_id=1, source_target_pairs={{0,1},{1,0},{2,3},{3,2},{4,5},{5,4},{6,7},{7,6},{8,9},{9,8},{10,11... | collective-permute-start | bytes 1179656 | tf_op jit(solution)/shard_map/ppermute | solution.py:303
  135.5 16.6 %collective-permute-start.16 = (bf16[768,128]{1,0:T(8,128)(2,1)S(1)}, bf16[768,128]{1,0:T(8,128)(2,1)S(1)}, u32[]{:S(2)}, u32[]{:S(2)}) collective-permute-start(bf16[768,128]{1,0:T(8,128)(2,1)S(1)} %get-tuple-element.43), channel_id=1, source_target_pairs={{0,8},{8,0},{1,9},{9,1},{2,10},{10,2},{3,11},{11,3},{4,12},{12,4},... | collective-permute-start | bytes 589832 | tf_op jit(solution)/shard_map/ppermute | solution.py:303
  137.1 15.0 %collective-permute-start.17 = (bf16[768,128]{1,0:T(8,128)(2,1)S(1)}, bf16[768,128]{1,0:T(8,128)(2,1)S(1)}, u32[]{:S(2)}, u32[]{:S(2)}) collective-permute-start(bf16[768,128]{1,0:T(8,128)(2,1)S(1)} %get-tuple-element.44), channel_id=1, source_target_pairs={{0,9},{1,8},{8,1},{9,0},{2,11},{3,10},{10,3},{11,2},{4,13},{5,12},... | collective-permute-start | bytes 589832 | tf_op jit(solution)/shard_map/ppermute | solution.py:303
  149.6 3.6 %collective-permute-start.15 = (bf16[768,128]{1,0:T(8,128)(2,1)S(1)}, bf16[768,128]{1,0:T(8,128)(2,1)S(1)}, u32[]{:S(2)}, u32[]{:S(2)}) collective-permute-start(bf16[768,128]{1,0:T(8,128)(2,1)S(1)} %get-tuple-element.39), channel_id=1, source_target_pairs={{0,1},{1,0},{2,3},{3,2},{4,5},{5,4},{6,7},{7,6},{8,9},{9,8},{10,11... | collective-permute-start | bytes 589832 | tf_op jit(solution)/shard_map/ppermute | solution.py:303

commit v6 on v5

--- a/solution.py
+++ b/solution.py
@@ -165,13 +165,18 @@
         for _ in range(UNROLL):
             item = after(item)
             nxt.append(item)
-        for k in range(UNROLL):
-            weigh(cur[k], s_bufs[k], p_bufs[k])
-            score(nxt[k], s_bufs[k])
-            if k == 0:
-                gather(prev, p_bufs[UNROLL - 1])
-            else:
-                gather(cur[k - 1], p_bufs[k - 1])
+        weigh(cur[0], s_bufs[0], p_bufs[0])
+        weigh(cur[1], s_bufs[1], p_bufs[1])
+        gather(prev, p_bufs[3])
+        score(nxt[0], s_bufs[0])
+        score(nxt[1], s_bufs[1])
+        gather(cur[0], p_bufs[0])
+        weigh(cur[2], s_bufs[2], p_bufs[2])
+        score(nxt[2], s_bufs[2])
+        weigh(cur[3], s_bufs[3], p_bufs[3])
+        gather(cur[1], p_bufs[1])
+        gather(cur[2], p_bufs[2])
+        score(nxt[3], s_bufs[3])
         return tuple(nxt), cur[-1]
 
     idle = (count, jnp.int32(dummy_tile))
@@ -254,21 +259,22 @@
     )(*inputs)
 
 
-def sort_kernel(query, key, value, out, sems):
-    copies = []
-    for head in range(16):
-        for source, left, width in ((query, 0, 2 * HEAD), (key, 2 * HEAD, HEAD), (value, 3 * HEAD, HEAD)):
-            copies.append(
-                pltpu.make_async_copy(
-                    source.at[:, head * width : (head + 1) * width],
-                    out.at[head, :, left : left + width],
-                    sems.at[len(copies)],
-                )
-            )
+def sort_kernel(query, key, value, out, q_rows, k_rows, v_rows, packed, sems):
+    copies = [
+        pltpu.make_async_copy(source, rows, sems.at[n])
+        for n, (source, rows) in enumerate(((query, q_rows), (key, k_rows), (value, v_rows)))
+    ]
     for copy in copies:
         copy.start()
     for copy in copies:
         copy.wait()
+    for head in range(16):
+        packed[head, :, : 2 * HEAD] = q_rows[:, 2 * head * HEAD : 2 * (head + 1) * HEAD]
+        packed[head, :, 2 * HEAD : 3 * HEAD] = k_rows[:, head * HEAD : (head + 1) * HEAD]
+        packed[head, :, 3 * HEAD :] = v_rows[:, head * HEAD : (head + 1) * HEAD]
+    done = pltpu.make_async_copy(packed, out, sems.at[3])
+    done.start()
+    done.wait()
 
 
 def split_kernel(got, low, high, keep, send):
@@ -310,7 +316,13 @@
         out_shape=jax.ShapeDtypeStruct((16, rows, 4 * HEAD), jnp.bfloat16),
         in_specs=[pl.BlockSpec(memory_space=pltpu.HBM)] * 3,
         out_specs=pl.BlockSpec(memory_space=pltpu.HBM),
-        scratch_shapes=[pltpu.SemaphoreType.DMA((48,))],
+        scratch_shapes=[
+            pltpu.VMEM(query.shape, jnp.bfloat16),
+            pltpu.VMEM(key.shape, jnp.bfloat16),
+            pltpu.VMEM(value.shape, jnp.bfloat16),
+            pltpu.VMEM((16, rows, 4 * HEAD), jnp.bfloat16),
+            pltpu.SemaphoreType.DMA((4,)),
+        ],
         compiler_params=pltpu.CompilerParams(vmem_limit_bytes=62 * 1024 * 1024),
         name="k_sort",
     )(query, key, value)
@@ -344,7 +356,8 @@
     state = step(own, both, (keep, got), first=True)
     state = step(near, both, state)
     remote, local = state[:3], state[3:]
-    same, cross = step(near_o + far, (REMOTE,), remote, last=True)
+    remote = step(near_o, (REMOTE,), remote)
+    same, cross = step(far, (REMOTE,), remote, last=True)
     z_same = mirror(same, "zhi")
     z_cross = mirror(cross, ("zhi", "core"))
     mine, cross = step(near_o + far, (LOCAL,), local, last=True)

time: 154 us -> 108 us (0.70)
  Pallas kernels: 97.1 us -> 50.5 us
    pallas_call x1, Pallas kernels: 49.2 us -> 2.72 us  [layer(): pl.pallas_call(sort_kernel, out_shape=jax.ShapeDtypeStruct((16, rows, 4 *...]
    pallas_call x4 -> x5, Pallas kernels: 46.7 us -> 46.5 us  [attend(): pl.pallas_call(functools.partial(attend_kernel, offsets=offsets, halves=h...]
  transfers between devices with their start and end apart: 18 -> 18, of which waited for: 4 -> 4; matrix products, arithmetic and copies ran while one was open for 0% -> 0% of each run, Pallas kernels for 23% -> 37%
where the time goes in v6:
time: 108 us
  Pallas kernels  50.5 us (47%)
  blocking collectives  29.6 us (27%)
  starting transfers between devices  17.5 us (16%)
  waiting for transfers between devices  10.3 us (10%)
    pallas_call x5, Pallas kernels, attend(): pl.pallas_call(functools.partial(attend_kernel, offsets=offsets, halves=h...  46.5 us
    all_to_all x1, blocking collectives, layer(): packed = lax.all_to_all(packed, ('y', 'zlo', 'zhi'), 0, 0)  29.6 us
    ppermute x12, starting transfers between devices, mirror(): return lax.ppermute(value, axes, [(i, size - 1 - i) for i in range(size)])  13.1 us
    ppermute x6, waiting for transfers between devices, along(): return lax.ppermute(value, axis, [(i, (i + by) % 4) for i in range(4)])  9.2 us
    ppermute x6, starting transfers between devices, along(): return lax.ppermute(value, axis, [(i, (i + by) % 4) for i in range(4)])  4.4 us
    pallas_call x1, Pallas kernels, layer(): pl.pallas_call(sort_kernel, out_shape=jax.ShapeDtypeStruct((16, rows, 4 *...  2.72 us
  transfers between devices with their start and end apart: 18, of which 4 were waited for; matrix products, arithmetic and copies ran while one was open for 0% of the time, Pallas kernels for 37%

profile of v6, /device:TPU:5, one launch (start us, length us, event | category | flops | bytes accessed | tf_op | source)
XLA Modules:
  0.0 108.1 jit_solution(11976631235049941927)
XLA Ops:
  0.0 2.7 %k_sort.1 = bf16[16,96,512]{2,1,0:T(8,128)(2,1)} custom-call(bf16[96,4096]{1,0:T(8,128)(2,1)} %query.1, bf16[96,2048]{1,0:T(8,128)(2,1)} %key.1, bf16[96,2048]{1,0:T(8,128)(2,1)} %value.1), custom_call_target="tpu_custom_call" | custom-call | tf_op jit(solution)/shard_map/k_sort/pallas_call | solution.py:314
  2.7 29.6 %all_to_all.5.got = bf16[16,96,512]{2,1,0:T(8,128)(2,1)S(1)} all-to-all(bf16[16,96,512]{2,1,0:T(8,128)(2,1)} %k_sort.1), channel_id=1, replica_groups=mesh['y'=4,'zlo'=2,'zhi'=2,'x'=4,'core'=2] {'y','zlo','zhi'}, dimensions={0} | all-to-all | bytes 3145728 | tf_op jit(solution)/shard_map/all_to_all | solution.py:329
  32.3 0.0 copy-start
  32.3 0.2 shard_map.46
  32.5 2.1 %collective-permute-start.12 = (bf16[8,96,256]{2,1,0:T(8,128)(2,1)S(1)}, bf16[8,96,256]{2,1,0:T(8,128)(2,1)S(1)}, u32[]{:S(2)}, u32[]{:S(2)}) collective-permute-start(bf16[8,96,256]{2,1,0:T(8,128)(2,1)S(1)} %get-tuple-element.28.refs_1_), channel_id=1, source_target_pairs={{0,1},{1,0},{2,3},{3,2},{4,5},{5,4},{6,7},{7,6},{8,9},{9,8},{10,11... | collective-permute-start | bytes 1179656 | tf_op jit(solution)/shard_map/ppermute | solution.py:309
  34.6 0.1 collective-permute-start.13
  34.7 0.9 collective-permute-start
  35.6 0.7 collective-permute-start.14
  36.3 0.5 collective-permute-start.2
  36.9 0.0 collective-permute-done.12.refs_3_
  36.9 0.9 collective-permute-start.4
  37.8 0.0 collective-permute-done.13.refs_4_
  37.8 0.5 collective-permute-start.6
  38.4 6.6 %collective-permute-done.refs_1_ = bf16[8,96,256]{2,1,0:T(8,128)(2,1)S(1)} collective-permute-done((bf16[8,96,256]{2,1,0:T(8,128)(2,1)S(1)}, bf16[8,96,256]{2,1,0:T(8,128)(2,1)S(1)}, u32[]{:S(2)}, u32[]{:S(2)}) %collective-permute-start) | collective-permute-done | bytes 393248 | tf_op jit(solution)/shard_map/ppermute | solution.py:304
  45.0 2.1 %collective-permute-start.1 = (bf16[8,96,256]{2,1,0:T(8,128)(2,1)S(1)}, bf16[8,96,256]{2,1,0:T(8,128)(2,1)S(1)}, u32[]{:S(2)}, u32[]{:S(2)}) collective-permute-start(bf16[8,96,256]{2,1,0:T(8,128)(2,1)S(1)} %collective-permute-done.refs_1_), channel_id=1, source_target_pairs={{0,1},{1,0},{2,3},{3,2},{4,5},{5,4},{6,7},{7,6},{8,9},{9,8},{10,11... | collective-permute-start | bytes 1179656 | tf_op jit(solution)/shard_map/ppermute | solution.py:309
  47.1 0.0 collective-permute-done.14.refs_6_
  47.1 0.9 collective-permute-start.8
  48.0 0.0 collective-permute-done.2.refs_2_
  48.0 0.5 collective-permute-start.9
  48.6 0.0 copy-done
  48.6 10.2 %shard_map.47 = (bf16[6,128,256]{2,1,0:T(8,128)(2,1)S(1)}, f32[6,128,256]{2,1,0:T(8,128)S(1)}, f32[6,8,256]{2,1,0:T(8,128)S(1)}, bf16[6,128,256]{2,1,0:T(8,128)(...) custom-call(s32[32]{0:T(128)S(1)} %copy-done, bf16[8,96,256]{2,1,0:T(8,128)(2,1)S(1)} %get-tuple-element.28.refs_1_, ...), custom_call_target="tpu_custom_call" | custom-call | flops 4800000000 | bytes 4000000 | tf_op jit(solution)/shard_map/pallas_call | solution.py:220
  58.8 0.0 collective-permute-done.4.refs_3_
  58.8 0.7 collective-permute-start.3
  59.5 0.0 collective-permute-done.6.refs_4_
  59.5 0.1 collective-permute-start.5
  59.6 0.0 collective-permute-done.1.refs_1_
  59.6 0.4 collective-permute-start.7
  60.0 1.8 %collective-permute-done.8.refs_5_.refs_1_ = bf16[8,96,256]{2,1,0:T(8,128)(2,1)S(1)} collective-permute-done((bf16[8,96,256]{2,1,0:T(8,128)(2,1)S(1)}, bf16[8,96,256]{2,1,0:T(8,128)(2,1)S(1)}, u32[]{:S(2)}, u32[]{:S(2)}) %collective-permute-start.8) | collective-permute-done | bytes 393248 | tf_op jit(solution)/shard_map/ppermute | solution.py:304
  61.8 1.3 %collective-permute-start.10 = (bf16[8,96,256]{2,1,0:T(8,128)(2,1)S(1)}, bf16[8,96,256]{2,1,0:T(8,128)(2,1)S(1)}, u32[]{:S(2)}, u32[]{:S(2)}) collective-permute-start(bf16[8,96,256]{2,1,0:T(8,128)(2,1)S(1)} %collective-permute-done.8.refs_5_.refs_1_), channel_id=1, source_target_pairs={{0,1},{1,0},{2,3},{3,2},{4,5},{5,4},{6,7},{7,6},{8,9},{9,8},{10,11... | collective-permute-start | bytes 1179656 | tf_op jit(solution)/shard_map/ppermute | solution.py:309
  63.1 0.8 collective-permute-done.9.refs_6_.refs_2_
  63.9 0.9 collective-permute-start.11
  64.7 13.1 %shard_map.48 = (bf16[6,128,256]{2,1,0:T(8,128)(2,1)S(1)}, f32[6,128,256]{2,1,0:T(8,128)S(1)}, f32[6,8,256]{2,1,0:T(8,128)S(1)}, bf16[6,128,256]{2,1,0:T(8,128)(...) custom-call(s32[32]{0:T(128)S(1)} %copy-done, bf16[8,96,256]{2,1,0:T(8,128)(2,1)S(1)} %collective-permute-done.refs_1_, ...), custom_call_target="tpu_custom_call" | custom-call | flops 4800000000 | bytes 4000000 | tf_op jit(solution)/shard_map/pallas_call | solution.py:220
  77.8 0.0 collective-permute-done.3.refs_2_
  77.8 0.0 collective-permute-done.5.refs_3_
  77.8 0.0 collective-permute-done.7.refs_4_
  77.8 5.2 %shard_map.50 = (bf16[6,128,256]{2,1,0:T(8,128)(2,1)S(1)}, f32[6,128,256]{2,1,0:T(8,128)S(1)}, f32[6,8,256]{2,1,0:T(8,128)S(1)}) custom-call(s32[32]{0:T(128)S(1)} %copy-done, bf16[8,96,256]{2,1,0:T(8,128)(2,1)S(1)} %collective-permute-done.1.refs_1_, bf16[8,96,256]{2,1,0:T(8,128)(2,1)S(1)} %collective-permute-done.3.refs_2_, ...), custom_call_target="tpu_custom_call" | custom-call | flops 2400000000 | bytes 4000000 | tf_op jit(solution)/shard_map/pallas_call | solution.py:220
  83.0 0.0 collective-permute-done.10.refs_7_.refs_3_
  83.0 0.0 collective-permute-done.11.refs_8_.refs_4_
  83.1 6.4 %shard_map.51 = (bf16[768,128]{1,0:T(8,128)(2,1)S(1)}, bf16[768,128]{1,0:T(8,128)(2,1)S(1)}) custom-call(s32[32]{0:T(128)S(1)} %copy-done, bf16[8,96,256]{2,1,0:T(8,128)(2,1)S(1)} %collective-permute-done.8.refs_5_.refs_1_, bf16[8,96,256]{2,1,0:T(8,128)(2,1)S(1)} %collective-permute-done.9.refs_6_.refs_2_, ...), custom_call_target="tpu_custom_call" | custom-call | flops 2400000000 | bytes 4000000 | tf_op jit(solution)/shard_map/pallas_call | solution.py:220
  89.5 2.3 %collective-permute-start.16 = (bf16[768,128]{1,0:T(8,128)(2,1)S(1)}, bf16[768,128]{1,0:T(8,128)(2,1)S(1)}, u32[]{:S(2)}, u32[]{:S(2)}) collective-permute-start(bf16[768,128]{1,0:T(8,128)(2,1)S(1)} %get-tuple-element.49), channel_id=1, source_target_pairs={{0,8},{8,0},{1,9},{9,1},{2,10},{10,2},{3,11},{11,3},{4,12},{12,4},... | collective-permute-start | bytes 589832 | tf_op jit(solution)/shard_map/ppermute | solution.py:309
  91.8 0.0 collective-permute-start.17
  91.8 11.6 %shard_map.49 = (bf16[768,128]{1,0:T(8,128)(2,1)S(1)}, bf16[768,128]{1,0:T(8,128)(2,1)S(1)}) custom-call(s32[32]{0:T(128)S(1)} %copy-done, bf16[8,96,256]{2,1,0:T(8,128)(2,1)S(1)} %collective-permute-done.1.refs_1_, bf16[8,96,256]{2,1,0:T(8,128)(2,1)S(1)} %collective-permute-done.3.refs_2_, bf16[8,96,256]{2,1,0:T(8,128)(2,1)S(1)} %collective-permute-done.5.refs_3_, ...), custom_call_target="tpu_custom_call" | custom-call | flops 4800000000 | bytes 4000000 | tf_op jit(solution)/shard_map/pallas_call | solution.py:220
  103.4 2.5 %collective-permute-start.15 = (bf16[768,128]{1,0:T(8,128)(2,1)S(1)}, bf16[768,128]{1,0:T(8,128)(2,1)S(1)}, u32[]{:S(2)}, u32[]{:S(2)}) collective-permute-start(bf16[768,128]{1,0:T(8,128)(2,1)S(1)} %get-tuple-element.42), channel_id=1, source_target_pairs={{0,1},{1,0},{2,3},{3,2},{4,5},{5,4},{6,7},{7,6},{8,9},{9,8},{10,11... | collective-permute-start | bytes 589832 | tf_op jit(solution)/shard_map/ppermute | solution.py:309
  105.9 0.0 collective-permute-done.16.z_same
  105.9 0.0 collective-permute-done.17.z_cross
  105.9 1.1 collective-permute-done.15.swapped
  107.0 1.1 %shard_map.52 = bf16[768,512]{1,0:T(8,128)(2,1)} custom-call(bf16[768,128]{1,0:T(8,128)(2,1)S(1)} %get-tuple-element.41.own, bf16[768,128]{1,0:T(8,128)(2,1)S(1)} %collective-permute-done.15.swapped, bf16[768,128]{1,0:T(8,128)(2,1)S(1)} %collective-permute-done.16.z_same, bf16[768,128]{1,0:T(8,128)(2,1)S(1)} %collective-permute-done.17.z_cross), custom_call_target="tpu_custom_call" | custom-call | tf_op jit(solution)/shard_map/pallas_call | solution.py:253
Async XLA Ops:
  32.3 16.2 %copy-start = (s32[32]{0:T(128)S(1)}, s32[32]{0:T(128)}, u32[]{:S(2)}) copy-start(s32[32]{0:T(128)} %refs_0_.9) | copy-start | bytes 388
  32.5 4.3 %collective-permute-start.12 = (bf16[8,96,256]{2,1,0:T(8,128)(2,1)S(1)}, bf16[8,96,256]{2,1,0:T(8,128)(2,1)S(1)}, u32[]{:S(2)}, u32[]{:S(2)}) collective-permute-start(bf16[8,96,256]{2,1,0:T(8,128)(2,1)S(1)} %get-tuple-element.28.refs_1_), channel_id=1, source_target_pairs={{0,1},{1,0},{2,3},{3,2},{4,5},{5,4},{6,7},{7,6},{8,9},{9,8},{10,11... | collective-permute-start | bytes 1179656 | tf_op jit(solution)/shard_map/ppermute | solution.py:309
  34.6 3.2 %collective-permute-start.13 = (bf16[8,96,256]{2,1,0:T(8,128)(2,1)S(1)}, bf16[8,96,256]{2,1,0:T(8,128)(2,1)S(1)}, u32[]{:S(2)}, u32[]{:S(2)}) collective-permute-start(bf16[8,96,256]{2,1,0:T(8,128)(2,1)S(1)} %get-tuple-element.29.refs_2_), channel_id=1, source_target_pairs={{0,1},{1,0},{2,3},{3,2},{4,5},{5,4},{6,7},{7,6},{8,9},{9,8},{10,11... | collective-permute-start | bytes 1179656 | tf_op jit(solution)/shard_map/ppermute | solution.py:309
  34.7 10.3 %collective-permute-start = (bf16[8,96,256]{2,1,0:T(8,128)(2,1)S(1)}, bf16[8,96,256]{2,1,0:T(8,128)(2,1)S(1)}, u32[]{:S(2)}, u32[]{:S(2)}) collective-permute-start(bf16[8,96,256]{2,1,0:T(8,128)(2,1)S(1)} %get-tuple-element.28.refs_1_), channel_id=1, source_target_pairs={{0,2},{2,4},{4,6},{6,0},{1,3},{3,5},{5,7},{7,1},{8,10},{10,12},{12... | collective-permute-start | bytes 1179656 | tf_op jit(solution)/shard_map/ppermute | solution.py:304
  35.6 11.5 %collective-permute-start.14 = (bf16[16,96,128]{2,1,0:T(8,128)(2,1)S(1)}, bf16[16,96,128]{2,1,0:T(8,128)(2,1)S(1)}, u32[]{:S(2)}, u32[]{:S(2)}) collective-permute-start(bf16[16,96,128]{2,1,0:T(8,128)(2,1)S(1)} %get-tuple-element.31), channel_id=1, source_target_pairs={{0,1},{1,0},{2,3},{3,2},{4,5},{5,4},{6,7},{7,6},{8,9},{9,8},{10,11... | collective-permute-start | bytes 1179656 | tf_op jit(solution)/shard_map/ppermute | solution.py:309
  36.3 11.7 %collective-permute-start.2 = (bf16[8,96,256]{2,1,0:T(8,128)(2,1)S(1)}, bf16[8,96,256]{2,1,0:T(8,128)(2,1)S(1)}, u32[]{:S(2)}, u32[]{:S(2)}) collective-permute-start(bf16[8,96,256]{2,1,0:T(8,128)(2,1)S(1)} %get-tuple-element.29.refs_2_), channel_id=1, source_target_pairs={{0,6},{2,0},{4,2},{6,4},{1,7},{3,1},{5,3},{7,5},{8,14},{10,8},{12,... | collective-permute-start | bytes 1179656 | tf_op jit(solution)/shard_map/ppermute | solution.py:304
  36.9 21.9 %collective-permute-start.4 = (bf16[8,96,256]{2,1,0:T(8,128)(2,1)S(1)}, bf16[8,96,256]{2,1,0:T(8,128)(2,1)S(1)}, u32[]{:S(2)}, u32[]{:S(2)}) collective-permute-start(bf16[8,96,256]{2,1,0:T(8,128)(2,1)S(1)} %get-tuple-element.29.refs_2_), channel_id=1, source_target_pairs={{0,2},{2,4},{4,6},{6,0},{1,3},{3,5},{5,7},{7,1},{8,10},{10,12},{12... | collective-permute-start | bytes 1179656 | tf_op jit(solution)/shard_map/ppermute | solution.py:304
  37.8 21.7 %collective-permute-start.6 = (bf16[8,96,256]{2,1,0:T(8,128)(2,1)S(1)}, bf16[8,96,256]{2,1,0:T(8,128)(2,1)S(1)}, u32[]{:S(2)}, u32[]{:S(2)}) collective-permute-start(bf16[8,96,256]{2,1,0:T(8,128)(2,1)S(1)} %get-tuple-element.28.refs_1_), channel_id=1, source_target_pairs={{0,6},{2,0},{4,2},{6,4},{1,7},{3,1},{5,3},{7,5},{8,14},{10,8},{12,... | collective-permute-start | bytes 1179656 | tf_op jit(solution)/shard_map/ppermute | solution.py:304
  45.0 14.6 %collective-permute-start.1 = (bf16[8,96,256]{2,1,0:T(8,128)(2,1)S(1)}, bf16[8,96,256]{2,1,0:T(8,128)(2,1)S(1)}, u32[]{:S(2)}, u32[]{:S(2)}) collective-permute-start(bf16[8,96,256]{2,1,0:T(8,128)(2,1)S(1)} %collective-permute-done.refs_1_), channel_id=1, source_target_pairs={{0,1},{1,0},{2,3},{3,2},{4,5},{5,4},{6,7},{7,6},{8,9},{9,8},{10,11... | collective-permute-start | bytes 1179656 | tf_op jit(solution)/shard_map/ppermute | solution.py:309
  47.1 14.7 %collective-permute-start.8 = (bf16[8,96,256]{2,1,0:T(8,128)(2,1)S(1)}, bf16[8,96,256]{2,1,0:T(8,128)(2,1)S(1)}, u32[]{:S(2)}, u32[]{:S(2)}) collective-permute-start(bf16[8,96,256]{2,1,0:T(8,128)(2,1)S(1)} %collective-permute-done.refs_1_), channel_id=1, source_target_pairs={{0,2},{2,4},{4,6},{6,0},{1,3},{3,5},{5,7},{7,1},{8,10},{10,12},{12... | collective-permute-start | bytes 1179656 | tf_op jit(solution)/shard_map/ppermute | solution.py:304
  48.0 15.8 %collective-permute-start.9 = (bf16[8,96,256]{2,1,0:T(8,128)(2,1)S(1)}, bf16[8,96,256]{2,1,0:T(8,128)(2,1)S(1)}, u32[]{:S(2)}, u32[]{:S(2)}) collective-permute-start(bf16[8,96,256]{2,1,0:T(8,128)(2,1)S(1)} %collective-permute-done.2.refs_2_), channel_id=1, source_target_pairs={{0,6},{2,0},{4,2},{6,4},{1,7},{3,1},{5,3},{7,5},{8,14},{10,8},{12,... | collective-permute-start | bytes 1179656 | tf_op jit(solution)/shard_map/ppermute | solution.py:304
  58.8 19.0 %collective-permute-start.3 = (bf16[8,96,256]{2,1,0:T(8,128)(2,1)S(1)}, bf16[8,96,256]{2,1,0:T(8,128)(2,1)S(1)}, u32[]{:S(2)}, u32[]{:S(2)}) collective-permute-start(bf16[8,96,256]{2,1,0:T(8,128)(2,1)S(1)} %collective-permute-done.2.refs_2_), channel_id=1, source_target_pairs={{0,1},{1,0},{2,3},{3,2},{4,5},{5,4},{6,7},{7,6},{8,9},{9,8},{10,11... | collective-permute-start | bytes 1179656 | tf_op jit(solution)/shard_map/ppermute | solution.py:309
  59.5 18.3 %collective-permute-start.5 = (bf16[8,96,256]{2,1,0:T(8,128)(2,1)S(1)}, bf16[8,96,256]{2,1,0:T(8,128)(2,1)S(1)}, u32[]{:S(2)}, u32[]{:S(2)}) collective-permute-start(bf16[8,96,256]{2,1,0:T(8,128)(2,1)S(1)} %collective-permute-done.4.refs_3_), channel_id=1, source_target_pairs={{0,1},{1,0},{2,3},{3,2},{4,5},{5,4},{6,7},{7,6},{8,9},{9,8},{10,11... | collective-permute-start | bytes 1179656 | tf_op jit(solution)/shard_map/ppermute | solution.py:309
  59.6 18.2 %collective-permute-start.7 = (bf16[8,96,256]{2,1,0:T(8,128)(2,1)S(1)}, bf16[8,96,256]{2,1,0:T(8,128)(2,1)S(1)}, u32[]{:S(2)}, u32[]{:S(2)}) collective-permute-start(bf16[8,96,256]{2,1,0:T(8,128)(2,1)S(1)} %collective-permute-done.6.refs_4_), channel_id=1, source_target_pairs={{0,1},{1,0},{2,3},{3,2},{4,5},{5,4},{6,7},{7,6},{8,9},{9,8},{10,11... | collective-permute-start | bytes 1179656 | tf_op jit(solution)/shard_map/ppermute | solution.py:309
  61.8 21.2 %collective-permute-start.10 = (bf16[8,96,256]{2,1,0:T(8,128)(2,1)S(1)}, bf16[8,96,256]{2,1,0:T(8,128)(2,1)S(1)}, u32[]{:S(2)}, u32[]{:S(2)}) collective-permute-start(bf16[8,96,256]{2,1,0:T(8,128)(2,1)S(1)} %collective-permute-done.8.refs_5_.refs_1_), channel_id=1, source_target_pairs={{0,1},{1,0},{2,3},{3,2},{4,5},{5,4},{6,7},{7,6},{8,9},{9,8},{10,11... | collective-permute-start | bytes 1179656 | tf_op jit(solution)/shard_map/ppermute | solution.py:309
  63.9 19.2 %collective-permute-start.11 = (bf16[8,96,256]{2,1,0:T(8,128)(2,1)S(1)}, bf16[8,96,256]{2,1,0:T(8,128)(2,1)S(1)}, u32[]{:S(2)}, u32[]{:S(2)}) collective-permute-start(bf16[8,96,256]{2,1,0:T(8,128)(2,1)S(1)} %collective-permute-done.9.refs_6_.refs_2_), channel_id=1, source_target_pairs={{0,1},{1,0},{2,3},{3,2},{4,5},{5,4},{6,7},{7,6},{8,9},{9,8},{10,11... | collective-permute-start | bytes 1179656 | tf_op jit(solution)/shard_map/ppermute | solution.py:309
  89.5 16.4 %collective-permute-start.16 = (bf16[768,128]{1,0:T(8,128)(2,1)S(1)}, bf16[768,128]{1,0:T(8,128)(2,1)S(1)}, u32[]{:S(2)}, u32[]{:S(2)}) collective-permute-start(bf16[768,128]{1,0:T(8,128)(2,1)S(1)} %get-tuple-element.49), channel_id=1, source_target_pairs={{0,8},{8,0},{1,9},{9,1},{2,10},{10,2},{3,11},{11,3},{4,12},{12,4},... | collective-permute-start | bytes 589832 | tf_op jit(solution)/shard_map/ppermute | solution.py:309
  91.8 14.1 %collective-permute-start.17 = (bf16[768,128]{1,0:T(8,128)(2,1)S(1)}, bf16[768,128]{1,0:T(8,128)(2,1)S(1)}, u32[]{:S(2)}, u32[]{:S(2)}) collective-permute-start(bf16[768,128]{1,0:T(8,128)(2,1)S(1)} %get-tuple-element.50), channel_id=1, source_target_pairs={{0,9},{1,8},{8,1},{9,0},{2,11},{3,10},{10,3},{11,2},{4,13},{5,12},... | collective-permute-start | bytes 589832 | tf_op jit(solution)/shard_map/ppermute | solution.py:309
  103.4 3.6 %collective-permute-start.15 = (bf16[768,128]{1,0:T(8,128)(2,1)S(1)}, bf16[768,128]{1,0:T(8,128)(2,1)S(1)}, u32[]{:S(2)}, u32[]{:S(2)}) collective-permute-start(bf16[768,128]{1,0:T(8,128)(2,1)S(1)} %get-tuple-element.42), channel_id=1, source_target_pairs={{0,1},{1,0},{2,3},{3,2},{4,5},{5,4},{6,7},{7,6},{8,9},{9,8},{10,11... | collective-permute-start | bytes 589832 | tf_op jit(solution)/shard_map/ppermute | solution.py:309

commit v7 on v6

--- a/solution.py
+++ b/solution.py
@@ -343,9 +343,10 @@
 
     own = [(low, 0, 0, 0), (high, 0, 0, 1)]
     own += [(swap(low), 0, 1, 0), (swap(high), 0, 1, 1)]
-    near = [(up_low, 1, 0, 0), (down_high, 3, 0, 1), (up_high, 1, 0, 1), (down_low, 3, 0, 0)]
-    near_o = [(swap(up_low), 1, 1, 0), (swap(down_high), 3, 1, 1)]
-    near_o += [(swap(up_high), 1, 1, 1), (swap(down_low), 3, 1, 0)]
+    near = [(up_low, 1, 0, 0), (down_high, 3, 0, 1)]
+    near += [(swap(up_low), 1, 1, 0), (swap(down_high), 3, 1, 1)]
+    rest = [(up_high, 1, 0, 1), (down_low, 3, 0, 0)]
+    rest += [(swap(up_high), 1, 1, 1), (swap(down_low), 3, 1, 0)]
     far = [(far_low, 2, 0, 0), (far_high, 2, 0, 1)]
     far += [(swap(far_low), 2, 1, 0), (swap(far_high), 2, 1, 1)]
 
@@ -356,13 +357,15 @@
     state = step(own, both, (keep, got), first=True)
     state = step(near, both, state)
     remote, local = state[:3], state[3:]
-    remote = step(near_o, (REMOTE,), remote)
+    remote = step(rest, (REMOTE,), remote)
     same, cross = step(far, (REMOTE,), remote, last=True)
     z_same = mirror(same, "zhi")
     z_cross = mirror(cross, ("zhi", "core"))
-    mine, cross = step(near_o + far, (LOCAL,), local, last=True)
+    mine, cross = step(rest + far, (LOCAL,), local, last=True)
     swapped = mirror(cross, "core")
-    (out,) = local_call(assemble_kernel, [(2 * BLK, 4 * HEAD)], (mine, swapped, z_same, z_cross))
+    (out,) = local_call(
+        assemble_kernel, [(2 * BLK, 4 * HEAD)], (mine, swapped, z_same, z_cross)
+    )
     return out
 
 

time: 108 us -> 110 us (1.019)
  waiting for transfers between devices: 10.3 us -> 13.1 us
  starting transfers between devices: 17.5 us -> 16.4 us
    ppermute x6, waiting for transfers between devices: 9.2 us -> 11.7 us  [along(): return lax.ppermute(value, axis, [(i, (i + by) % 4) for i in range(4)])]
  transfers between devices with their start and end apart: 18 -> 18, of which waited for: 4 -> 3; matrix products, arithmetic and copies ran while one was open for 0% -> 0% of each run, Pallas kernels for 37% -> 37%
where the time goes in v7:
time: 110 us
  Pallas kernels  50.5 us (46%)
  blocking collectives  29.6 us (27%)
  starting transfers between devices  16.4 us (15%)
  waiting for transfers between devices  13.1 us (12%)
    pallas_call x5, Pallas kernels, attend(): pl.pallas_call(functools.partial(attend_kernel, offsets=offsets, halves=h...  46.5 us
    all_to_all x1, blocking collectives, layer(): packed = lax.all_to_all(packed, ('y', 'zlo', 'zhi'), 0, 0)  29.6 us
    ppermute x12, starting transfers between devices, mirror(): return lax.ppermute(value, axes, [(i, size - 1 - i) for i in range(size)])  12.3 us
    ppermute x6, waiting for transfers between devices, along(): return lax.ppermute(value, axis, [(i, (i + by) % 4) for i in range(4)])  11.7 us
    ppermute x6, starting transfers between devices, along(): return lax.ppermute(value, axis, [(i, (i + by) % 4) for i in range(4)])  4.11 us
    pallas_call x1, Pallas kernels, layer(): pl.pallas_call(sort_kernel, out_shape=jax.ShapeDtypeStruct((16, rows, 4 *...  2.72 us
  transfers between devices with their start and end apart: 18, of which 3 were waited for; matrix products, arithmetic and copies ran while one was open for 0% of the time, Pallas kernels for 37%

profile of v7, /device:TPU:5, one launch (start us, length us, event | category | flops | bytes accessed | tf_op | source)
XLA Modules:
  0.0 109.9 jit_solution(11208068087470155137)
XLA Ops:
  0.0 2.7 %k_sort.1 = bf16[16,96,512]{2,1,0:T(8,128)(2,1)} custom-call(bf16[96,4096]{1,0:T(8,128)(2,1)} %query.1, bf16[96,2048]{1,0:T(8,128)(2,1)} %key.1, bf16[96,2048]{1,0:T(8,128)(2,1)} %value.1), custom_call_target="tpu_custom_call" | custom-call | tf_op jit(solution)/shard_map/k_sort/pallas_call | solution.py:314
  2.7 29.6 %all_to_all.5.got = bf16[16,96,512]{2,1,0:T(8,128)(2,1)S(1)} all-to-all(bf16[16,96,512]{2,1,0:T(8,128)(2,1)} %k_sort.1), channel_id=1, replica_groups=mesh['y'=4,'zlo'=2,'zhi'=2,'x'=4,'core'=2] {'y','zlo','zhi'}, dimensions={0} | all-to-all | bytes 3145728 | tf_op jit(solution)/shard_map/all_to_all | solution.py:329
  32.3 0.0 copy-start
  32.3 0.2 shard_map.46
  32.5 2.1 %collective-permute-start.12 = (bf16[8,96,256]{2,1,0:T(8,128)(2,1)S(1)}, bf16[8,96,256]{2,1,0:T(8,128)(2,1)S(1)}, u32[]{:S(2)}, u32[]{:S(2)}) collective-permute-start(bf16[8,96,256]{2,1,0:T(8,128)(2,1)S(1)} %get-tuple-element.29.refs_1_), channel_id=1, source_target_pairs={{0,1},{1,0},{2,3},{3,2},{4,5},{5,4},{6,7},{7,6},{8,9},{9,8},{10,11... | collective-permute-start | bytes 1179656 | tf_op jit(solution)/shard_map/ppermute | solution.py:309
  34.6 0.1 collective-permute-start.13
  34.7 0.9 collective-permute-start.4
  35.6 0.7 collective-permute-start.14
  36.3 0.5 collective-permute-start.6
  36.9 0.0 collective-permute-done.12.refs_3_
  36.9 0.9 collective-permute-start
  37.8 0.0 collective-permute-done.13.refs_4_
  37.8 0.5 collective-permute-start.1
  38.4 6.6 %collective-permute-done.4.refs_1_ = bf16[8,96,256]{2,1,0:T(8,128)(2,1)S(1)} collective-permute-done((bf16[8,96,256]{2,1,0:T(8,128)(2,1)S(1)}, bf16[8,96,256]{2,1,0:T(8,128)(2,1)S(1)}, u32[]{:S(2)}, u32[]{:S(2)}) %collective-permute-start.4) | collective-permute-done | bytes 393248 | tf_op jit(solution)/shard_map/ppermute | solution.py:304
  45.0 2.1 %collective-permute-start.10 = (bf16[8,96,256]{2,1,0:T(8,128)(2,1)S(1)}, bf16[8,96,256]{2,1,0:T(8,128)(2,1)S(1)}, u32[]{:S(2)}, u32[]{:S(2)}) collective-permute-start(bf16[8,96,256]{2,1,0:T(8,128)(2,1)S(1)} %collective-permute-done.4.refs_1_), channel_id=1, source_target_pairs={{0,1},{1,0},{2,3},{3,2},{4,5},{5,4},{6,7},{7,6},{8,9},{9,8},{10,11... | collective-permute-start | bytes 1179656 | tf_op jit(solution)/shard_map/ppermute | solution.py:309
  47.1 0.0 collective-permute-done.14.refs_6_
  47.1 0.9 collective-permute-start.5
  48.0 0.0 collective-permute-done.6.refs_2_
  48.0 0.3 collective-permute-start.11
  48.3 5.1 %collective-permute-done.refs_1_ = bf16[8,96,256]{2,1,0:T(8,128)(2,1)S(1)} collective-permute-done((bf16[8,96,256]{2,1,0:T(8,128)(2,1)S(1)}, bf16[8,96,256]{2,1,0:T(8,128)(2,1)S(1)}, u32[]{:S(2)}, u32[]{:S(2)}) %collective-permute-start) | collective-permute-done | bytes 393248 | tf_op jit(solution)/shard_map/ppermute | solution.py:304
  53.4 0.3 collective-permute-start.7
  53.7 0.0 copy-done
  53.7 10.2 %shard_map.47 = (bf16[6,128,256]{2,1,0:T(8,128)(2,1)S(1)}, f32[6,128,256]{2,1,0:T(8,128)S(1)}, f32[6,8,256]{2,1,0:T(8,128)S(1)}, bf16[6,128,256]{2,1,0:T(8,128)(...) custom-call(s32[32]{0:T(128)S(1)} %copy-done, bf16[8,96,256]{2,1,0:T(8,128)(2,1)S(1)} %get-tuple-element.29.refs_1_, ...), custom_call_target="tpu_custom_call" | custom-call | flops 4800000000 | bytes 4000000 | tf_op jit(solution)/shard_map/pallas_call | solution.py:220
  63.9 0.0 collective-permute-done.1.refs_2_
  63.9 2.5 %collective-permute-start.2 = (bf16[8,96,256]{2,1,0:T(8,128)(2,1)S(1)}, bf16[8,96,256]{2,1,0:T(8,128)(2,1)S(1)}, u32[]{:S(2)}, u32[]{:S(2)}) collective-permute-start(bf16[8,96,256]{2,1,0:T(8,128)(2,1)S(1)} %collective-permute-done.refs_1_), channel_id=1, source_target_pairs={{0,1},{1,0},{2,3},{3,2},{4,5},{5,4},{6,7},{7,6},{8,9},{9,8},{10,11... | collective-permute-start | bytes 1179656 | tf_op jit(solution)/shard_map/ppermute | solution.py:309
  66.4 0.0 collective-permute-done.10.refs_3_
  66.4 0.1 collective-permute-start.3
  66.5 0.0 collective-permute-done.5.refs_5_.refs_1_
  66.5 0.4 collective-permute-start.8
  66.9 0.0 collective-permute-done.7.refs_6_.refs_2_
  66.9 0.1 collective-permute-start.9
  67.0 0.0 collective-permute-done.11.refs_4_
  67.0 10.9 %shard_map.48 = (bf16[6,128,256]{2,1,0:T(8,128)(2,1)S(1)}, f32[6,128,256]{2,1,0:T(8,128)S(1)}, f32[6,8,256]{2,1,0:T(8,128)S(1)}, bf16[6,128,256]{2,1,0:T(8,128)(...) custom-call(s32[32]{0:T(128)S(1)} %copy-done, bf16[8,96,256]{2,1,0:T(8,128)(2,1)S(1)} %collective-permute-done.4.refs_1_, ...), custom_call_target="tpu_custom_call" | custom-call | flops 4800000000 | bytes 4000000 | tf_op jit(solution)/shard_map/pallas_call | solution.py:220
  78.0 0.0 collective-permute-done.2.refs_3_
  78.0 0.0 collective-permute-done.3.refs_4_
  78.0 6.3 %shard_map.50 = (bf16[6,128,256]{2,1,0:T(8,128)(2,1)S(1)}, f32[6,128,256]{2,1,0:T(8,128)S(1)}, f32[6,8,256]{2,1,0:T(8,128)S(1)}) custom-call(s32[32]{0:T(128)S(1)} %copy-done, bf16[8,96,256]{2,1,0:T(8,128)(2,1)S(1)} %collective-permute-done.refs_1_, bf16[8,96,256]{2,1,0:T(8,128)(2,1)S(1)} %collective-permute-done.1.refs_2_, ...), custom_call_target="tpu_custom_call" | custom-call | flops 2400000000 | bytes 4000000 | tf_op jit(solution)/shard_map/pallas_call | solution.py:220
  84.3 0.0 collective-permute-done.8.refs_7_.refs_3_
  84.3 0.0 collective-permute-done.9.refs_8_.refs_4_
  84.3 6.4 %shard_map.51 = (bf16[768,128]{1,0:T(8,128)(2,1)S(1)}, bf16[768,128]{1,0:T(8,128)(2,1)S(1)}) custom-call(s32[32]{0:T(128)S(1)} %copy-done, bf16[8,96,256]{2,1,0:T(8,128)(2,1)S(1)} %collective-permute-done.5.refs_5_.refs_1_, bf16[8,96,256]{2,1,0:T(8,128)(2,1)S(1)} %collective-permute-done.7.refs_6_.refs_2_, ...), custom_call_target="tpu_custom_call" | custom-call | flops 2400000000 | bytes 4000000 | tf_op jit(solution)/shard_map/pallas_call | solution.py:220
  90.7 1.7 %collective-permute-start.16 = (bf16[768,128]{1,0:T(8,128)(2,1)S(1)}, bf16[768,128]{1,0:T(8,128)(2,1)S(1)}, u32[]{:S(2)}, u32[]{:S(2)}) collective-permute-start(bf16[768,128]{1,0:T(8,128)(2,1)S(1)} %get-tuple-element.49), channel_id=1, source_target_pairs={{0,8},{8,0},{1,9},{9,1},{2,10},{10,2},{3,11},{11,3},{4,12},{12,4},... | collective-permute-start | bytes 589832 | tf_op jit(solution)/shard_map/ppermute | solution.py:309
  92.5 2.1 %collective-permute-start.17 = (bf16[768,128]{1,0:T(8,128)(2,1)S(1)}, bf16[768,128]{1,0:T(8,128)(2,1)S(1)}, u32[]{:S(2)}, u32[]{:S(2)}) collective-permute-start(bf16[768,128]{1,0:T(8,128)(2,1)S(1)} %get-tuple-element.50), channel_id=1, source_target_pairs={{0,9},{1,8},{8,1},{9,0},{2,11},{3,10},{10,3},{11,2},{4,13},{5,12},... | collective-permute-start | bytes 589832 | tf_op jit(solution)/shard_map/ppermute | solution.py:309
  94.5 12.7 %shard_map.49 = (bf16[768,128]{1,0:T(8,128)(2,1)S(1)}, bf16[768,128]{1,0:T(8,128)(2,1)S(1)}) custom-call(s32[32]{0:T(128)S(1)} %copy-done, bf16[8,96,256]{2,1,0:T(8,128)(2,1)S(1)} %collective-permute-done.refs_1_, bf16[8,96,256]{2,1,0:T(8,128)(2,1)S(1)} %collective-permute-done.1.refs_2_, bf16[8,96,256]{2,1,0:T(8,128)(2,1)S(1)} %collective-permute-done.2.refs_3_, ...), custom_call_target="tpu_custom_call" | custom-call | flops 4800000000 | bytes 4000000 | tf_op jit(solution)/shard_map/pallas_call | solution.py:220
  107.2 0.1 collective-permute-start.15
  107.3 0.0 collective-permute-done.16.z_same
  107.3 0.0 collective-permute-done.17.z_cross
  107.4 1.4 %collective-permute-done.15.swapped = bf16[768,128]{1,0:T(8,128)(2,1)S(1)} collective-permute-done((bf16[768,128]{1,0:T(8,128)(2,1)S(1)}, bf16[768,128]{1,0:T(8,128)(2,1)S(1)}, u32[]{:S(2)}, u32[]{:S(2)}) %collective-permute-start.15) | collective-permute-done | bytes 196640 | tf_op jit(solution)/shard_map/ppermute | solution.py:309
  108.8 1.1 shard_map.52
Async XLA Ops:
  32.3 21.3 %copy-start = (s32[32]{0:T(128)S(1)}, s32[32]{0:T(128)}, u32[]{:S(2)}) copy-start(s32[32]{0:T(128)} %refs_0_.9) | copy-start | bytes 388
  32.5 4.3 %collective-permute-start.12 = (bf16[8,96,256]{2,1,0:T(8,128)(2,1)S(1)}, bf16[8,96,256]{2,1,0:T(8,128)(2,1)S(1)}, u32[]{:S(2)}, u32[]{:S(2)}) collective-permute-start(bf16[8,96,256]{2,1,0:T(8,128)(2,1)S(1)} %get-tuple-element.29.refs_1_), channel_id=1, source_target_pairs={{0,1},{1,0},{2,3},{3,2},{4,5},{5,4},{6,7},{7,6},{8,9},{9,8},{10,11... | collective-permute-start | bytes 1179656 | tf_op jit(solution)/shard_map/ppermute | solution.py:309
  34.6 3.2 %collective-permute-start.13 = (bf16[8,96,256]{2,1,0:T(8,128)(2,1)S(1)}, bf16[8,96,256]{2,1,0:T(8,128)(2,1)S(1)}, u32[]{:S(2)}, u32[]{:S(2)}) collective-permute-start(bf16[8,96,256]{2,1,0:T(8,128)(2,1)S(1)} %get-tuple-element.28.refs_2_), channel_id=1, source_target_pairs={{0,1},{1,0},{2,3},{3,2},{4,5},{5,4},{6,7},{7,6},{8,9},{9,8},{10,11... | collective-permute-start | bytes 1179656 | tf_op jit(solution)/shard_map/ppermute | solution.py:309
  34.7 10.3 %collective-permute-start.4 = (bf16[8,96,256]{2,1,0:T(8,128)(2,1)S(1)}, bf16[8,96,256]{2,1,0:T(8,128)(2,1)S(1)}, u32[]{:S(2)}, u32[]{:S(2)}) collective-permute-start(bf16[8,96,256]{2,1,0:T(8,128)(2,1)S(1)} %get-tuple-element.29.refs_1_), channel_id=1, source_target_pairs={{0,2},{2,4},{4,6},{6,0},{1,3},{3,5},{5,7},{7,1},{8,10},{10,12},{12... | collective-permute-start | bytes 1179656 | tf_op jit(solution)/shard_map/ppermute | solution.py:304
  35.6 11.5 %collective-permute-start.14 = (bf16[16,96,128]{2,1,0:T(8,128)(2,1)S(1)}, bf16[16,96,128]{2,1,0:T(8,128)(2,1)S(1)}, u32[]{:S(2)}, u32[]{:S(2)}) collective-permute-start(bf16[16,96,128]{2,1,0:T(8,128)(2,1)S(1)} %get-tuple-element.31), channel_id=1, source_target_pairs={{0,1},{1,0},{2,3},{3,2},{4,5},{5,4},{6,7},{7,6},{8,9},{9,8},{10,11... | collective-permute-start | bytes 1179656 | tf_op jit(solution)/shard_map/ppermute | solution.py:309
  36.3 11.7 %collective-permute-start.6 = (bf16[8,96,256]{2,1,0:T(8,128)(2,1)S(1)}, bf16[8,96,256]{2,1,0:T(8,128)(2,1)S(1)}, u32[]{:S(2)}, u32[]{:S(2)}) collective-permute-start(bf16[8,96,256]{2,1,0:T(8,128)(2,1)S(1)} %get-tuple-element.28.refs_2_), channel_id=1, source_target_pairs={{0,6},{2,0},{4,2},{6,4},{1,7},{3,1},{5,3},{7,5},{8,14},{10,8},{12,... | collective-permute-start | bytes 1179656 | tf_op jit(solution)/shard_map/ppermute | solution.py:304
  36.9 16.5 %collective-permute-start = (bf16[8,96,256]{2,1,0:T(8,128)(2,1)S(1)}, bf16[8,96,256]{2,1,0:T(8,128)(2,1)S(1)}, u32[]{:S(2)}, u32[]{:S(2)}) collective-permute-start(bf16[8,96,256]{2,1,0:T(8,128)(2,1)S(1)} %get-tuple-element.28.refs_2_), channel_id=1, source_target_pairs={{0,2},{2,4},{4,6},{6,0},{1,3},{3,5},{5,7},{7,1},{8,10},{10,12},{12... | collective-permute-start | bytes 1179656 | tf_op jit(solution)/shard_map/ppermute | solution.py:304
  37.8 26.1 %collective-permute-start.1 = (bf16[8,96,256]{2,1,0:T(8,128)(2,1)S(1)}, bf16[8,96,256]{2,1,0:T(8,128)(2,1)S(1)}, u32[]{:S(2)}, u32[]{:S(2)}) collective-permute-start(bf16[8,96,256]{2,1,0:T(8,128)(2,1)S(1)} %get-tuple-element.29.refs_1_), channel_id=1, source_target_pairs={{0,6},{2,0},{4,2},{6,4},{1,7},{3,1},{5,3},{7,5},{8,14},{10,8},{12,... | collective-permute-start | bytes 1179656 | tf_op jit(solution)/shard_map/ppermute | solution.py:304
  45.0 21.4 %collective-permute-start.10 = (bf16[8,96,256]{2,1,0:T(8,128)(2,1)S(1)}, bf16[8,96,256]{2,1,0:T(8,128)(2,1)S(1)}, u32[]{:S(2)}, u32[]{:S(2)}) collective-permute-start(bf16[8,96,256]{2,1,0:T(8,128)(2,1)S(1)} %collective-permute-done.4.refs_1_), channel_id=1, source_target_pairs={{0,1},{1,0},{2,3},{3,2},{4,5},{5,4},{6,7},{7,6},{8,9},{9,8},{10,11... | collective-permute-start | bytes 1179656 | tf_op jit(solution)/shard_map/ppermute | solution.py:309
  47.1 19.4 %collective-permute-start.5 = (bf16[8,96,256]{2,1,0:T(8,128)(2,1)S(1)}, bf16[8,96,256]{2,1,0:T(8,128)(2,1)S(1)}, u32[]{:S(2)}, u32[]{:S(2)}) collective-permute-start(bf16[8,96,256]{2,1,0:T(8,128)(2,1)S(1)} %collective-permute-done.4.refs_1_), channel_id=1, source_target_pairs={{0,2},{2,4},{4,6},{6,0},{1,3},{3,5},{5,7},{7,1},{8,10},{10,12},{12... | collective-permute-start | bytes 1179656 | tf_op jit(solution)/shard_map/ppermute | solution.py:304
  48.0 19.0 %collective-permute-start.11 = (bf16[8,96,256]{2,1,0:T(8,128)(2,1)S(1)}, bf16[8,96,256]{2,1,0:T(8,128)(2,1)S(1)}, u32[]{:S(2)}, u32[]{:S(2)}) collective-permute-start(bf16[8,96,256]{2,1,0:T(8,128)(2,1)S(1)} %collective-permute-done.6.refs_2_), channel_id=1, source_target_pairs={{0,1},{1,0},{2,3},{3,2},{4,5},{5,4},{6,7},{7,6},{8,9},{9,8},{10,11... | collective-permute-start | bytes 1179656 | tf_op jit(solution)/shard_map/ppermute | solution.py:309
  53.4 13.5 %collective-permute-start.7 = (bf16[8,96,256]{2,1,0:T(8,128)(2,1)S(1)}, bf16[8,96,256]{2,1,0:T(8,128)(2,1)S(1)}, u32[]{:S(2)}, u32[]{:S(2)}) collective-permute-start(bf16[8,96,256]{2,1,0:T(8,128)(2,1)S(1)} %collective-permute-done.6.refs_2_), channel_id=1, source_target_pairs={{0,6},{2,0},{4,2},{6,4},{1,7},{3,1},{5,3},{7,5},{8,14},{10,8},{12,... | collective-permute-start | bytes 1179656 | tf_op jit(solution)/shard_map/ppermute | solution.py:304
  63.9 14.1 %collective-permute-start.2 = (bf16[8,96,256]{2,1,0:T(8,128)(2,1)S(1)}, bf16[8,96,256]{2,1,0:T(8,128)(2,1)S(1)}, u32[]{:S(2)}, u32[]{:S(2)}) collective-permute-start(bf16[8,96,256]{2,1,0:T(8,128)(2,1)S(1)} %collective-permute-done.refs_1_), channel_id=1, source_target_pairs={{0,1},{1,0},{2,3},{3,2},{4,5},{5,4},{6,7},{7,6},{8,9},{9,8},{10,11... | collective-permute-start | bytes 1179656 | tf_op jit(solution)/shard_map/ppermute | solution.py:309
  66.4 11.6 %collective-permute-start.3 = (bf16[8,96,256]{2,1,0:T(8,128)(2,1)S(1)}, bf16[8,96,256]{2,1,0:T(8,128)(2,1)S(1)}, u32[]{:S(2)}, u32[]{:S(2)}) collective-permute-start(bf16[8,96,256]{2,1,0:T(8,128)(2,1)S(1)} %collective-permute-done.1.refs_2_), channel_id=1, source_target_pairs={{0,1},{1,0},{2,3},{3,2},{4,5},{5,4},{6,7},{7,6},{8,9},{9,8},{10,11... | collective-permute-start | bytes 1179656 | tf_op jit(solution)/shard_map/ppermute | solution.py:309
  66.5 17.8 %collective-permute-start.8 = (bf16[8,96,256]{2,1,0:T(8,128)(2,1)S(1)}, bf16[8,96,256]{2,1,0:T(8,128)(2,1)S(1)}, u32[]{:S(2)}, u32[]{:S(2)}) collective-permute-start(bf16[8,96,256]{2,1,0:T(8,128)(2,1)S(1)} %collective-permute-done.5.refs_5_.refs_1_), channel_id=1, source_target_pairs={{0,1},{1,0},{2,3},{3,2},{4,5},{5,4},{6,7},{7,6},{8,9},{9,8},{10,11... | collective-permute-start | bytes 1179656 | tf_op jit(solution)/shard_map/ppermute | solution.py:309
  66.9 17.4 %collective-permute-start.9 = (bf16[8,96,256]{2,1,0:T(8,128)(2,1)S(1)}, bf16[8,96,256]{2,1,0:T(8,128)(2,1)S(1)}, u32[]{:S(2)}, u32[]{:S(2)}) collective-permute-start(bf16[8,96,256]{2,1,0:T(8,128)(2,1)S(1)} %collective-permute-done.7.refs_6_.refs_2_), channel_id=1, source_target_pairs={{0,1},{1,0},{2,3},{3,2},{4,5},{5,4},{6,7},{7,6},{8,9},{9,8},{10,11... | collective-permute-start | bytes 1179656 | tf_op jit(solution)/shard_map/ppermute | solution.py:309
  90.7 16.6 %collective-permute-start.16 = (bf16[768,128]{1,0:T(8,128)(2,1)S(1)}, bf16[768,128]{1,0:T(8,128)(2,1)S(1)}, u32[]{:S(2)}, u32[]{:S(2)}) collective-permute-start(bf16[768,128]{1,0:T(8,128)(2,1)S(1)} %get-tuple-element.49), channel_id=1, source_target_pairs={{0,8},{8,0},{1,9},{9,1},{2,10},{10,2},{3,11},{11,3},{4,12},{12,4},... | collective-permute-start | bytes 589832 | tf_op jit(solution)/shard_map/ppermute | solution.py:309
  92.5 14.9 %collective-permute-start.17 = (bf16[768,128]{1,0:T(8,128)(2,1)S(1)}, bf16[768,128]{1,0:T(8,128)(2,1)S(1)}, u32[]{:S(2)}, u32[]{:S(2)}) collective-permute-start(bf16[768,128]{1,0:T(8,128)(2,1)S(1)} %get-tuple-element.50), channel_id=1, source_target_pairs={{0,9},{1,8},{8,1},{9,0},{2,11},{3,10},{10,3},{11,2},{4,13},{5,12},... | collective-permute-start | bytes 589832 | tf_op jit(solution)/shard_map/ppermute | solution.py:309
  107.2 1.5 %collective-permute-start.15 = (bf16[768,128]{1,0:T(8,128)(2,1)S(1)}, bf16[768,128]{1,0:T(8,128)(2,1)S(1)}, u32[]{:S(2)}, u32[]{:S(2)}) collective-permute-start(bf16[768,128]{1,0:T(8,128)(2,1)S(1)} %get-tuple-element.42), channel_id=1, source_target_pairs={{0,1},{1,0},{2,3},{3,2},{4,5},{5,4},{6,7},{7,6},{8,9},{9,8},{10,11... | collective-permute-start | bytes 589832 | tf_op jit(solution)/shard_map/ppermute | solution.py:309

commit v8 on v7

--- a/solution.py
+++ b/solution.py
@@ -345,10 +345,9 @@
     own += [(swap(low), 0, 1, 0), (swap(high), 0, 1, 1)]
     near = [(up_low, 1, 0, 0), (down_high, 3, 0, 1)]
     near += [(swap(up_low), 1, 1, 0), (swap(down_high), 3, 1, 1)]
-    rest = [(up_high, 1, 0, 1), (down_low, 3, 0, 0)]
-    rest += [(swap(up_high), 1, 1, 1), (swap(down_low), 3, 1, 0)]
-    far = [(far_low, 2, 0, 0), (far_high, 2, 0, 1)]
-    far += [(swap(far_low), 2, 1, 0), (swap(far_high), 2, 1, 1)]
+    rest = [(up_high, 1, 0, 1), (down_low, 3, 0, 0), (far_low, 2, 0, 0), (far_high, 2, 0, 1)]
+    rest_o = [(swap(up_high), 1, 1, 1), (swap(down_low), 3, 1, 0)]
+    rest_o += [(swap(far_low), 2, 1, 0), (swap(far_high), 2, 1, 1)]
 
     def step(given, halves, carry, first=False, last=False):
         return attend(block_order, given, halves, carry, first, last)
@@ -358,14 +357,12 @@
     state = step(near, both, state)
     remote, local = state[:3], state[3:]
     remote = step(rest, (REMOTE,), remote)
-    same, cross = step(far, (REMOTE,), remote, last=True)
+    same, cross = step(rest_o, (REMOTE,), remote, last=True)
     z_same = mirror(same, "zhi")
     z_cross = mirror(cross, ("zhi", "core"))
-    mine, cross = step(rest + far, (LOCAL,), local, last=True)
+    mine, cross = step(rest + rest_o, (LOCAL,), local, last=True)
     swapped = mirror(cross, "core")
-    (out,) = local_call(
-        assemble_kernel, [(2 * BLK, 4 * HEAD)], (mine, swapped, z_same, z_cross)
-    )
+    (out,) = local_call(assemble_kernel, [(2 * BLK, 4 * HEAD)], (mine, swapped, z_same, z_cross))
     return out
 
 

time: 110 us -> 110 us (level)
  transfers between devices with their start and end apart: 18 -> 18, of which waited for: 3 -> 3; matrix products, arithmetic and copies ran while one was open for 0% -> 0% of each run, Pallas kernels for 37% -> 36%
where the time goes in v8:
time: 110 us
  Pallas kernels  50.5 us (46%)
  blocking collectives  29.6 us (27%)
  starting transfers between devices  16.4 us (15%)
  waiting for transfers between devices  13.1 us (12%)
    pallas_call x5, Pallas kernels, attend(): pl.pallas_call(functools.partial(attend_kernel, offsets=offsets, halves=h...  46.5 us
    all_to_all x1, blocking collectives, layer(): packed = lax.all_to_all(packed, ('y', 'zlo', 'zhi'), 0, 0)  29.6 us
    ppermute x12, starting transfers between devices, mirror(): return lax.ppermute(value, axes, [(i, size - 1 - i) for i in range(size)])  12.3 us
    ppermute x6, waiting for transfers between devices, along(): return lax.ppermute(value, axis, [(i, (i + by) % 4) for i in range(4)])  11.7 us
    ppermute x6, starting transfers between devices, along(): return lax.ppermute(value, axis, [(i, (i + by) % 4) for i in range(4)])  4.11 us
    pallas_call x1, Pallas kernels, layer(): pl.pallas_call(sort_kernel, out_shape=jax.ShapeDtypeStruct((16, rows, 4 *...  2.72 us
  transfers between devices with their start and end apart: 18, of which 3 were waited for; matrix products, arithmetic and copies ran while one was open for 0% of the time, Pallas kernels for 36%

profile of v8, /device:TPU:5, one launch (start us, length us, event | category | flops | bytes accessed | tf_op | source)
XLA Modules:
  0.0 109.8 jit_solution(3599168932719559777)
XLA Ops:
  0.0 2.7 %k_sort.1 = bf16[16,96,512]{2,1,0:T(8,128)(2,1)} custom-call(bf16[96,4096]{1,0:T(8,128)(2,1)} %query.1, bf16[96,2048]{1,0:T(8,128)(2,1)} %key.1, bf16[96,2048]{1,0:T(8,128)(2,1)} %value.1), custom_call_target="tpu_custom_call" | custom-call | tf_op jit(solution)/shard_map/k_sort/pallas_call | solution.py:314
  2.7 29.6 %all_to_all.5.got = bf16[16,96,512]{2,1,0:T(8,128)(2,1)S(1)} all-to-all(bf16[16,96,512]{2,1,0:T(8,128)(2,1)} %k_sort.1), channel_id=1, replica_groups=mesh['y'=4,'zlo'=2,'zhi'=2,'x'=4,'core'=2] {'y','zlo','zhi'}, dimensions={0} | all-to-all | bytes 3145728 | tf_op jit(solution)/shard_map/all_to_all | solution.py:329
  32.3 0.0 copy-start
  32.3 0.2 shard_map.46
  32.5 2.1 %collective-permute-start.12 = (bf16[8,96,256]{2,1,0:T(8,128)(2,1)S(1)}, bf16[8,96,256]{2,1,0:T(8,128)(2,1)S(1)}, u32[]{:S(2)}, u32[]{:S(2)}) collective-permute-start(bf16[8,96,256]{2,1,0:T(8,128)(2,1)S(1)} %get-tuple-element.29.refs_1_), channel_id=1, source_target_pairs={{0,1},{1,0},{2,3},{3,2},{4,5},{5,4},{6,7},{7,6},{8,9},{9,8},{10,11... | collective-permute-start | bytes 1179656 | tf_op jit(solution)/shard_map/ppermute | solution.py:309
  34.6 0.1 collective-permute-start.13
  34.7 0.9 collective-permute-start.2
  35.6 0.7 collective-permute-start.14
  36.3 0.5 collective-permute-start.4
  36.9 0.0 collective-permute-done.12.refs_3_
  36.9 0.9 collective-permute-start
  37.8 0.0 collective-permute-done.13.refs_4_
  37.8 0.5 collective-permute-start.1
  38.4 6.6 %collective-permute-done.2.refs_1_ = bf16[8,96,256]{2,1,0:T(8,128)(2,1)S(1)} collective-permute-done((bf16[8,96,256]{2,1,0:T(8,128)(2,1)S(1)}, bf16[8,96,256]{2,1,0:T(8,128)(2,1)S(1)}, u32[]{:S(2)}, u32[]{:S(2)}) %collective-permute-start.2) | collective-permute-done | bytes 393248 | tf_op jit(solution)/shard_map/ppermute | solution.py:304
  45.0 2.1 %collective-permute-start.10 = (bf16[8,96,256]{2,1,0:T(8,128)(2,1)S(1)}, bf16[8,96,256]{2,1,0:T(8,128)(2,1)S(1)}, u32[]{:S(2)}, u32[]{:S(2)}) collective-permute-start(bf16[8,96,256]{2,1,0:T(8,128)(2,1)S(1)} %collective-permute-done.2.refs_1_), channel_id=1, source_target_pairs={{0,1},{1,0},{2,3},{3,2},{4,5},{5,4},{6,7},{7,6},{8,9},{9,8},{10,11... | collective-permute-start | bytes 1179656 | tf_op jit(solution)/shard_map/ppermute | solution.py:309
  47.1 0.0 collective-permute-done.14.refs_6_
  47.1 0.9 collective-permute-start.3
  48.0 0.0 collective-permute-done.4.refs_2_
  48.0 0.3 collective-permute-start.11
  48.3 5.1 %collective-permute-done.refs_1_ = bf16[8,96,256]{2,1,0:T(8,128)(2,1)S(1)} collective-permute-done((bf16[8,96,256]{2,1,0:T(8,128)(2,1)S(1)}, bf16[8,96,256]{2,1,0:T(8,128)(2,1)S(1)}, u32[]{:S(2)}, u32[]{:S(2)}) %collective-permute-start) | collective-permute-done | bytes 393248 | tf_op jit(solution)/shard_map/ppermute | solution.py:304
  53.4 0.3 collective-permute-start.5
  53.7 0.0 copy-done
  53.7 10.2 %shard_map.47 = (bf16[6,128,256]{2,1,0:T(8,128)(2,1)S(1)}, f32[6,128,256]{2,1,0:T(8,128)S(1)}, f32[6,8,256]{2,1,0:T(8,128)S(1)}, bf16[6,128,256]{2,1,0:T(8,128)(...) custom-call(s32[32]{0:T(128)S(1)} %copy-done, bf16[8,96,256]{2,1,0:T(8,128)(2,1)S(1)} %get-tuple-element.29.refs_1_, ...), custom_call_target="tpu_custom_call" | custom-call | flops 4800000000 | bytes 4000000 | tf_op jit(solution)/shard_map/pallas_call | solution.py:220
  63.9 0.0 collective-permute-done.1.refs_2_
  63.9 2.5 %collective-permute-start.6 = (bf16[8,96,256]{2,1,0:T(8,128)(2,1)S(1)}, bf16[8,96,256]{2,1,0:T(8,128)(2,1)S(1)}, u32[]{:S(2)}, u32[]{:S(2)}) collective-permute-start(bf16[8,96,256]{2,1,0:T(8,128)(2,1)S(1)} %collective-permute-done.refs_1_), channel_id=1, source_target_pairs={{0,1},{1,0},{2,3},{3,2},{4,5},{5,4},{6,7},{7,6},{8,9},{9,8},{10,11... | collective-permute-start | bytes 1179656 | tf_op jit(solution)/shard_map/ppermute | solution.py:309
  66.4 0.0 collective-permute-done.10.refs_3_
  66.4 0.1 collective-permute-start.7
  66.5 0.0 collective-permute-done.3.refs_3_
  66.5 0.4 collective-permute-start.8
  66.9 0.0 collective-permute-done.5.refs_4_
  66.9 0.1 collective-permute-start.9
  67.0 0.0 collective-permute-done.11.refs_4_
  67.0 10.9 %shard_map.48 = (bf16[6,128,256]{2,1,0:T(8,128)(2,1)S(1)}, f32[6,128,256]{2,1,0:T(8,128)S(1)}, f32[6,8,256]{2,1,0:T(8,128)S(1)}, bf16[6,128,256]{2,1,0:T(8,128)(...) custom-call(s32[32]{0:T(128)S(1)} %copy-done, bf16[8,96,256]{2,1,0:T(8,128)(2,1)S(1)} %collective-permute-done.2.refs_1_, ...), custom_call_target="tpu_custom_call" | custom-call | flops 4800000000 | bytes 4000000 | tf_op jit(solution)/shard_map/pallas_call | solution.py:220
  78.0 5.7 %shard_map.50 = (bf16[6,128,256]{2,1,0:T(8,128)(2,1)S(1)}, f32[6,128,256]{2,1,0:T(8,128)S(1)}, f32[6,8,256]{2,1,0:T(8,128)S(1)}) custom-call(s32[32]{0:T(128)S(1)} %copy-done, bf16[8,96,256]{2,1,0:T(8,128)(2,1)S(1)} %collective-permute-done.refs_1_, bf16[8,96,256]{2,1,0:T(8,128)(2,1)S(1)} %collective-permute-done.1.refs_2_, ...), custom_call_target="tpu_custom_call" | custom-call | flops 2400000000 | bytes 4000000 | tf_op jit(solution)/shard_map/pallas_call | solution.py:220
  83.7 0.0 collective-permute-done.6.refs_5_.refs_1_
  83.7 0.0 collective-permute-done.7.refs_6_.refs_2_
  83.7 0.0 collective-permute-done.8.refs_7_.refs_3_
  83.7 0.0 collective-permute-done.9.refs_8_.refs_4_
  83.8 7.0 %shard_map.51 = (bf16[768,128]{1,0:T(8,128)(2,1)S(1)}, bf16[768,128]{1,0:T(8,128)(2,1)S(1)}) custom-call(s32[32]{0:T(128)S(1)} %copy-done, bf16[8,96,256]{2,1,0:T(8,128)(2,1)S(1)} %collective-permute-done.6.refs_5_.refs_1_, bf16[8,96,256]{2,1,0:T(8,128)(2,1)S(1)} %collective-permute-done.7.refs_6_.refs_2_, ...), custom_call_target="tpu_custom_call" | custom-call | flops 2400000000 | bytes 4000000 | tf_op jit(solution)/shard_map/pallas_call | solution.py:220
  90.7 1.7 %collective-permute-start.16 = (bf16[768,128]{1,0:T(8,128)(2,1)S(1)}, bf16[768,128]{1,0:T(8,128)(2,1)S(1)}, u32[]{:S(2)}, u32[]{:S(2)}) collective-permute-start(bf16[768,128]{1,0:T(8,128)(2,1)S(1)} %get-tuple-element.49), channel_id=1, source_target_pairs={{0,8},{8,0},{1,9},{9,1},{2,10},{10,2},{3,11},{11,3},{4,12},{12,4},... | collective-permute-start | bytes 589832 | tf_op jit(solution)/shard_map/ppermute | solution.py:309
  92.4 2.1 %collective-permute-start.17 = (bf16[768,128]{1,0:T(8,128)(2,1)S(1)}, bf16[768,128]{1,0:T(8,128)(2,1)S(1)}, u32[]{:S(2)}, u32[]{:S(2)}) collective-permute-start(bf16[768,128]{1,0:T(8,128)(2,1)S(1)} %get-tuple-element.50), channel_id=1, source_target_pairs={{0,9},{1,8},{8,1},{9,0},{2,11},{3,10},{10,3},{11,2},{4,13},{5,12},... | collective-permute-start | bytes 589832 | tf_op jit(solution)/shard_map/ppermute | solution.py:309
  94.5 12.7 %shard_map.49 = (bf16[768,128]{1,0:T(8,128)(2,1)S(1)}, bf16[768,128]{1,0:T(8,128)(2,1)S(1)}) custom-call(s32[32]{0:T(128)S(1)} %copy-done, bf16[8,96,256]{2,1,0:T(8,128)(2,1)S(1)} %collective-permute-done.refs_1_, bf16[8,96,256]{2,1,0:T(8,128)(2,1)S(1)} %collective-permute-done.1.refs_2_, bf16[8,96,256]{2,1,0:T(8,128)(2,1)S(1)} %collective-permute-done.3.refs_3_, ...), custom_call_target="tpu_custom_call" | custom-call | flops 4800000000 | bytes 4000000 | tf_op jit(solution)/shard_map/pallas_call | solution.py:220
  107.2 0.1 collective-permute-start.15
  107.3 0.0 collective-permute-done.16.z_same
  107.3 0.0 collective-permute-done.17.z_cross
  107.3 1.4 %collective-permute-done.15.swapped = bf16[768,128]{1,0:T(8,128)(2,1)S(1)} collective-permute-done((bf16[768,128]{1,0:T(8,128)(2,1)S(1)}, bf16[768,128]{1,0:T(8,128)(2,1)S(1)}, u32[]{:S(2)}, u32[]{:S(2)}) %collective-permute-start.15) | collective-permute-done | bytes 196640 | tf_op jit(solution)/shard_map/ppermute | solution.py:309
  108.8 1.1 shard_map.52
Async XLA Ops:
  32.3 21.3 %copy-start = (s32[32]{0:T(128)S(1)}, s32[32]{0:T(128)}, u32[]{:S(2)}) copy-start(s32[32]{0:T(128)} %refs_0_.9) | copy-start | bytes 388
  32.5 4.3 %collective-permute-start.12 = (bf16[8,96,256]{2,1,0:T(8,128)(2,1)S(1)}, bf16[8,96,256]{2,1,0:T(8,128)(2,1)S(1)}, u32[]{:S(2)}, u32[]{:S(2)}) collective-permute-start(bf16[8,96,256]{2,1,0:T(8,128)(2,1)S(1)} %get-tuple-element.29.refs_1_), channel_id=1, source_target_pairs={{0,1},{1,0},{2,3},{3,2},{4,5},{5,4},{6,7},{7,6},{8,9},{9,8},{10,11... | collective-permute-start | bytes 1179656 | tf_op jit(solution)/shard_map/ppermute | solution.py:309
  34.6 3.2 %collective-permute-start.13 = (bf16[8,96,256]{2,1,0:T(8,128)(2,1)S(1)}, bf16[8,96,256]{2,1,0:T(8,128)(2,1)S(1)}, u32[]{:S(2)}, u32[]{:S(2)}) collective-permute-start(bf16[8,96,256]{2,1,0:T(8,128)(2,1)S(1)} %get-tuple-element.28.refs_2_), channel_id=1, source_target_pairs={{0,1},{1,0},{2,3},{3,2},{4,5},{5,4},{6,7},{7,6},{8,9},{9,8},{10,11... | collective-permute-start | bytes 1179656 | tf_op jit(solution)/shard_map/ppermute | solution.py:309
  34.7 10.3 %collective-permute-start.2 = (bf16[8,96,256]{2,1,0:T(8,128)(2,1)S(1)}, bf16[8,96,256]{2,1,0:T(8,128)(2,1)S(1)}, u32[]{:S(2)}, u32[]{:S(2)}) collective-permute-start(bf16[8,96,256]{2,1,0:T(8,128)(2,1)S(1)} %get-tuple-element.29.refs_1_), channel_id=1, source_target_pairs={{0,2},{2,4},{4,6},{6,0},{1,3},{3,5},{5,7},{7,1},{8,10},{10,12},{12... | collective-permute-start | bytes 1179656 | tf_op jit(solution)/shard_map/ppermute | solution.py:304
  35.6 11.5 %collective-permute-start.14 = (bf16[16,96,128]{2,1,0:T(8,128)(2,1)S(1)}, bf16[16,96,128]{2,1,0:T(8,128)(2,1)S(1)}, u32[]{:S(2)}, u32[]{:S(2)}) collective-permute-start(bf16[16,96,128]{2,1,0:T(8,128)(2,1)S(1)} %get-tuple-element.31), channel_id=1, source_target_pairs={{0,1},{1,0},{2,3},{3,2},{4,5},{5,4},{6,7},{7,6},{8,9},{9,8},{10,11... | collective-permute-start | bytes 1179656 | tf_op jit(solution)/shard_map/ppermute | solution.py:309
  36.3 11.7 %collective-permute-start.4 = (bf16[8,96,256]{2,1,0:T(8,128)(2,1)S(1)}, bf16[8,96,256]{2,1,0:T(8,128)(2,1)S(1)}, u32[]{:S(2)}, u32[]{:S(2)}) collective-permute-start(bf16[8,96,256]{2,1,0:T(8,128)(2,1)S(1)} %get-tuple-element.28.refs_2_), channel_id=1, source_target_pairs={{0,6},{2,0},{4,2},{6,4},{1,7},{3,1},{5,3},{7,5},{8,14},{10,8},{12,... | collective-permute-start | bytes 1179656 | tf_op jit(solution)/shard_map/ppermute | solution.py:304
  36.9 16.5 %collective-permute-start = (bf16[8,96,256]{2,1,0:T(8,128)(2,1)S(1)}, bf16[8,96,256]{2,1,0:T(8,128)(2,1)S(1)}, u32[]{:S(2)}, u32[]{:S(2)}) collective-permute-start(bf16[8,96,256]{2,1,0:T(8,128)(2,1)S(1)} %get-tuple-element.28.refs_2_), channel_id=1, source_target_pairs={{0,2},{2,4},{4,6},{6,0},{1,3},{3,5},{5,7},{7,1},{8,10},{10,12},{12... | collective-permute-start | bytes 1179656 | tf_op jit(solution)/shard_map/ppermute | solution.py:304
  37.8 26.1 %collective-permute-start.1 = (bf16[8,96,256]{2,1,0:T(8,128)(2,1)S(1)}, bf16[8,96,256]{2,1,0:T(8,128)(2,1)S(1)}, u32[]{:S(2)}, u32[]{:S(2)}) collective-permute-start(bf16[8,96,256]{2,1,0:T(8,128)(2,1)S(1)} %get-tuple-element.29.refs_1_), channel_id=1, source_target_pairs={{0,6},{2,0},{4,2},{6,4},{1,7},{3,1},{5,3},{7,5},{8,14},{10,8},{12,... | collective-permute-start | bytes 1179656 | tf_op jit(solution)/shard_map/ppermute | solution.py:304
  45.0 21.4 %collective-permute-start.10 = (bf16[8,96,256]{2,1,0:T(8,128)(2,1)S(1)}, bf16[8,96,256]{2,1,0:T(8,128)(2,1)S(1)}, u32[]{:S(2)}, u32[]{:S(2)}) collective-permute-start(bf16[8,96,256]{2,1,0:T(8,128)(2,1)S(1)} %collective-permute-done.2.refs_1_), channel_id=1, source_target_pairs={{0,1},{1,0},{2,3},{3,2},{4,5},{5,4},{6,7},{7,6},{8,9},{9,8},{10,11... | collective-permute-start | bytes 1179656 | tf_op jit(solution)/shard_map/ppermute | solution.py:309
  47.1 19.4 %collective-permute-start.3 = (bf16[8,96,256]{2,1,0:T(8,128)(2,1)S(1)}, bf16[8,96,256]{2,1,0:T(8,128)(2,1)S(1)}, u32[]{:S(2)}, u32[]{:S(2)}) collective-permute-start(bf16[8,96,256]{2,1,0:T(8,128)(2,1)S(1)} %collective-permute-done.2.refs_1_), channel_id=1, source_target_pairs={{0,2},{2,4},{4,6},{6,0},{1,3},{3,5},{5,7},{7,1},{8,10},{10,12},{12... | collective-permute-start | bytes 1179656 | tf_op jit(solution)/shard_map/ppermute | solution.py:304
  48.0 19.0 %collective-permute-start.11 = (bf16[8,96,256]{2,1,0:T(8,128)(2,1)S(1)}, bf16[8,96,256]{2,1,0:T(8,128)(2,1)S(1)}, u32[]{:S(2)}, u32[]{:S(2)}) collective-permute-start(bf16[8,96,256]{2,1,0:T(8,128)(2,1)S(1)} %collective-permute-done.4.refs_2_), channel_id=1, source_target_pairs={{0,1},{1,0},{2,3},{3,2},{4,5},{5,4},{6,7},{7,6},{8,9},{9,8},{10,11... | collective-permute-start | bytes 1179656 | tf_op jit(solution)/shard_map/ppermute | solution.py:309
  53.4 13.5 %collective-permute-start.5 = (bf16[8,96,256]{2,1,0:T(8,128)(2,1)S(1)}, bf16[8,96,256]{2,1,0:T(8,128)(2,1)S(1)}, u32[]{:S(2)}, u32[]{:S(2)}) collective-permute-start(bf16[8,96,256]{2,1,0:T(8,128)(2,1)S(1)} %collective-permute-done.4.refs_2_), channel_id=1, source_target_pairs={{0,6},{2,0},{4,2},{6,4},{1,7},{3,1},{5,3},{7,5},{8,14},{10,8},{12,... | collective-permute-start | bytes 1179656 | tf_op jit(solution)/shard_map/ppermute | solution.py:304
  63.9 19.8 %collective-permute-start.6 = (bf16[8,96,256]{2,1,0:T(8,128)(2,1)S(1)}, bf16[8,96,256]{2,1,0:T(8,128)(2,1)S(1)}, u32[]{:S(2)}, u32[]{:S(2)}) collective-permute-start(bf16[8,96,256]{2,1,0:T(8,128)(2,1)S(1)} %collective-permute-done.refs_1_), channel_id=1, source_target_pairs={{0,1},{1,0},{2,3},{3,2},{4,5},{5,4},{6,7},{7,6},{8,9},{9,8},{10,11... | collective-permute-start | bytes 1179656 | tf_op jit(solution)/shard_map/ppermute | solution.py:309
  66.4 17.3 %collective-permute-start.7 = (bf16[8,96,256]{2,1,0:T(8,128)(2,1)S(1)}, bf16[8,96,256]{2,1,0:T(8,128)(2,1)S(1)}, u32[]{:S(2)}, u32[]{:S(2)}) collective-permute-start(bf16[8,96,256]{2,1,0:T(8,128)(2,1)S(1)} %collective-permute-done.1.refs_2_), channel_id=1, source_target_pairs={{0,1},{1,0},{2,3},{3,2},{4,5},{5,4},{6,7},{7,6},{8,9},{9,8},{10,11... | collective-permute-start | bytes 1179656 | tf_op jit(solution)/shard_map/ppermute | solution.py:309
  66.5 17.2 %collective-permute-start.8 = (bf16[8,96,256]{2,1,0:T(8,128)(2,1)S(1)}, bf16[8,96,256]{2,1,0:T(8,128)(2,1)S(1)}, u32[]{:S(2)}, u32[]{:S(2)}) collective-permute-start(bf16[8,96,256]{2,1,0:T(8,128)(2,1)S(1)} %collective-permute-done.3.refs_3_), channel_id=1, source_target_pairs={{0,1},{1,0},{2,3},{3,2},{4,5},{5,4},{6,7},{7,6},{8,9},{9,8},{10,11... | collective-permute-start | bytes 1179656 | tf_op jit(solution)/shard_map/ppermute | solution.py:309
  66.9 16.8 %collective-permute-start.9 = (bf16[8,96,256]{2,1,0:T(8,128)(2,1)S(1)}, bf16[8,96,256]{2,1,0:T(8,128)(2,1)S(1)}, u32[]{:S(2)}, u32[]{:S(2)}) collective-permute-start(bf16[8,96,256]{2,1,0:T(8,128)(2,1)S(1)} %collective-permute-done.5.refs_4_), channel_id=1, source_target_pairs={{0,1},{1,0},{2,3},{3,2},{4,5},{5,4},{6,7},{7,6},{8,9},{9,8},{10,11... | collective-permute-start | bytes 1179656 | tf_op jit(solution)/shard_map/ppermute | solution.py:309
  90.7 16.6 %collective-permute-start.16 = (bf16[768,128]{1,0:T(8,128)(2,1)S(1)}, bf16[768,128]{1,0:T(8,128)(2,1)S(1)}, u32[]{:S(2)}, u32[]{:S(2)}) collective-permute-start(bf16[768,128]{1,0:T(8,128)(2,1)S(1)} %get-tuple-element.49), channel_id=1, source_target_pairs={{0,8},{8,0},{1,9},{9,1},{2,10},{10,2},{3,11},{11,3},{4,12},{12,4},... | collective-permute-start | bytes 589832 | tf_op jit(solution)/shard_map/ppermute | solution.py:309
  92.4 14.9 %collective-permute-start.17 = (bf16[768,128]{1,0:T(8,128)(2,1)S(1)}, bf16[768,128]{1,0:T(8,128)(2,1)S(1)}, u32[]{:S(2)}, u32[]{:S(2)}) collective-permute-start(bf16[768,128]{1,0:T(8,128)(2,1)S(1)} %get-tuple-element.50), channel_id=1, source_target_pairs={{0,9},{1,8},{8,1},{9,0},{2,11},{3,10},{10,3},{11,2},{4,13},{5,12},... | collective-permute-start | bytes 589832 | tf_op jit(solution)/shard_map/ppermute | solution.py:309
  107.2 1.5 %collective-permute-start.15 = (bf16[768,128]{1,0:T(8,128)(2,1)S(1)}, bf16[768,128]{1,0:T(8,128)(2,1)S(1)}, u32[]{:S(2)}, u32[]{:S(2)}) collective-permute-start(bf16[768,128]{1,0:T(8,128)(2,1)S(1)} %get-tuple-element.42), channel_id=1, source_target_pairs={{0,1},{1,0},{2,3},{3,2},{4,5},{5,4},{6,7},{7,6},{8,9},{9,8},{10,11... | collective-permute-start | bytes 589832 | tf_op jit(solution)/shard_map/ppermute | solution.py:309
